TPU v7x, 8 devices: a whole 2x2x1 slice. The times are simulated.
8 devices in a mesh: rep: 2 (over z, y), model: 4 (over x, core).
Axes of the slice: x: 2, y: 2, z: 1, core: 2. Of those that a mesh axis runs over, the one named last changes fastest.
Arguments:
- x_real: bfloat16 [1024, 1280], P('rep'), parts along dimension 0
- x_fake: bfloat16 [1024, 1280], P('rep'), parts along dimension 0
- weight0: bfloat16 [10240, 1280], P(('rep', 'model')), parts along dimension 0
- weight1: bfloat16 [2560, 5120], P(('rep', 'model')), parts along dimension 0
- weight2: bfloat16 [2560, 1280], P(('rep', 'model')), parts along dimension 0
- u_left0: float32 [10240], P(('rep', 'model')), parts along dimension 0
- u_left1: float32 [2560], P(('rep', 'model')), parts along dimension 0
- u_left2: float32 [2560], P(('rep', 'model')), parts along dimension 0
- t_real: bfloat16 [1024, 1280], P('rep', 'model'), parts along dimension 0
- t_fake: bfloat16 [1024, 1280], P('rep', 'model'), parts along dimension 0
Outputs:
- output 1: float32 [2], P('rep'), parts along dimension 0
- output 2: float32 [1024, 1280], P('rep'), parts along dimension 0
- output 3: float32 [1024, 1280], P('rep'), parts along dimension 0
- output 4: float32 [10240, 1280], P(('rep', 'model')), parts along dimension 0
- output 5: float32 [2560, 5120], P(('rep', 'model')), parts along dimension 0
- output 6: float32 [2560, 1280], P(('rep', 'model')), parts along dimension 0
- output 7: float32 [10240], P(('rep', 'model')), parts along dimension 0
- output 8: float32 [2560], P(('rep', 'model')), parts along dimension 0
- output 9: float32 [2560], P(('rep', 'model')), parts along dimension 0
- output 10: float32 [2560], P('rep'), parts along dimension 0
- output 11: float32 [10240], P('rep'), parts along dimension 0
- output 12: float32 [2560], P('rep'), parts along dimension 0
- output 13: float32 [6], P('rep'), parts along dimension 0
There are 2 independent parts. A program takes and returns all parts, laid end to end along the dimension named above; each array names one.
All inputs are finite; a program needn't handle non-finite values.
Results may differ from a plain program's by a relative error of at most 0.0189091.
Values are sent between devices in bfloat16 or wider.
A program may use at most 1 GiB of HBM per device.

v0:
```python
import jax
import jax.numpy as jnp
from jax import lax
from jax.sharding import PartitionSpec as P

SLOPE = 0.2
EPSILON = 1e-12


def leaky_relu(values):
    return jnp.where(values > 0, values, SLOPE * values)


def leaky_slope(values):
    return jnp.where(values > 0, 1.0, SLOPE)


def power_step(weight, u_left):
    p_part = jnp.dot(u_left.astype(jnp.bfloat16), weight, preferred_element_type=jnp.float32)
    p_vec = lax.psum(p_part, "model")
    v_new = p_vec / jnp.maximum(jnp.sqrt(jnp.sum(p_vec * p_vec)), EPSILON)
    s_vec = jnp.dot(weight, v_new.astype(jnp.bfloat16), preferred_element_type=jnp.float32)
    sigma_val = jnp.sqrt(lax.psum(jnp.sum(s_vec * s_vec), "model"))
    return s_vec / sigma_val, v_new, sigma_val


def solution(mesh):
    rows_spec = P("rep", None)
    weight_spec = P(("rep", "model"), None)
    left_spec = P(("rep", "model"))
    target_spec = P("rep", "model")
    group_spec = P("rep")

    def local_step(x_real, x_fake, weight0, weight1, weight2, u_left0, u_left1, u_left2, t_real, t_fake):
        n_rows = x_real.shape[0]
        weights = (weight0, weight1, weight2)
        powered = [power_step(weight, u_left) for weight, u_left in zip(weights, (u_left0, u_left1, u_left2))]
        layer_in = jnp.concatenate([x_real, x_fake], axis=0)
        inputs = []
        outputs = []
        for layer_no in range(3):
            inputs.append(layer_in)
            y_local = jnp.einsum("bi,oi->bo", layer_in, weights[layer_no], preferred_element_type=jnp.float32) / powered[layer_no][2]
            outputs.append(y_local)
            if layer_no < 2:
                layer_in = lax.all_gather(leaky_relu(y_local).astype(jnp.bfloat16), "model", axis=1, tiled=True)
        target = jnp.concatenate([t_real, t_fake], axis=0).astype(jnp.float32)
        upstream = outputs[2] - target
        loss_val = lax.psum(jnp.sum(upstream * upstream), "model") * (0.5 / n_rows)
        dweights = [None, None, None]
        back_sum = upstream
        for layer_no in (2, 1, 0):
            u_new, v_new, sigma_val = powered[layer_no]
            up_half = upstream.astype(jnp.bfloat16)
            outer_sum = jnp.einsum("bo,bi->oi", up_half, inputs[layer_no], preferred_element_type=jnp.float32)
            corr_sum = lax.psum(jnp.sum(upstream * outputs[layer_no]), "model")
            dweights[layer_no] = (outer_sum - corr_sum * u_new[:, None] * v_new[None, :]) / (n_rows * sigma_val)
            part_sum = jnp.dot(up_half, weights[layer_no], preferred_element_type=jnp.float32).astype(jnp.bfloat16)
            if layer_no > 0:
                back_sum = lax.psum_scatter(part_sum, "model", scatter_dimension=1, tiled=True).astype(jnp.float32) / sigma_val
                upstream = back_sum * leaky_slope(outputs[layer_no - 1])
            else:
                back_sum = lax.psum(part_sum, "model").astype(jnp.float32) / sigma_val
        sigmas = jnp.stack([step_out[2] for step_out in powered])
        return (loss_val.reshape(1), back_sum[:n_rows], back_sum[n_rows:], dweights[0], dweights[1], dweights[2], powered[0][0], powered[1][0], powered[2][0], powered[0][1], powered[1][1], powered[2][1], sigmas)

    return jax.shard_map(local_step, mesh=mesh, in_specs=(rows_spec, rows_spec, weight_spec, weight_spec, weight_spec, left_spec, left_spec, left_spec, target_spec, target_spec), out_specs=(group_spec, rows_spec, rows_spec, weight_spec, weight_spec, weight_spec, left_spec, left_spec, left_spec, group_spec, group_spec, group_spec, group_spec), check_vma=False)
```

profile of v0, /device:TPU:0, one launch (start us, length us, event | category | flops | bytes accessed | tf_op | source)
XLA Modules:
  0.0 358.7 jit_solution(8440766773206342645)
XLA Ops:
  7.2 0.8 convert_element_type.54
  8.1 0.8 convert_element_type.57
  8.9 0.7 convert_element_type.60
  9.6 2.6 convolution_reduce_fusion.1
  12.1 0.5 fusion.16
  12.7 0.2 convolution_reduce_fusion.2
  12.9 13.5 %all-reduce.2 = (f32[1280]{0:T(1024)S(1)}, f32[5120]{0:T(1024)S(1)}, f32[1280]{0:T(1024)S(1)}) all-reduce(f32[1280]{0:T(1024)S(1)} %convolution_reduce_fusion.1, f32[5120]{0:T(1024)S(1)} %bitcast.33, f32[1280]{0:T(1024)S(1)} %convolution_reduce_fusion.2), channel_id=1, replica_groups=mesh['rep'=2,'model'=4] {'model'}, use_global_device_ids=true, to_apply=%region_0.0 | all-reduce | flops 7680 | bytes 61440 | tf_op jit(solution)/shard_map/psum | solution.py:20
  26.5 0.6 multiply_reduce_fusion.5
  27.8 2.9 convolution_reduce_fusion
  30.8 0.6 multiply_reduce_fusion.6
  31.4 0.6 multiply_reduce_fusion.4
  32.7 1.0 convolution_reduce_fusion.4
  33.7 0.6 multiply_reduce_fusion.9
  35.0 1.5 convolution_reduce_fusion.3
  36.5 0.6 multiply_reduce_fusion.8
  37.1 6.4 %all-reduce.1 = (f32[]{:T(128)}, f32[]{:T(128)}, f32[]{:T(128)}) all-reduce(f32[]{:T(128)} %multiply_reduce_fusion.6, f32[]{:T(128)} %multiply_reduce_fusion.9, f32[]{:T(128)} %multiply_reduce_fusion.8), channel_id=1, replica_groups=mesh['rep'=2,'model'=4] {'model'}, use_global_device_ids=true, to_apply=%region_3.0 | all-reduce | flops 3 | bytes 24 | tf_op jit(solution)/shard_map/psum | solution.py:23
  44.2 1.6 constant_dynamic-update-slice_fusion.1
  45.8 1.4 constant_dynamic-update-slice_fusion
  47.2 5.8 %fusion.3 = (bf16[1024,1280]{1,0:T(8,128)(2,1)}, f32[1024,1280]{1,0:T(8,128)}) fusion(f32[]{:T(128)} %sqrt.19, bf16[1024,1280]{1,0:T(8,128)(2,1)S(1)} %constant_dynamic-update-slice_fusion, bf16[1280,1280]{1,0:T(8,128)(2,1)S(1)} %copy-done.2), kind=kOutput, calls=%fused_computation.8 | convolution fusion | flops 3361996800 | bytes 13762564 | tf_op jit(solution)/shard_map/bi,oi->bo/dot_general | solution.py:43
  53.0 0.0 all-gather.5.cloned.1.call-start
  53.8 67.4 %all-gather.3.cloned.1.call-done = bf16[1024,5120]{1,0:T(8,128)(2,1)} async-done(((bf16[1024,1280]{1,0:T(8,128)(2,1)}), bf16[1024,5120]{1,0:T(8,128)(2,1)}) %all-gather.3.cloned.1.call-update) | async-done | bytes 10485776 | tf_op jit(solution)/shard_map/all_gather | solution.py:46
  121.2 8.8 %fusion.7 = (bf16[1024,320]{0,1:T(8,128)(2,1)}, f32[1024,320]{0,1:T(8,128)}) fusion(f32[]{:T(128)} %sqrt.21, bf16[1024,5120]{1,0:T(8,128)(2,1)} %all-gather.3.cloned.1.call-done, bf16[320,5120]{1,0:T(8,128)(2,1)S(1)} %copy-done), kind=kOutput, calls=%fused_computation.20 | convolution fusion | flops 3357081600 | bytes 15728644 | tf_op jit(solution)/shard_map/bi,oi->bo/dot_general | solution.py:43
  130.8 21.8 %all-gather.5.cloned.1.call-done = bf16[1024,1280]{0,1:T(8,128)(2,1)} async-done(((bf16[1024,320]{0,1:T(8,128)(2,1)}), bf16[1024,1280]{0,1:T(8,128)(2,1)}) %all-gather.5.cloned.1.call-update) | async-done | bytes 2621456 | tf_op jit(solution)/shard_map/all_gather | solution.py:46
  152.6 3.9 %multiply_reduce_fusion.1 = (f32[]{:T(128)}, f32[]{:T(128)}, f32[1024,320]{0,1:T(8,128)S(1)}) fusion(bf16[512,320]{0,1:T(8,128)(2,1)} %param.19, bf16[512,320]{0,1:T(8,128)(2,1)} %param.18, f32[]{:T(128)} %sqrt.23, bf16[320,1280]{1,0:T(8,128)(2,1)} %param.14, bf16[1024,1280]{0,1:T(8,128)(2,1)} %all-gather.5.cloned.1.call-done), kind=kOutput, calls=%fused_computation.21 | convolution fusion | flops 842137600 | bytes 5406732 | tf_op jit(solution)/shard_map/bi,oi->bo/dot_general | solution.py:43
  156.6 1.1 copy-done.19
  157.7 3.1 convolution_convert_fusion.2
  160.8 0.2 reduce-scatter.5.cloned.1.call-start
  161.0 28.6 %reduce-scatter.3.cloned.1.call-done = bf16[1024,320]{0,1:T(8,128)(2,1)} async-done(((bf16[1024,1280]{0,1:T(8,128)(2,1)}), bf16[1024,320]{0,1:T(8,128)(2,1)}) %reduce-scatter.3.cloned.1.call-update) | async-done | bytes 655376 | tf_op jit(solution)/shard_map/reduce_scatter | solution.py:60
  189.6 2.5 multiply_reduce_fusion.2
  192.1 0.8 copy-done.9
  193.0 8.2 %convolution_convert_fusion = bf16[1024,5120]{1,0:T(8,128)(2,1)} fusion(bf16[1024,320]{0,1:T(8,128)(2,1)S(1)} %get-tuple-element.42, bf16[320,5120]{1,0:T(8,128)(2,1)S(1)} %copy-done), kind=kOutput, calls=%fused_computation.1 | convolution fusion | flops 3360686080 | bytes 14417920 | tf_op jit(solution)/shard_map/dot_general | solution.py:58
  201.2 0.0 all-reduce.5.cloned.1.call-start
  201.3 0.6 pad_maximum_fusion.1
  201.9 77.4 %reduce-scatter.5.cloned.1.call-done = bf16[1024,1280]{1,0:T(8,128)(2,1)} async-done(((bf16[1024,5120]{1,0:T(8,128)(2,1)}), bf16[1024,1280]{1,0:T(8,128)(2,1)}) %reduce-scatter.5.cloned.1.call-update) | async-done | bytes 2621456 | tf_op jit(solution)/shard_map/reduce_scatter | solution.py:60
  279.2 5.5 %fusion.5 = (bf16[1024,1280]{1,0:T(8,128)(2,1)S(1)}, f32[]{:T(128)}) fusion(f32[1024,1280]{1,0:T(8,128)} %get-tuple-element.44, f32[]{:T(128)} %sqrt.21, bf16[1024,1280]{1,0:T(8,128)(2,1)} %reduce-scatter.5.cloned.1.call-done), kind=kLoop, calls=%fused_computation.16 | loop fusion | flops 10485759 | bytes 10485768 | tf_op jit(solution)/shard_map/convert_element_type | solution.py:54
  284.7 1.5 copy-done.6
  286.2 4.8 %convolution_convert_fusion.1 = bf16[1024,1280]{1,0:T(8,128)(2,1)} fusion(bf16[1024,1280]{1,0:T(8,128)(2,1)S(1)} %get-tuple-element.37, bf16[1280,1280]{1,0:T(8,128)(2,1)S(1)} %copy-done.3), kind=kOutput, calls=%fused_computation.12 | convolution fusion | flops 3356753920 | bytes 8519680 | tf_op jit(solution)/shard_map/dot_general | solution.py:58
  291.1 6.6 %all-reduce = (f32[]{:T(128)}, f32[]{:T(128)}, f32[]{:T(128)}, f32[]{:T(128)}) all-reduce(f32[]{:T(128)} %get-tuple-element.14, f32[]{:T(128)} %get-tuple-element.38, f32[]{:T(128)} %get-tuple-element.41, f32[]{:T(128)} %get-tuple-element.13), channel_id=1, replica_groups=mesh['rep'=2,'model'=4] {'model'}, use_global_device_ids=true, to_apply=%region_13.14 | all-reduce | flops 4 | bytes 32 | tf_op jit(solution)/shard_map/psum | solution.py:49
  297.6 1.2 broadcast_multiply_fusion.2
  298.9 1.3 broadcast_multiply_fusion.1
  300.2 9.7 %fusion.1 = f32[320,5120]{1,0:T(8,128)} fusion(bf16[1024,320]{0,1:T(8,128)(2,1)S(1)} %copy-done.10, bf16[1024,5120]{1,0:T(8,128)(2,1)} %all-gather.3.cloned.1.call-done, f32[]{:T(128)S(6)} %mul.147, f32[5120]{0:T(1024)S(1)} %get-tuple-element.34, f32[320]{0:T(512)S(1)} %get-tuple-element.27), kind=kOutput, calls=%fused_computation.6 | convolution fusion | flops 3360358400 | bytes 17716484 | tf_op jit(solution)/shard_map/bo,bi->oi/dot_general | solution.py:55
  309.9 2.3 fusion.4
  312.2 1.2 broadcast_multiply_fusion
  314.2 7.4 %fusion = f32[1280,1280]{1,0:T(8,128)} fusion(bf16[1024,1280]{1,0:T(8,128)(2,1)S(1)} %copy-done.7, bf16[1024,1280]{1,0:T(8,128)(2,1)} %copy-done.8, f32[]{:T(128)S(6)} %mul.140, f32[1280]{0:T(1024)S(1)} %get-tuple-element.36, f32[1280]{0:T(1024)S(1)} %get-tuple-element.29), kind=kOutput, calls=%fused_computation.2 | convolution fusion | flops 3360358400 | bytes 11806724 | tf_op jit(solution)/shard_map/bo,bi->oi/dot_general | solution.py:55
  321.6 23.9 %all-reduce.5.cloned.1.call-done = bf16[1024,1280]{1,0:T(8,128)(2,1)} async-done(((bf16[1024,1280]{1,0:T(8,128)(2,1)}), bf16[1024,1280]{1,0:T(8,128)(2,1)}) %all-reduce.5.cloned.1.call-update) | async-done | bytes 2621456 | tf_op jit(solution)/shard_map/psum | solution.py:63
  345.4 2.1 convert_divide_fusion
  347.6 2.8 fusion.15
  350.4 0.6 copy-done.1
  (54 shorter events, 0.3 us)
Async XLA Ops:
  7.2 5.0 %copy-start = (bf16[320,5120]{1,0:T(8,128)(2,1)S(1)}, bf16[320,5120]{1,0:T(8,128)(2,1)}, u32[]{:S(2)}) copy-start(bf16[320,5120]{1,0:T(8,128)(2,1)} %param.13) | copy-start | bytes 9830404
  7.2 114.0 %all-gather.3.cloned.1.call-start = ((), (), s32[]{:S(2)}) async-start(), calls=%async_computation.2 | async-start | bytes 13107200 | tf_op jit(solution)/shard_map/all_gather | solution.py:46
  9.6 3.1 copy-start.4
  27.8 286.4 %copy-start.12 = (f32[1280]{0:T(1024)}, f32[1280]{0:T(1024)S(1)}, u32[]{:S(2)}) copy-start(f32[1280]{0:T(1024)S(1)} %get-tuple-element.36) | copy-start | bytes 15364
  32.7 267.5 %copy-start.11 = (f32[5120]{0:T(1024)}, f32[5120]{0:T(1024)S(1)}, u32[]{:S(2)}) copy-start(f32[5120]{0:T(1024)S(1)} %get-tuple-element.34) | copy-start | bytes 61444
  35.0 274.9 %copy-start.13 = (f32[1280]{0:T(1024)}, f32[1280]{0:T(1024)S(1)}, u32[]{:S(2)}) copy-start(f32[1280]{0:T(1024)S(1)} %get-tuple-element.32) | copy-start | bytes 15364
  44.2 3.0 copy-start.2
  47.2 5.8 %copy-start.8 = (bf16[1024,1280]{1,0:T(8,128)(2,1)}, bf16[1024,1280]{1,0:T(8,128)(2,1)S(1)}, u32[]{:S(2)}) copy-start(bf16[1024,1280]{1,0:T(8,128)(2,1)S(1)} %constant_dynamic-update-slice_fusion) | copy-start | bytes 7864324
  53.0 99.6 %all-gather.5.cloned.1.call-start = ((), (), s32[]{:S(2)}) async-start(), calls=%async_computation.3 | async-start | bytes 3276800 | tf_op jit(solution)/shard_map/all_gather | solution.py:46
  130.1 59.6 %reduce-scatter.3.cloned.1.call-start = ((), (), s32[]{:S(2)}) async-start(), calls=%async_computation.4 | async-start | bytes 3276800 | tf_op jit(solution)/shard_map/reduce_scatter | solution.py:60
  152.6 5.0 %copy-start.5 = (bf16[320,1280]{1,0:T(8,128)(2,1)S(1)}, bf16[320,1280]{1,0:T(8,128)(2,1)}, u32[]{:S(2)}) copy-start(bf16[320,1280]{1,0:T(8,128)(2,1)} %param.14) | copy-start | bytes 2457604
  152.6 5.0 %copy-start.15 = (bf16[512,320]{0,1:T(8,128)(2,1)S(1)}, bf16[512,320]{0,1:T(8,128)(2,1)}, u32[]{:S(2)}) copy-start(bf16[512,320]{0,1:T(8,128)(2,1)} %param.19) | copy-start | bytes 983044
  152.6 5.0 %copy-start.17 = (bf16[512,320]{0,1:T(8,128)(2,1)S(1)}, bf16[512,320]{0,1:T(8,128)(2,1)}, u32[]{:S(2)}) copy-start(bf16[512,320]{0,1:T(8,128)(2,1)} %param.18) | copy-start | bytes 983044
  156.6 1.1 copy-start.19
  160.8 118.5 %reduce-scatter.5.cloned.1.call-start = ((), (), s32[]{:S(2)}) async-start(), calls=%async_computation.5 | async-start | bytes 13107200 | tf_op jit(solution)/shard_map/reduce_scatter | solution.py:60
  192.1 0.8 copy-start.9
  201.2 144.2 %all-reduce.5.cloned.1.call-start = ((), (), s32[]{:S(2)}) async-start(), calls=%async_computation.6 | async-start | bytes 5242880 | tf_op jit(solution)/shard_map/psum | solution.py:63
  279.2 7.0 %copy-start.3 = (bf16[1280,1280]{1,0:T(8,128)(2,1)S(1)}, bf16[1280,1280]{1,0:T(8,128)(2,1)}, u32[]{:S(2)}) copy-start(bf16[1280,1280]{1,0:T(8,128)(2,1)} %param.12) | copy-start | bytes 9830404
  284.7 1.5 copy-start.6
  291.0 9.1 %copy-start.10 = (bf16[1024,320]{0,1:T(8,128)(2,1)S(1)}, bf16[1024,320]{0,1:T(8,128)(2,1)}, u32[]{:S(2)}) copy-start(bf16[1024,320]{0,1:T(8,128)(2,1)} %copy-done.9) | copy-start | bytes 1966084
  300.1 9.8 %copy-start.14 = (bf16[1024,1280]{0,1:T(8,128)(2,1)S(1)}, bf16[1024,1280]{0,1:T(8,128)(2,1)}, u32[]{:S(2)}) copy-start(bf16[1024,1280]{0,1:T(8,128)(2,1)} %all-gather.5.cloned.1.call-done) | copy-start | bytes 7864324
  300.1 9.8 %copy-start.16 = (bf16[512,320]{0,1:T(8,128)(2,1)S(1)}, bf16[512,320]{0,1:T(8,128)(2,1)}, u32[]{:S(2)}) copy-start(bf16[512,320]{0,1:T(8,128)(2,1)} %param.19) | copy-start | bytes 983044
  300.2 9.8 %copy-start.18 = (bf16[512,320]{0,1:T(8,128)(2,1)S(1)}, bf16[512,320]{0,1:T(8,128)(2,1)}, u32[]{:S(2)}) copy-start(bf16[512,320]{0,1:T(8,128)(2,1)} %param.18) | copy-start | bytes 983044
  300.2 9.8 %copy-start.20 = (f32[1024,320]{0,1:T(8,128)S(1)}, f32[1024,320]{0,1:T(8,128)}, u32[]{:S(2)}) copy-start(f32[1024,320]{0,1:T(8,128)} %copy-done.19) | copy-start | bytes 3932164
  309.9 4.2 %copy-start.7 = (bf16[1024,1280]{1,0:T(8,128)(2,1)S(1)}, bf16[1024,1280]{1,0:T(8,128)(2,1)}, u32[]{:S(2)}) copy-start(bf16[1024,1280]{1,0:T(8,128)(2,1)} %copy-done.6) | copy-start | bytes 7864324
  347.6 3.5 copy-start.1
Sparse Core Ops, SparseCore 0:
  53.1 68.0 all-gather.2
  130.2 22.4 all-gather.4
  160.9 28.6 reduce-scatter.2
  201.3 77.8 reduce-scatter.4
  291.2 54.2 all-reduce.4
where the time goes:
time: 359 us
  waiting for transfers between devices  219 us (61%)
  matrix products  62.8 us (17%)
  blocking collectives  26.5 us (7%)
  between operations  20 us (6%)
  other arithmetic  19.8 us (6%)
  local copies, waits for them, and re-layouts  9.94 us (3%)
    reduce_scatter x2, waiting for transfers between devices, local_step(): lax.psum_scatter(part_sum, 'model', scatter_dimension=1, tiled=True)  106 us
    all_gather x2, waiting for transfers between devices, local_step(): lax.all_gather(leaky_relu(y_local).astype(jnp.bfloat16), 'model', axis=1,...  89.3 us
    psum x1, waiting for transfers between devices, local_step(): back_sum = lax.psum(part_sum, 'model').astype(jnp.float32) / sigma_val  23.9 us
    dot_general x3, matrix products, local_step(): jnp.einsum('bo,bi->oi', up_half, inputs[layer_no], preferred_element_type...  19.4 us
    dot_general x3, matrix products, local_step(): jnp.einsum('bi,oi->bo', layer_in, weights[layer_no], preferred_element_ty...  18.6 us
    dot_general x3, matrix products, local_step(): jnp.dot(up_half, weights[layer_no], preferred_element_type=jnp.float32)  16.1 us
    psum x1, blocking collectives, power_step(): p_vec = lax.psum(p_part, 'model')  13.5 us
  transfers between devices with their start and end apart: 5, of which 5 were waited for; matrix products, arithmetic and copies ran while one was open for 7% of the time, Pallas kernels for 0%

commit v1 on v0

v1 whole, which is shorter than its diff:
```python
import jax
import jax.numpy as jnp
from jax import lax
from jax.experimental import pallas as pl
from jax.experimental.pallas import tpu as pltpu
from jax.sharding import PartitionSpec as P

SLOPE = 0.2
EPSILON = 1e-12
MESH = pl.DeviceIdType.MESH
CHUNKS = 4
PIECES = 4
TILE = 256
BF16 = jnp.bfloat16
F32 = jnp.float32


def leaky_relu(values):
    return jnp.where(values > 0, values, SLOPE * values)


def leaky_slope(values):
    return jnp.where(values > 0, 1.0, SLOPE)


def dot_t(left, right):
    return lax.dot_general(left, right, (((1,), (1,)), ((), ())), preferred_element_type=F32)


def dot_n(left, right):
    return lax.dot_general(left, right, (((1,), (0,)), ((), ())), preferred_element_type=F32)


def t_dot(left, right):
    return lax.dot_general(left, right, (((0,), (0,)), ((), ())), preferred_element_type=F32)


def total(values):
    return jnp.sum(jnp.sum(values, axis=1, keepdims=True), axis=0, keepdims=True)


def chain_kernel(x_real, x_fake, w0_in, w1_in, w2_in, u0_in, u1_in, u2_in, t_real, t_fake,
                 x1_out, x2_out, e2_out, e1_out, e0_out, dx_out, v0_out, v1_out, v2_out, u0_out, u1_out, u2_out, sig_out, cor_out,
                 w0, w1, w1x, w2, x0, x1, x2, y0, y1, tt, e2, h2_own, h2_put, h2_got, e1, e0, h0_put, h0_got, dx,
                 p_buf, n_buf, c_buf,
                 load_sem, put_sem, w_send, w_recv, w1x_send, w1x_recv, fwd_send, fwd_recv, small_send, small_recv,
                 x1_send, x1_recv, x2_send, x2_recv, h2_send, h2_recv, e1_send, e1_recv, h0_send, h0_recv, out_send, out_recv, dx_sem, dx_send, dx_recv):
    me = lax.axis_index("model")
    chip = me // 2
    core = me % 2
    other = 1 - chip
    mate = me + 1 - 2 * core
    far = me + 2 - 4 * chip
    diag = mate + 2 - 4 * chip
    n_rows, n0 = x0.shape
    wide1 = w0.shape[0]
    rows1 = wide1 // 2
    wide2 = w2.shape[0]
    rows2 = wide2 // 2
    n1 = 2 * wide1
    step = n_rows // CHUNKS
    piece = rows2 // PIECES

    def send(src, dst, send_sem, recv_sem, device):
        return pltpu.make_async_remote_copy(src_ref=src, dst_ref=dst, send_sem=send_sem, recv_sem=recv_sem, device_id={"model": device}, device_id_type=MESH)

    def part(index, size):
        return pl.ds(pl.multiple_of(index * size, size), size)

    barrier = pltpu.get_barrier_semaphore()
    for device in (mate, far, diag):
        pl.semaphore_signal(barrier, inc=1, device_id={"model": device}, device_id_type=MESH)
    pl.semaphore_wait(barrier, 3)

    def w1x_copy(piece_no):
        return send(
            w1_in.at[pl.ds(piece_no * piece, piece), part(other, wide1)],
            w1x.at[pl.ds(pl.multiple_of(core * rows2 + piece_no * piece, piece), piece), :],
            w1x_send.at[piece_no], w1x_recv.at[piece_no], far)

    def w1x_forward(piece_no):
        rows = w1x.at[pl.ds(pl.multiple_of(core * rows2 + piece_no * piece, piece), piece), :]
        return send(rows, rows, fwd_send.at[piece_no], fwd_recv.at[piece_no], mate)

    own1, own2 = part(core, rows1), part(core, rows2)
    loads = [
        pltpu.make_async_copy(w0_in, w0.at[own1, :], load_sem.at[0]),
        pltpu.make_async_copy(w1_in, w1.at[own2, :], load_sem.at[1]),
        pltpu.make_async_copy(w2_in, w2.at[own2, :], load_sem.at[2]),
    ]
    gives = [
        send(w0_in, w0.at[own1, :], w_send.at[0], w_recv.at[0], mate),
        send(w1_in, w1.at[own2, :], w_send.at[1], w_recv.at[1], mate),
        send(w2_in, w2.at[own2, :], w_send.at[2], w_recv.at[2], mate),
    ]
    loads[0].start()
    w1x_copy(0).start()
    for copy in loads[1:]:
        copy.start()

    def mine(x_in, t_own, t_mate):
        return (
            pltpu.make_async_copy(x_in, x0, load_sem.at[3]),
            pltpu.make_async_copy(t_own, tt.at[core], load_sem.at[4]),
            send(t_mate, tt.at[core], w_send.at[3], w_recv.at[3], mate),
        )

    @pl.when(core == 0)
    def _():
        for copy in mine(x_real, t_real, t_fake):
            copy.start()

    @pl.when(core == 1)
    def _():
        for copy in mine(x_fake, t_fake, t_real):
            copy.start()

    for copy in gives:
        copy.start()

    def row(values):
        return jnp.broadcast_to(values.astype(BF16), (16, values.shape[1]))

    u_rows = [row(u0_in[...]), row(u1_in[...]), row(u2_in[...])]
    loads[0].wait()
    p_buf[me, :, pl.ds(0, n0)] = dot_n(u_rows[0], w0[own1, :])[0:1]
    loads[1].wait()

    def p1_tile(tile_no, carry):
        cols = part(tile_no, wide1 // 2)
        p_buf[me, :, pl.ds(pl.multiple_of(n0 + tile_no * (wide1 // 2), 128), wide1 // 2)] = dot_n(u_rows[1], w1[own2, cols])[0:1]
        return carry

    lax.fori_loop(0, 4, p1_tile, 0)
    loads[2].wait()
    p_buf[me, :, pl.ds(n0 + n1, wide2 * 2)] = dot_n(u_rows[2], w2[own2, :])[0:1]

    def spread(buf, first):
        return [send(buf.at[me], buf.at[me], small_send.at[first + which], small_recv.at[first + which], device) for which, device in enumerate((mate, far, diag))]

    p_copies = spread(p_buf, 0)
    for copy in p_copies:
        copy.start()
    w1x_copy(1).start()
    for copy in p_copies:
        copy.wait()
    p_all = p_buf[0] + p_buf[1] + p_buf[2] + p_buf[3]
    spans = ((0, n0, v0_out), (n0, n1, v1_out), (n0 + n1, 2 * wide2, v2_out))
    for first, size, v_out in spans:
        p_vec = p_all[:, first:first + size]
        v_out[...] = p_vec / jnp.maximum(jnp.sqrt(total(p_vec * p_vec)), EPSILON)
    u0_out[...] = dot_t(row(v0_out[...]), w0[own1, :])[0:1]
    u1_out[...] = dot_t(row(v1_out[...]), w1[own2, :])[0:1]
    u2_out[...] = dot_t(row(v2_out[...]), w2[own2, :])[0:1]
    lane = lax.broadcasted_iota(jnp.int32, (8, 128), 1)

    def pack(values):
        packed = jnp.zeros((8, 128), F32)
        for place, value in enumerate(values):
            packed = jnp.where(lane == place, value, packed)
        return packed

    n_buf[me] = pack([total(u_out[...] * u_out[...]) for u_out in (u0_out, u1_out, u2_out)])
    n_copies = spread(n_buf, 3)
    for copy in n_copies:
        copy.start()
    for piece_no in range(2, PIECES):
        w1x_copy(piece_no).start()
    for copy in n_copies:
        copy.wait()
    sigmas = jnp.sqrt(n_buf[0] + n_buf[1] + n_buf[2] + n_buf[3])
    sig_out[...] = sigmas
    sig0, sig1, sig2 = sigmas[0:1, 0:1], sigmas[0:1, 1:2], sigmas[0:1, 2:3]
    u0_out[...] = u0_out[...] / sig0
    u1_out[...] = u1_out[...] / sig1
    u2_out[...] = u2_out[...] / sig2

    pltpu.make_async_copy(x_real, x0, load_sem.at[3]).wait()
    gives[0].wait_recv()

    def y0_tile(tile_no, carry):
        cols = part(tile_no, TILE)
        y_tile = dot_t(x0[...], w0[cols, :]) / sig0
        y0[:, cols] = y_tile
        x1[chip, :, cols] = leaky_relu(y_tile).astype(BF16)
        return carry

    lax.fori_loop(0, wide1 // TILE, y0_tile, 0)

    def chunk_copy(buf, slot, chunk_no, send_sem, recv_sem):
        rows = buf.at[slot, part(chunk_no, step), :]
        return send(rows, rows, send_sem.at[chunk_no], recv_sem.at[chunk_no], far)

    for chunk_no in range(CHUNKS):
        chunk_copy(x1, chip, chunk_no, x1_send, x1_recv).start()

    batch = part(core, n_rows)

    def outputs(src, dst, which):
        return (
            pltpu.make_async_copy(src, dst, put_sem.at[which]),
            send(src, dst, out_send.at[which], out_recv.at[which], mate),
        )

    x1_near = outputs(x1.at[chip], x1_out.at[batch, part(chip, wide1)], 0)
    for copy in x1_near:
        copy.start()
    for piece_no in range(PIECES):
        w1x_copy(piece_no).wait_recv()
        w1x_forward(piece_no).start()

    gives[1].wait_recv()

    def layer1(chunk_no, carry):
        rows = part(chunk_no, step)
        chunk_copy(x1, other, chunk_no, x1_send, x1_recv).wait_recv()
        y_val = (dot_t(x1[0, rows, :], w1[:, pl.ds(0, wide1)]) + dot_t(x1[1, rows, :], w1[:, pl.ds(wide1, wide1)])) / sig1
        y1[rows, :] = y_val
        x2[chip, rows, :] = leaky_relu(y_val).astype(BF16)
        chunk_copy(x2, chip, chunk_no, x2_send, x2_recv).start()
        return carry

    lax.fori_loop(0, CHUNKS, layer1, 0)
    x1_far = outputs(x1.at[other], x1_out.at[batch, part(other, wide1)], 1)
    for copy in x1_far:
        copy.start()

    gives[2].wait_recv()
    pltpu.make_async_copy(t_real, tt.at[core], load_sem.at[4]).wait()
    send(t_real, tt.at[core], w_send.at[3], w_recv.at[3], mate).wait_recv()

    def layer2(chunk_no, carry):
        corr2, loss = carry
        rows = part(chunk_no, step)
        chunk_copy(x2, other, chunk_no, x2_send, x2_recv).wait_recv()
        y_val = (dot_t(x2[0, rows, :], w2[:, pl.ds(0, wide2)]) + dot_t(x2[1, rows, :], w2[:, pl.ds(wide2, wide2)])) / sig2
        target = jnp.concatenate([tt[0, rows, :].astype(F32), tt[1, rows, :].astype(F32)], axis=1)
        e_val = y_val - target
        corr2 = corr2 + total(e_val * y_val)
        loss = loss + total(e_val * e_val)
        e_half = e_val.astype(BF16)
        e2[rows, :] = e_half
        h2_put[rows, :] = dot_n(e_half, w2[:, part(other, wide2)]).astype(BF16)
        send(h2_put.at[rows, :], h2_got.at[rows, :], h2_send.at[chunk_no], h2_recv.at[chunk_no], far).start()
        h2_own[rows, :] = dot_n(e_half, w2[:, part(chip, wide2)])
        return corr2, loss

    zero = jnp.zeros((1, 1), F32)
    corr2, loss = lax.fori_loop(0, CHUNKS, layer2, (zero, zero))

    def back1(chunk_no, corr1):
        rows = part(chunk_no, step)
        send(h2_put.at[rows, :], h2_got.at[rows, :], h2_send.at[chunk_no], h2_recv.at[chunk_no], far).wait_recv()
        y_val = y1[rows, :]
        e_val = (h2_own[rows, :] + h2_got[rows, :].astype(F32)) / sig2 * leaky_slope(y_val)
        e1[chip, rows, :] = e_val.astype(BF16)
        chunk_copy(e1, chip, chunk_no, e1_send, e1_recv).start()
        return corr1 + total(e_val * y_val)

    corr1 = lax.fori_loop(0, CHUNKS, back1, zero)
    lesser = [
        outputs(x2.at[0], x2_out.at[batch, pl.ds(0, wide2)], 2),
        outputs(x2.at[1], x2_out.at[batch, pl.ds(wide2, wide2)], 3),
        outputs(e2, e2_out.at[batch, :], 4),
        outputs(e1.at[chip], e1_out.at[batch, :], 5),
    ]
    for pair in lesser:
        for copy in pair:
            copy.start()
    for piece_no in range(PIECES):
        w1x_forward(piece_no).wait_recv()

    def back0(chunk_no, corr0):
        rows = part(chunk_no, step)
        chunk_copy(e1, other, chunk_no, e1_send, e1_recv).wait_recv()

        def h1_tile(tile_no, corr):
            cols = part(tile_no, TILE)
            own_cols = pl.ds(pl.multiple_of(chip * wide1 + tile_no * TILE, TILE), TILE)
            h_val = (dot_n(e1[chip, rows, :], w1[:, own_cols]) + dot_n(e1[other, rows, :], w1x[:, cols])) / sig1
            y_val = y0[rows, cols]
            e_val = h_val * leaky_slope(y_val)
            e0[rows, cols] = e_val.astype(BF16)
            return corr + total(e_val * y_val)

        corr0 = lax.fori_loop(0, wide1 // TILE, h1_tile, corr0)
        h0_put[rows, :] = dot_n(e0[rows, :], w0[...]).astype(BF16)
        send(h0_put.at[rows, :], h0_got.at[rows, :], h0_send.at[chunk_no], h0_recv.at[chunk_no], far).start()
        return corr0

    corr0 = lax.fori_loop(0, CHUNKS, back0, zero)
    e0_near = pltpu.make_async_copy(e0.at[:, part(core, rows1)], e0_out.at[batch, :], put_sem.at[6])
    e0_mate = send(e0.at[:, part(1 - core, rows1)], e0_out.at[batch, :], out_send.at[6], out_recv.at[6], mate)
    e0_near.start()
    e0_mate.start()
    c_buf[me] = pack([corr0, corr1, corr2, loss])
    c_copies = spread(c_buf, 6)
    for copy in c_copies:
        copy.start()

    def dx_copies(chunk_no):
        rows = part(chunk_no, step)
        dst = dx_out.at[pl.ds(pl.multiple_of(core * n_rows + chunk_no * step, step), step), :]
        return (
            pltpu.make_async_copy(dx.at[rows, :], dst, dx_sem.at[chunk_no]),
            send(dx.at[rows, :], dst, dx_send.at[chunk_no], dx_recv.at[chunk_no], mate),
        )

    def finish(chunk_no, carry):
        rows = part(chunk_no, step)
        send(h0_put.at[rows, :], h0_got.at[rows, :], h0_send.at[chunk_no], h0_recv.at[chunk_no], far).wait_recv()
        dx[rows, :] = (h0_put[rows, :].astype(F32) + h0_got[rows, :].astype(F32)) / sig0
        for copy in dx_copies(chunk_no):
            copy.start()
        return carry

    lax.fori_loop(0, CHUNKS, finish, 0)
    for copy in c_copies:
        copy.wait()
    cor_out[...] = c_buf[0] + c_buf[1] + c_buf[2] + c_buf[3]

    for copy in gives:
        copy.wait_send()
    send(t_real, tt.at[core], w_send.at[3], w_recv.at[3], mate).wait_send()
    for piece_no in range(PIECES):
        w1x_copy(piece_no).wait_send()
        w1x_forward(piece_no).wait_send()
    for pair in (x1_near, x1_far, *lesser, (e0_near, e0_mate)):
        for copy in pair:
            copy.wait()

    def drain(chunk_no, carry):
        rows = part(chunk_no, step)
        chunk_copy(x1, chip, chunk_no, x1_send, x1_recv).wait_send()
        chunk_copy(x2, chip, chunk_no, x2_send, x2_recv).wait_send()
        send(h2_put.at[rows, :], h2_got.at[rows, :], h2_send.at[chunk_no], h2_recv.at[chunk_no], far).wait_send()
        chunk_copy(e1, chip, chunk_no, e1_send, e1_recv).wait_send()
        send(h0_put.at[rows, :], h0_got.at[rows, :], h0_send.at[chunk_no], h0_recv.at[chunk_no], far).wait_send()
        for copy in dx_copies(chunk_no):
            copy.wait()
        return carry

    lax.fori_loop(0, CHUNKS, drain, 0)


def run_chain(x_real, x_fake, weight0, weight1, weight2, u_left0, u_left1, u_left2, t_real, t_fake):
    n_rows, n0 = x_real.shape
    rows1 = weight0.shape[0]
    rows2, n1 = weight1.shape
    wide1, wide2 = 2 * rows1, 2 * rows2
    n2 = 2 * wide2
    hbm = pl.BlockSpec(memory_space=pl.ANY)
    vmem = pl.BlockSpec(memory_space=pltpu.VMEM)
    shape = jax.ShapeDtypeStruct
    dma = pltpu.SemaphoreType.DMA
    return pl.pallas_call(
        chain_kernel,
        out_shape=(
            shape((2 * n_rows, n1), BF16), shape((2 * n_rows, n2), BF16), shape((2 * n_rows, wide2), BF16), shape((2 * n_rows, wide2), BF16),
            shape((2 * n_rows, rows1), BF16), shape((2 * n_rows, n0), F32),
            shape((1, n0), F32), shape((1, n1), F32), shape((1, n2), F32),
            shape((1, rows1), F32), shape((1, rows2), F32), shape((1, rows2), F32),
            shape((8, 128), F32), shape((8, 128), F32),
        ),
        in_specs=[hbm] * 5 + [vmem] * 3 + [hbm] * 2,
        out_specs=[hbm] * 6 + [vmem] * 8,
        scratch_shapes=[
            pltpu.VMEM((wide1, n0), BF16), pltpu.VMEM((wide2, n1), BF16), pltpu.VMEM((wide2, wide1), BF16), pltpu.VMEM((wide2, n2), BF16),
            pltpu.VMEM((n_rows, n0), BF16), pltpu.VMEM((2, n_rows, wide1), BF16), pltpu.VMEM((2, n_rows, wide2), BF16),
            pltpu.VMEM((n_rows, wide1), F32), pltpu.VMEM((n_rows, wide2), F32), pltpu.VMEM((2, n_rows, rows2), BF16),
            pltpu.VMEM((n_rows, wide2), BF16), pltpu.VMEM((n_rows, wide2), F32), pltpu.VMEM((n_rows, wide2), BF16), pltpu.VMEM((n_rows, wide2), BF16),
            pltpu.VMEM((2, n_rows, wide2), BF16), pltpu.VMEM((n_rows, wide1), BF16),
            pltpu.VMEM((n_rows, n0), BF16), pltpu.VMEM((n_rows, n0), BF16), pltpu.VMEM((n_rows, n0), F32),
            pltpu.VMEM((4, 1, n0 + n1 + n2), F32), pltpu.VMEM((4, 8, 128), F32), pltpu.VMEM((4, 8, 128), F32),
            dma((5,)), dma((7,)), dma((4,)), dma((4,)), dma((PIECES,)), dma((PIECES,)), dma((PIECES,)), dma((PIECES,)), dma((9,)), dma((9,)),
            dma((CHUNKS,)), dma((CHUNKS,)), dma((CHUNKS,)), dma((CHUNKS,)), dma((CHUNKS,)), dma((CHUNKS,)),
            dma((CHUNKS,)), dma((CHUNKS,)), dma((CHUNKS,)), dma((CHUNKS,)), dma((7,)), dma((7,)), dma((CHUNKS,)), dma((CHUNKS,)), dma((CHUNKS,)),
        ],
        compiler_params=pltpu.CompilerParams(collective_id=0, has_side_effects=True, vmem_limit_bytes=60 * 1024 * 1024),
        name="chain",
    )(x_real, x_fake, weight0, weight1, weight2, u_left0[None, :], u_left1[None, :], u_left2[None, :], t_real, t_fake)


def solution(mesh):
    rows_spec = P("rep", None)
    weight_spec = P(("rep", "model"), None)
    left_spec = P(("rep", "model"))
    target_spec = P("rep", "model")
    group_spec = P("rep")

    def local_step(x_real, x_fake, weight0, weight1, weight2, u_left0, u_left1, u_left2, t_real, t_fake):
        core = lax.axis_index("model") % 2
        n_rows = x_real.shape[0]
        rows2 = weight1.shape[0]
        x1, x2, e2, e1, e0, dx, v0, v1, v2, u0, u1, u2, sig, cor = run_chain(x_real, x_fake, weight0, weight1, weight2, u_left0, u_left1, u_left2, t_real, t_fake)
        x0 = jnp.concatenate([x_real, x_fake], axis=0)
        e2_own = lax.dynamic_slice(e2, (0, core * rows2), (2 * n_rows, rows2))
        e1_own = lax.dynamic_slice(e1, (0, core * rows2), (2 * n_rows, rows2))

        def gradient(up_half, layer_in, layer_no, u_new, v_new):
            return (t_dot(up_half, layer_in) - cor[0, layer_no] * u_new[0][:, None] * v_new) / (n_rows * sig[0, layer_no])

        dw0 = gradient(e0, x0, 0, u0, v0)
        dw1 = gradient(e1_own, x1, 1, u1, v1)
        dw2 = gradient(e2_own, x2, 2, u2, v2)
        loss_val = cor[0, 3:4] * (0.5 / n_rows)
        return (loss_val, dx[:n_rows], dx[n_rows:], dw0, dw1, dw2, u0[0], u1[0], u2[0], v0[0], v1[0], v2[0], sig[0, :3])

    return jax.shard_map(local_step, mesh=mesh, in_specs=(rows_spec, rows_spec, weight_spec, weight_spec, weight_spec, left_spec, left_spec, left_spec, target_spec, target_spec), out_specs=(group_spec, rows_spec, rows_spec, weight_spec, weight_spec, weight_spec, left_spec, left_spec, left_spec, group_spec, group_spec, group_spec, group_spec), check_vma=False)
```

time: 359 us -> 218 us (0.61)
  waiting for transfers between devices: 219 us -> 0 us
  Pallas kernels: 0 us -> 172 us
  matrix products: 62.8 us -> 24.1 us
  blocking collectives: 26.5 us -> 0 us
  other arithmetic: 19.8 us -> 3.37 us
  between operations: 20 us -> 4.6 us
  local copies, waits for them, and re-layouts: 9.94 us -> 13.6 us
    pallas_call x0 -> x1, Pallas kernels: none -> 172 us  [run_chain(): pl.pallas_call(chain_kernel, out_shape=(shape((2 * n_rows, n1), BF16), sh...]
    reduce_scatter x2 -> x0, waiting for transfers between devices: 106 us -> none  [local_step(): lax.psum_scatter(part_sum, 'model', scatter_dimension=1, tiled=True)]
    all_gather x2 -> x0, waiting for transfers between devices: 89.3 us -> none  [local_step(): lax.all_gather(leaky_relu(y_local).astype(jnp.bfloat16), 'model', axis=1,...]
    dot_general x15 -> x3, matrix products: 62.8 us -> 24.1 us  [t_dot(): lax.dot_general(left, right, (((0,), (0,)), ((), ())), preferred_element_...]
    psum x3 -> x0, blocking collectives: 26.5 us -> none  [the longest x1 13.5 us: power_step(): p_vec = lax.psum(p_part, 'model')]
    psum x1 -> x0, waiting for transfers between devices: 23.9 us -> none  [local_step(): back_sum = lax.psum(part_sum, 'model').astype(jnp.float32) / sigma_val]
    convert_element_type x7 -> x0, other arithmetic: 7.82 us -> none  [the longest x1 5.49 us: local_step(): up_half = upstream.astype(jnp.bfloat16)]
    reduce_sum x6 -> x0, other arithmetic: 5.53 us -> none  [the longest x1 2.51 us: local_step(): corr_sum = lax.psum(jnp.sum(upstream * outputs[layer_no]), 'model')]
  transfers between devices with their start and end apart: 5 -> 0, of which waited for: 5 -> 0; matrix products, arithmetic and copies ran while one was open for 7% -> 0% of each run, Pallas kernels for 0% -> 0%
where the time goes in v1:
time: 218 us
  Pallas kernels  172 us (79%)
  matrix products  24.1 us (11%)
  local copies, waits for them, and re-layouts  13.6 us (6%)
  between operations  4.6 us (2%)
  other arithmetic  3.37 us (2%)
    pallas_call x1, Pallas kernels, run_chain(): pl.pallas_call(chain_kernel, out_shape=(shape((2 * n_rows, n1), BF16), sh...  172 us
    dot_general x3, matrix products, t_dot(): lax.dot_general(left, right, (((0,), (0,)), ((), ())), preferred_element_...  24.1 us
    unnamed x29, local copies, waits for them, and re-layouts  4.46 us

profile of v1, /device:TPU:0, one launch (start us, length us, event | category | flops | bytes accessed | tf_op | source)
XLA Modules:
  0.0 217.6 jit_solution(11287913392959327886)
XLA Ops:
  0.7 1.9 copy.23.t_real
  2.6 1.9 copy.24.t_fake
  4.4 1.3 broadcast_in_dim.9.u0_in
  5.7 1.2 broadcast_in_dim.10.u1_in
  7.0 1.2 broadcast_in_dim.11.u2_in
  8.2 172.0 %chain.1 = (bf16[1024,5120]{1,0:T(8,128)(2,1)}, bf16[1024,1280]{1,0:T(8,128)(2,1)}, bf16[1024,640]{1,0:T(8,128)(2,1)}, bf16[1024,640]{1,0:T(8,128)(2,1)}, bf16[1...) custom-call(bf16[512,1280]{1,0:T(8,128)(2,1)} %x_real.1, ...), custom_call_target="tpu_custom_call" | custom-call | tf_op jit(solution)/shard_map/chain/pallas_call | solution.py:356
  180.3 1.4 fusion.12
  181.7 0.6 reduce.3
  182.3 0.0 copy-start.6
  182.4 0.7 broadcast_multiply_fusion.1
  183.7 0.7 reduce.4
  184.4 0.0 copy-start.4
  184.4 0.0 copy-start.10
  184.4 0.0 copy-start.3
  184.4 4.5 %fusion.2 = f32[320,1280]{1,0:T(8,128)} fusion(bf16[1024,1280]{1,0:T(8,128)(2,1)} %get-tuple-element.38, f32[]{:T(128)} %bitcast.7, f32[1280]{0:T(1024)S(1)} %reduce.4, f32[320]{0:T(512)S(1)} %broadcast_multiply_fusion.1, bf16[1024,640]{1,0:T(8,128)(2,1)} %get-tuple-element.37, s32[]{:T(128)S(6)} %select_n.12), kind=kOutput, calls=%fused_computation.5 | convolution fusion | flops 840089600 | bytes 5053188 | tf_op jit(solution)/shard_map/dot_general | solution.py:35
  188.9 0.0 copy-done.6
  188.9 0.0 copy-done.4
  188.9 0.0 copy-done.10
  188.9 0.0 copy-start.7
  188.9 0.7 broadcast_multiply_fusion.2
  190.2 0.0 copy-done.3
  190.3 0.0 copy-start.9
  190.3 0.0 copy-start.8
  190.3 0.0 copy-start
  190.3 0.0 copy-start.1
  190.3 11.2 %fusion.1 = f32[320,5120]{1,0:T(8,128)} fusion(bf16[1024,5120]{1,0:T(8,128)(2,1)} %get-tuple-element.34, f32[]{:T(128)} %bitcast.5, f32[5120]{0:T(1024)S(1)} %bitcast.15, f32[320]{0:T(512)S(1)} %broadcast_multiply_fusion.2, bf16[1024,640]{1,0:T(8,128)(2,1)} %get-tuple-element.33, s32[]{:T(128)S(6)} %select_n.12), kind=kOutput, calls=%fused_computation.3 | convolution fusion | flops 3360358400 | bytes 17848068 | tf_op jit(solution)/shard_map/dot_general | solution.py:35
  201.5 0.0 copy-done.7
  201.5 0.0 copy-done.9
  201.5 0.0 copy-start.2
  201.5 0.7 broadcast_multiply_fusion
  202.8 0.0 copy-done.8
  202.9 0.0 copy-start.5
  202.9 0.0 slice-start
  202.9 0.0 copy-done
  202.9 0.0 copy-done.1
  202.9 0.0 slice-start.1
  202.9 8.4 %fusion = f32[1280,1280]{1,0:T(8,128)} fusion(bf16[1024,1280]{1,0:T(8,128)(2,1)} %get-tuple-element.29, f32[]{:T(128)} %bitcast.2, f32[1280]{0:T(1024)S(1)} %reduce.1, f32[1280]{0:T(1024)S(1)} %broadcast_multiply_fusion, bf16[512,1280]{1,0:T(8,128)(2,1)S(1)} %copy-done.1, bf16[512,1280]{1,0:T(8,128)(2,1)S(1)} %copy-done), kind=kOutput, calls=%fused_computation.1 | convolution fusion | flops 3365601280 | bytes 11806724 | tf_op jit(solution)/shard_map/dot_general | solution.py:35
  211.3 0.0 copy-done.2
  211.3 0.0 copy-done.5
  212.0 0.0 slice-done
  212.0 0.0 slice-done.1
  212.0 2.7 %fusion.11 = (f32[512,1280]{1,0:T(8,128)}, f32[512,1280]{1,0:T(8,128)}) fusion(f32[1024,1280]{1,0:T(8,128)S(1)} %bitcast.14), kind=kLoop, calls=%fused_computation.18 | loop fusion | bytes 10485760 | tf_op jit(solution)/shard_map/slice | solution.py:407
  214.7 1.2 slice_bitcast_fusion
  215.9 0.6 copy.26
  (4 shorter events, 0.1 us)
Async XLA Ops:
  182.3 6.6 %copy-start.6 = (f32[320]{0:T(512)}, f32[320]{0:T(512)S(1)}, u32[]{:S(2)}) copy-start(f32[320]{0:T(512)S(1)} %reduce.3) | copy-start | bytes 3844
  184.4 4.5 %copy-start.4 = (f32[1280]{0:T(1024)}, f32[1280]{0:T(1024)S(1)}, u32[]{:S(2)}) copy-start(f32[1280]{0:T(1024)S(1)} %reduce.4) | copy-start | bytes 15364
  184.4 4.5 %copy-start.10 = (f32[1,320]{1,0:T(1,128)S(1)}, f32[1,320]{1,0:T(1,128)}, u32[]{:S(2)}) copy-start(f32[1,320]{1,0:T(1,128)} %get-tuple-element.35) | copy-start | bytes 3844
  184.4 5.8 %copy-start.3 = (f32[1,5120]{1,0:T(1,128)S(1)}, f32[1,5120]{1,0:T(1,128)}, u32[]{:S(2)}) copy-start(f32[1,5120]{1,0:T(1,128)} %get-tuple-element.36) | copy-start | bytes 61444
  188.9 12.6 %copy-start.7 = (f32[320]{0:T(512)}, f32[320]{0:T(512)S(1)}, u32[]{:S(2)}) copy-start(f32[320]{0:T(512)S(1)} %reduce.2) | copy-start | bytes 3844
  190.3 11.2 %copy-start.9 = (f32[1,1280]{1,0:T(1,128)S(1)}, f32[1,1280]{1,0:T(1,128)}, u32[]{:S(2)}) copy-start(f32[1,1280]{1,0:T(1,128)} %get-tuple-element.30) | copy-start | bytes 15364
  190.3 12.6 %copy-start.8 = (f32[1,1280]{1,0:T(1,128)S(1)}, f32[1,1280]{1,0:T(1,128)}, u32[]{:S(2)}) copy-start(f32[1,1280]{1,0:T(1,128)} %get-tuple-element.31) | copy-start | bytes 15364
  190.3 12.6 %copy-start = (bf16[512,1280]{1,0:T(8,128)(2,1)S(1)}, bf16[512,1280]{1,0:T(8,128)(2,1)}, u32[]{:S(2)}) copy-start(bf16[512,1280]{1,0:T(8,128)(2,1)} %x_real.1) | copy-start | bytes 3932164
  190.3 12.6 %copy-start.1 = (bf16[512,1280]{1,0:T(8,128)(2,1)S(1)}, bf16[512,1280]{1,0:T(8,128)(2,1)}, u32[]{:S(2)}) copy-start(bf16[512,1280]{1,0:T(8,128)(2,1)} %x_fake.1) | copy-start | bytes 3932164
  201.5 9.8 %copy-start.2 = (f32[1280]{0:T(1024)}, f32[1280]{0:T(1024)S(1)}, u32[]{:S(2)}) copy-start(f32[1280]{0:T(1024)S(1)} %reduce) | copy-start | bytes 15364
  202.9 8.5 %copy-start.5 = (f32[1280]{0:T(1024)}, f32[1280]{0:T(1024)S(1)}, u32[]{:S(2)}) copy-start(f32[1280]{0:T(1024)S(1)} %reduce.1) | copy-start | bytes 15364
  202.9 9.1 %slice-start = ((s8[5242880]{0:T(1024)(128)(4,1)}), s8[4194304]{0:T(1024)(128)(4,1)S(1)}, s32[]{:S(2)}) async-start(s8[5242880]{0:T(1024)(128)(4,1)} %bitcast.13), calls=%async_computation | async-start | bytes 8388608
  202.9 9.1 %slice-start.1 = ((s8[5242880]{0:T(1024)(128)(4,1)}), s8[1048576]{0:T(1024)(128)(4,1)S(1)}, s32[]{:S(2)}) async-start(s8[5242880]{0:T(1024)(128)(4,1)} %bitcast.13), calls=%async_computation.1 | async-start | bytes 2097152

commit v2 on v1

--- a/solution.py
+++ b/solution.py
@@ -41,9 +41,9 @@
 
 def chain_kernel(x_real, x_fake, w0_in, w1_in, w2_in, u0_in, u1_in, u2_in, t_real, t_fake,
                  x1_out, x2_out, e2_out, e1_out, e0_out, dx_out, v0_out, v1_out, v2_out, u0_out, u1_out, u2_out, sig_out, cor_out,
-                 w0, w1, w1x, w2, x0, x1, x2, y0, y1, tt, e2, h2_own, h2_put, h2_got, e1, e0, h0_put, h0_got, dx,
+                 w0, w1, w1x, w2, x0, x1, x2, y0, y1, tt, e2_t, h2_own, h2_put, h2_got, e1, e1_t, e0, e0_t, h0_put, h0_got, dx,
                  p_buf, n_buf, c_buf,
-                 load_sem, put_sem, w_send, w_recv, w1x_send, w1x_recv, fwd_send, fwd_recv, small_send, small_recv,
+                 eye, load_sem, put_sem, w_send, w_recv, w1x_send, w1x_recv, fwd_send, fwd_recv, small_send, small_recv,
                  x1_send, x1_recv, x2_send, x2_recv, h2_send, h2_recv, e1_send, e1_recv, h0_send, h0_recv, out_send, out_recv, dx_sem, dx_send, dx_recv):
     me = lax.axis_index("model")
     chip = me // 2
@@ -101,8 +101,8 @@
     def mine(x_in, t_own, t_mate):
         return (
             pltpu.make_async_copy(x_in, x0, load_sem.at[3]),
-            pltpu.make_async_copy(t_own, tt.at[core], load_sem.at[4]),
-            send(t_mate, tt.at[core], w_send.at[3], w_recv.at[3], mate),
+            pltpu.make_async_copy(t_own, tt.at[own2, :], load_sem.at[4]),
+            send(t_mate, tt.at[own2, :], w_send.at[3], w_recv.at[3], mate),
         )
 
     @pl.when(core == 0)
@@ -119,7 +119,15 @@
         copy.start()
 
     def row(values):
-        return jnp.broadcast_to(values.astype(BF16), (16, values.shape[1]))
+        return jnp.broadcast_to(values.reshape(1, values.size).astype(BF16), (16, values.size))
+
+    lanes = lax.broadcasted_iota(jnp.int32, (128, 128), 1)
+    eye[...] = jnp.where(lanes == lax.broadcasted_iota(jnp.int32, (128, 128), 0), 1.0, 0.0).astype(BF16)
+
+    def store_transposed(dst, first, rows, values):
+        for place in range(values.shape[1] // 128):
+            block = dot_t(eye[...], values[:, place * 128:(place + 1) * 128])
+            dst[pl.ds(pl.multiple_of(first + place * 128, 128), 128), rows] = block.astype(BF16)
 
     u_rows = [row(u0_in[...]), row(u1_in[...]), row(u2_in[...])]
     loads[0].wait()
@@ -202,6 +210,12 @@
             send(src, dst, out_send.at[which], out_recv.at[which], mate),
         )
 
+    def halves(src, dst, size, which):
+        return (
+            pltpu.make_async_copy(src.at[part(core, size), :], dst.at[:, batch], put_sem.at[which]),
+            send(src.at[part(1 - core, size), :], dst.at[:, batch], out_send.at[which], out_recv.at[which], mate),
+        )
+
     x1_near = outputs(x1.at[chip], x1_out.at[batch, part(chip, wide1)], 0)
     for copy in x1_near:
         copy.start()
@@ -226,23 +240,23 @@
         copy.start()
 
     gives[2].wait_recv()
-    pltpu.make_async_copy(t_real, tt.at[core], load_sem.at[4]).wait()
-    send(t_real, tt.at[core], w_send.at[3], w_recv.at[3], mate).wait_recv()
+    pltpu.make_async_copy(t_real, tt.at[own2, :], load_sem.at[4]).wait()
+    t_give = send(t_real, tt.at[own2, :], w_send.at[3], w_recv.at[3], mate)
+    t_give.wait_recv()
 
     def layer2(chunk_no, carry):
         corr2, loss = carry
         rows = part(chunk_no, step)
         chunk_copy(x2, other, chunk_no, x2_send, x2_recv).wait_recv()
         y_val = (dot_t(x2[0, rows, :], w2[:, pl.ds(0, wide2)]) + dot_t(x2[1, rows, :], w2[:, pl.ds(wide2, wide2)])) / sig2
-        target = jnp.concatenate([tt[0, rows, :].astype(F32), tt[1, rows, :].astype(F32)], axis=1)
-        e_val = y_val - target
+        e_val = y_val - dot_t(eye[...], tt[:, rows])
         corr2 = corr2 + total(e_val * y_val)
         loss = loss + total(e_val * e_val)
         e_half = e_val.astype(BF16)
-        e2[rows, :] = e_half
         h2_put[rows, :] = dot_n(e_half, w2[:, part(other, wide2)]).astype(BF16)
         send(h2_put.at[rows, :], h2_got.at[rows, :], h2_send.at[chunk_no], h2_recv.at[chunk_no], far).start()
         h2_own[rows, :] = dot_n(e_half, w2[:, part(chip, wide2)])
+        store_transposed(e2_t, 0, rows, e_half)
         return corr2, loss
 
     zero = jnp.zeros((1, 1), F32)
@@ -253,16 +267,18 @@
         send(h2_put.at[rows, :], h2_got.at[rows, :], h2_send.at[chunk_no], h2_recv.at[chunk_no], far).wait_recv()
         y_val = y1[rows, :]
         e_val = (h2_own[rows, :] + h2_got[rows, :].astype(F32)) / sig2 * leaky_slope(y_val)
-        e1[chip, rows, :] = e_val.astype(BF16)
+        e_half = e_val.astype(BF16)
+        e1[chip, rows, :] = e_half
         chunk_copy(e1, chip, chunk_no, e1_send, e1_recv).start()
+        store_transposed(e1_t, 0, rows, e_half)
         return corr1 + total(e_val * y_val)
 
     corr1 = lax.fori_loop(0, CHUNKS, back1, zero)
     lesser = [
         outputs(x2.at[0], x2_out.at[batch, pl.ds(0, wide2)], 2),
         outputs(x2.at[1], x2_out.at[batch, pl.ds(wide2, wide2)], 3),
-        outputs(e2, e2_out.at[batch, :], 4),
-        outputs(e1.at[chip], e1_out.at[batch, :], 5),
+        halves(e2_t, e2_out, rows2, 4),
+        halves(e1_t, e1_out, rows2, 5),
     ]
     for pair in lesser:
         for copy in pair:
@@ -280,19 +296,20 @@
             h_val = (dot_n(e1[chip, rows, :], w1[:, own_cols]) + dot_n(e1[other, rows, :], w1x[:, cols])) / sig1
             y_val = y0[rows, cols]
             e_val = h_val * leaky_slope(y_val)
-            e0[rows, cols] = e_val.astype(BF16)
+            e_half = e_val.astype(BF16)
+            e0[:, cols] = e_half
+            store_transposed(e0_t, tile_no * TILE, rows, e_half)
             return corr + total(e_val * y_val)
 
         corr0 = lax.fori_loop(0, wide1 // TILE, h1_tile, corr0)
-        h0_put[rows, :] = dot_n(e0[rows, :], w0[...]).astype(BF16)
+        h0_put[rows, :] = dot_n(e0[...], w0[...]).astype(BF16)
         send(h0_put.at[rows, :], h0_got.at[rows, :], h0_send.at[chunk_no], h0_recv.at[chunk_no], far).start()
         return corr0
 
     corr0 = lax.fori_loop(0, CHUNKS, back0, zero)
-    e0_near = pltpu.make_async_copy(e0.at[:, part(core, rows1)], e0_out.at[batch, :], put_sem.at[6])
-    e0_mate = send(e0.at[:, part(1 - core, rows1)], e0_out.at[batch, :], out_send.at[6], out_recv.at[6], mate)
-    e0_near.start()
-    e0_mate.start()
+    e0_pair = halves(e0_t, e0_out, rows1, 6)
+    for copy in e0_pair:
+        copy.start()
     c_buf[me] = pack([corr0, corr1, corr2, loss])
     c_copies = spread(c_buf, 6)
     for copy in c_copies:
@@ -321,11 +338,11 @@
 
     for copy in gives:
         copy.wait_send()
-    send(t_real, tt.at[core], w_send.at[3], w_recv.at[3], mate).wait_send()
+    t_give.wait_send()
     for piece_no in range(PIECES):
         w1x_copy(piece_no).wait_send()
         w1x_forward(piece_no).wait_send()
-    for pair in (x1_near, x1_far, *lesser, (e0_near, e0_mate)):
+    for pair in (x1_near, x1_far, *lesser, e0_pair):
         for copy in pair:
             copy.wait()
 
@@ -356,8 +373,8 @@
     return pl.pallas_call(
         chain_kernel,
         out_shape=(
-            shape((2 * n_rows, n1), BF16), shape((2 * n_rows, n2), BF16), shape((2 * n_rows, wide2), BF16), shape((2 * n_rows, wide2), BF16),
-            shape((2 * n_rows, rows1), BF16), shape((2 * n_rows, n0), F32),
+            shape((2 * n_rows, n1), BF16), shape((2 * n_rows, n2), BF16), shape((rows2, 2 * n_rows), BF16), shape((rows2, 2 * n_rows), BF16),
+            shape((rows1, 2 * n_rows), BF16), shape((2 * n_rows, n0), F32),
             shape((1, n0), F32), shape((1, n1), F32), shape((1, n2), F32),
             shape((1, rows1), F32), shape((1, rows2), F32), shape((1, rows2), F32),
             shape((8, 128), F32), shape((8, 128), F32),
@@ -367,18 +384,106 @@
         scratch_shapes=[
             pltpu.VMEM((wide1, n0), BF16), pltpu.VMEM((wide2, n1), BF16), pltpu.VMEM((wide2, wide1), BF16), pltpu.VMEM((wide2, n2), BF16),
             pltpu.VMEM((n_rows, n0), BF16), pltpu.VMEM((2, n_rows, wide1), BF16), pltpu.VMEM((2, n_rows, wide2), BF16),
-            pltpu.VMEM((n_rows, wide1), F32), pltpu.VMEM((n_rows, wide2), F32), pltpu.VMEM((2, n_rows, rows2), BF16),
-            pltpu.VMEM((n_rows, wide2), BF16), pltpu.VMEM((n_rows, wide2), F32), pltpu.VMEM((n_rows, wide2), BF16), pltpu.VMEM((n_rows, wide2), BF16),
-            pltpu.VMEM((2, n_rows, wide2), BF16), pltpu.VMEM((n_rows, wide1), BF16),
+            pltpu.VMEM((n_rows, wide1), F32), pltpu.VMEM((n_rows, wide2), F32), pltpu.VMEM((wide2, n_rows), BF16),
+            pltpu.VMEM((wide2, n_rows), BF16), pltpu.VMEM((n_rows, wide2), F32), pltpu.VMEM((n_rows, wide2), BF16), pltpu.VMEM((n_rows, wide2), BF16),
+            pltpu.VMEM((2, n_rows, wide2), BF16), pltpu.VMEM((wide2, n_rows), BF16), pltpu.VMEM((n_rows // CHUNKS, wide1), BF16), pltpu.VMEM((wide1, n_rows), BF16),
             pltpu.VMEM((n_rows, n0), BF16), pltpu.VMEM((n_rows, n0), BF16), pltpu.VMEM((n_rows, n0), F32),
-            pltpu.VMEM((4, 1, n0 + n1 + n2), F32), pltpu.VMEM((4, 8, 128), F32), pltpu.VMEM((4, 8, 128), F32),
+            pltpu.VMEM((4, 1, n0 + n1 + n2), F32), pltpu.VMEM((4, 8, 128), F32), pltpu.VMEM((4, 8, 128), F32), pltpu.VMEM((128, 128), BF16),
             dma((5,)), dma((7,)), dma((4,)), dma((4,)), dma((PIECES,)), dma((PIECES,)), dma((PIECES,)), dma((PIECES,)), dma((9,)), dma((9,)),
             dma((CHUNKS,)), dma((CHUNKS,)), dma((CHUNKS,)), dma((CHUNKS,)), dma((CHUNKS,)), dma((CHUNKS,)),
             dma((CHUNKS,)), dma((CHUNKS,)), dma((CHUNKS,)), dma((CHUNKS,)), dma((7,)), dma((7,)), dma((CHUNKS,)), dma((CHUNKS,)), dma((CHUNKS,)),
         ],
         compiler_params=pltpu.CompilerParams(collective_id=0, has_side_effects=True, vmem_limit_bytes=60 * 1024 * 1024),
         name="chain",
-    )(x_real, x_fake, weight0, weight1, weight2, u_left0[None, :], u_left1[None, :], u_left2[None, :], t_real, t_fake)
+    )(x_real, x_fake, weight0, weight1, weight2, u_left0, u_left1, u_left2, t_real.T, t_fake.T)
+
+
+def grad_kernel(x1, e1, x2, e2, x_real, x_fake, e0, dx_a, dx_b, u0, u1, u2, v0, v1, v2, sig, cor,
+                dw0, dw1, dw2, dx_real, dx_fake, u0_out, u1_out, u2_out, v0_out, v1_out, v2_out, sig_out, loss_out, col0, col1, col2):
+    step = pl.program_id(0)
+    n_rows = x_real.shape[0]
+    dx_real[...] = dx_a[...]
+    dx_fake[...] = dx_b[...]
+
+    def scale(layer_no):
+        return 1.0 / (n_rows * sig[0:1, layer_no:layer_no + 1])
+
+    @pl.when(step == 0)
+    def _():
+        for src, dst in ((u0, u0_out), (u1, u1_out), (u2, u2_out), (v0, v0_out), (v1, v1_out), (v2, v2_out)):
+            dst[...] = src[...].reshape(dst.shape)
+        sig_out[...] = sig[...]
+        loss_out[...] = cor[0:1, 3:4] * (0.5 / n_rows)
+        for layer_no, (src, dst) in enumerate(((u0, col0), (u1, col1), (u2, col2))):
+            spread = jnp.broadcast_to(src[...] * cor[0:1, layer_no:layer_no + 1], (128, src.shape[1]))
+            dst[...] = spread.T
+
+    @pl.when(step < 8)
+    def _():
+        cols = pl.ds(pl.multiple_of(step * dw1.shape[1], 128), dw1.shape[1])
+        dw1[...] = (dot_n(e1[...], x1[...]) - col1[:, 0:1] * v1[:, cols]) * scale(1)
+
+    @pl.when((step >= 8) & (step < 10))
+    def _():
+        cols = pl.ds(pl.multiple_of((step - 8) * dw2.shape[1], 128), dw2.shape[1])
+        dw2[...] = (dot_n(e2[...], x2[...]) - col2[:, 0:1] * v2[:, cols]) * scale(2)
+
+    @pl.when((step >= 10) & (step < 15))
+    def _():
+        rows = pl.ds(pl.multiple_of((step - 10) * dw0.shape[0], 128), dw0.shape[0])
+        outer = dot_n(e0[:, 0:n_rows], x_real[...]) + dot_n(e0[:, n_rows:], x_fake[...])
+        dw0[...] = (outer - col0[rows, 0:1] * v0[...]) * scale(0)
+
+
+def run_grads(x1, e1, x2, e2, x_real, x_fake, e0, dx, u0, u1, u2, v0, v1, v2, sig, cor):
+    both, n1 = x1.shape
+    n_rows, n0 = x_real.shape
+    n2 = x2.shape[1]
+    rows2 = e1.shape[0]
+    rows1 = e0.shape[0]
+    steps = 16
+    dx_rows = n_rows // steps
+    shape = jax.ShapeDtypeStruct
+    vmem = pl.BlockSpec(memory_space=pltpu.VMEM)
+
+    def whole(array):
+        return pl.BlockSpec(array.shape, lambda step: (0, 0))
+
+    def at1(step):
+        return (0, jnp.minimum(step, 7))
+
+    def at2(step):
+        return (0, jnp.clip(step - 8, 0, 1))
+
+    def at0(step):
+        return (jnp.clip(step - 10, 0, 4), 0)
+
+    flops = 2 * both * (rows2 * (n1 + n2) + rows1 * n0)
+    return pl.pallas_call(
+        grad_kernel,
+        grid=(steps,),
+        out_shape=(
+            shape((rows1, n0), F32), shape((rows2, n1), F32), shape((rows2, n2), F32), shape((n_rows, n0), F32), shape((n_rows, n0), F32),
+            shape((rows1,), F32), shape((rows2,), F32), shape((rows2,), F32), shape((n0,), F32), shape((n1,), F32), shape((n2,), F32),
+            shape((8, 128), F32), shape((1, 1), F32),
+        ),
+        in_specs=[
+            pl.BlockSpec((both, n1 // 8), at1), whole(e1), pl.BlockSpec((both, n2 // 2), at2), whole(e2),
+            whole(x_real), whole(x_fake), pl.BlockSpec((rows1 // 5, both), at0),
+            pl.BlockSpec((dx_rows, n0), lambda step: (step, 0)), pl.BlockSpec((dx_rows, n0), lambda step: (step + steps, 0)),
+            whole(u0), whole(u1), whole(u2), whole(v0), whole(v1), whole(v2), whole(sig), whole(cor),
+        ],
+        out_specs=[
+            pl.BlockSpec((rows1 // 5, n0), at0), pl.BlockSpec((rows2, n1 // 8), at1), pl.BlockSpec((rows2, n2 // 2), at2),
+            pl.BlockSpec((dx_rows, n0), lambda step: (step, 0)), pl.BlockSpec((dx_rows, n0), lambda step: (step, 0)),
+            *[pl.BlockSpec((size,), lambda step: (0,)) for size in (rows1, rows2, rows2, n0, n1, n2)],
+            pl.BlockSpec((8, 128), lambda step: (0, 0)), pl.BlockSpec((1, 1), lambda step: (0, 0)),
+        ],
+        scratch_shapes=[pltpu.VMEM((rows1, 128), F32), pltpu.VMEM((rows2, 128), F32), pltpu.VMEM((rows2, 128), F32)],
+        compiler_params=pltpu.CompilerParams(dimension_semantics=("arbitrary",), vmem_limit_bytes=48 * 1024 * 1024),
+        cost_estimate=pl.CostEstimate(flops=flops, bytes_accessed=45 * 1024 * 1024, transcendentals=0),
+        name="grads",
+    )(x1, e1, x2, e2, x_real, x_fake, e0, dx, dx, u0, u1, u2, v0, v1, v2, sig, cor)
 
 
 def solution(mesh):
@@ -389,21 +494,8 @@
     group_spec = P("rep")
 
     def local_step(x_real, x_fake, weight0, weight1, weight2, u_left0, u_left1, u_left2, t_real, t_fake):
-        core = lax.axis_index("model") % 2
-        n_rows = x_real.shape[0]
-        rows2 = weight1.shape[0]
         x1, x2, e2, e1, e0, dx, v0, v1, v2, u0, u1, u2, sig, cor = run_chain(x_real, x_fake, weight0, weight1, weight2, u_left0, u_left1, u_left2, t_real, t_fake)
-        x0 = jnp.concatenate([x_real, x_fake], axis=0)
-        e2_own = lax.dynamic_slice(e2, (0, core * rows2), (2 * n_rows, rows2))
-        e1_own = lax.dynamic_slice(e1, (0, core * rows2), (2 * n_rows, rows2))
-
-        def gradient(up_half, layer_in, layer_no, u_new, v_new):
-            return (t_dot(up_half, layer_in) - cor[0, layer_no] * u_new[0][:, None] * v_new) / (n_rows * sig[0, layer_no])
-
-        dw0 = gradient(e0, x0, 0, u0, v0)
-        dw1 = gradient(e1_own, x1, 1, u1, v1)
-        dw2 = gradient(e2_own, x2, 2, u2, v2)
-        loss_val = cor[0, 3:4] * (0.5 / n_rows)
-        return (loss_val, dx[:n_rows], dx[n_rows:], dw0, dw1, dw2, u0[0], u1[0], u2[0], v0[0], v1[0], v2[0], sig[0, :3])
+        dw0, dw1, dw2, dx_real, dx_fake, u0, u1, u2, v0, v1, v2, sig, loss = run_grads(x1, e1, x2, e2, x_real, x_fake, e0, dx, u0, u1, u2, v0, v1, v2, sig, cor)
+        return (loss[0], dx_real, dx_fake, dw0, dw1, dw2, u0, u1, u2, v0, v1, v2, sig[0, :3])
 
     return jax.shard_map(local_step, mesh=mesh, in_specs=(rows_spec, rows_spec, weight_spec, weight_spec, weight_spec, left_spec, left_spec, left_spec, target_spec, target_spec), out_specs=(group_spec, rows_spec, rows_spec, weight_spec, weight_spec, weight_spec, left_spec, left_spec, left_spec, group_spec, group_spec, group_spec, group_spec), check_vma=False)

time: 218 us -> 205 us (0.940)
  matrix products: 24.1 us -> 0 us
  Pallas kernels: 172 us -> 195 us
  local copies, waits for them, and re-layouts: 13.6 us -> 8.18 us
  between operations: 4.6 us -> 0.71 us
  other arithmetic: 3.37 us -> 0 us
    dot_general x3 -> x0, matrix products: 24.1 us -> none  [t_dot(): lax.dot_general(left, right, (((0,), (0,)), ((), ())), preferred_element_...]
    pallas_call x0 -> x1, Pallas kernels: none -> 22.6 us  [run_grads(): pl.pallas_call(grad_kernel, grid=(steps,), out_shape=(shape((rows1, n0),...]
    slice x2 -> x0, local copies, waits for them, and re-layouts: 4.13 us -> none  [the longest x1 2.69 us: local_step(): dx[n_rows:]]
    broadcast_in_dim x3 -> x0, local copies, waits for them, and re-layouts: 3.78 us -> none  [the longest x1 1.29 us: run_chain(): u_left0[None, :]]
    unnamed x29 -> x24, local copies, waits for them, and re-layouts: 4.46 us -> 7.67 us
where the time goes in v2:
time: 205 us; the launch traced here: 204 us
  Pallas kernels  195 us (95%)
  local copies, waits for them, and re-layouts  8.18 us (4%)
    pallas_call x1, Pallas kernels, run_chain(): pl.pallas_call(chain_kernel, out_shape=(shape((2 * n_rows, n1), BF16), sh...  172 us
    pallas_call x1, Pallas kernels, run_grads(): pl.pallas_call(grad_kernel, grid=(steps,), out_shape=(shape((rows1, n0),...  22.6 us
    unnamed x24, local copies, waits for them, and re-layouts  7.67 us

profile of v2, /device:TPU:0, one launch (start us, length us, event | category | flops | bytes accessed | tf_op | source)
XLA Modules:
  0.0 203.7 jit_solution(1313652558733489493)
XLA Ops:
  0.6 0.0 copy-start
  0.7 0.0 copy-start.1
  0.7 172.2 %chain.1 = (bf16[1024,5120]{1,0:T(8,128)(2,1)}, bf16[1024,1280]{1,0:T(8,128)(2,1)}, bf16[320,1024]{1,0:T(8,128)(2,1)}, bf16[320,1024]{1,0:T(8,128)(2,1)}, bf16[1...) custom-call(bf16[512,1280]{1,0:T(8,128)(2,1)} %x_real.3, ...), custom_call_target="tpu_custom_call" | custom-call | tf_op jit(solution)/shard_map/chain/pallas_call | solution.py:373
  172.9 0.0 copy-done
  172.9 0.0 copy-done.1
  172.9 0.0 copy-start.2
  172.9 1.1 copy-done.2
  174.0 0.0 copy-start.3
  174.0 1.1 copy-done.3
  175.1 0.0 copy-start.4
  175.1 0.7 copy-done.4
  175.8 0.0 copy-start.5
  175.8 0.7 copy-done.5
  176.5 0.0 copy-start.6
  176.5 0.7 copy-done.6
  177.2 0.0 copy-start.7
  177.2 0.7 copy-done.7
  177.9 0.0 copy-start.8
  177.9 0.7 copy-done.8
  178.6 0.0 copy-start.9
  178.6 0.7 copy-done.9
  179.2 0.0 copy-start.10
  179.2 0.7 copy-done.10
  179.9 0.0 copy-start.11
  179.9 0.7 copy-done.11
  180.6 22.6 %grads.1 = (f32[1280,1280]{1,0:T(8,128)}, f32[320,5120]{1,0:T(8,128)}, f32[320,1280]{1,0:T(8,128)}, f32[512,1280]{1,0:T(8,128)}, f32[512,1280]{1,0:T(8,128)}, /*...) custom-call(bf16[1024,5120]{1,0:T(8,128)(2,1)} %get-tuple-element.40, ...), custom_call_target="tpu_custom_call" | custom-call | flops 7549747200 | bytes 47185920 | tf_op jit(solution)/shard_map/grads/pallas_call | solution.py:462
  203.2 0.5 slice_bitcast_fusion
Async XLA Ops:
  0.6 172.2 %copy-start = (bf16[512,1280]{1,0:T(8,128)(2,1)S(1)}, bf16[512,1280]{1,0:T(8,128)(2,1)}, u32[]{:S(2)}) copy-start(bf16[512,1280]{1,0:T(8,128)(2,1)} %x_real.3) | copy-start | bytes 3932164
  0.7 172.2 %copy-start.1 = (bf16[512,1280]{1,0:T(8,128)(2,1)S(1)}, bf16[512,1280]{1,0:T(8,128)(2,1)}, u32[]{:S(2)}) copy-start(bf16[512,1280]{1,0:T(8,128)(2,1)} %x_fake.3) | copy-start | bytes 3932164
  172.9 1.1 copy-start.2
  174.0 1.1 copy-start.3
  175.1 0.7 copy-start.4
  175.8 0.7 copy-start.5
  176.5 0.7 copy-start.6
  177.2 0.7 copy-start.7
  177.9 0.7 copy-start.8
  178.6 0.7 copy-start.9
  179.2 0.7 copy-start.10
  179.9 0.7 copy-start.11

commit v3 on v2

--- a/solution.py
+++ b/solution.py
@@ -393,46 +393,109 @@
             dma((CHUNKS,)), dma((CHUNKS,)), dma((CHUNKS,)), dma((CHUNKS,)), dma((CHUNKS,)), dma((CHUNKS,)),
             dma((CHUNKS,)), dma((CHUNKS,)), dma((CHUNKS,)), dma((CHUNKS,)), dma((7,)), dma((7,)), dma((CHUNKS,)), dma((CHUNKS,)), dma((CHUNKS,)),
         ],
-        compiler_params=pltpu.CompilerParams(collective_id=0, has_side_effects=True, vmem_limit_bytes=60 * 1024 * 1024),
+        compiler_params=pltpu.CompilerParams(collective_id=0, has_side_effects=True, vmem_limit_bytes=67043328),
         name="chain",
     )(x_real, x_fake, weight0, weight1, weight2, u_left0, u_left1, u_left2, t_real.T, t_fake.T)
 
 
-def grad_kernel(x1, e1, x2, e2, x_real, x_fake, e0, dx_a, dx_b, u0, u1, u2, v0, v1, v2, sig, cor,
-                dw0, dw1, dw2, dx_real, dx_fake, u0_out, u1_out, u2_out, v0_out, v1_out, v2_out, sig_out, loss_out, col0, col1, col2):
-    step = pl.program_id(0)
+def grad_kernel(x1_in, e1_in, x2_in, e2_in, x_real, x_fake, e0_in, dx_in, u0_in, u1_in, u2_in, v0_in, v1_in, v2_in, sig_in, cor_in,
+                dw0_out, dw1_out, dw2_out, dx_real, dx_fake, u0_out, u1_out, u2_out, v0_out, v1_out, v2_out, sig_out, loss_out,
+                x1, e1, x2, e2, x0, e0, dx, dw0, dw1, dw2, u0, u1, u2, v0, v1, v2, sig, cor, in_sem, x1_sem, out_sem, dw1_sem, dw0_sem):
     n_rows = x_real.shape[0]
-    dx_real[...] = dx_a[...]
-    dx_fake[...] = dx_b[...]
+    tiles1 = x1_sem.shape[0]
+    tiles0 = dw0_sem.shape[0]
+    wide1 = x1.shape[1] // tiles1
+    wide0 = x0.shape[1] // tiles0
+
+    def pull(src, dst, which):
+        copy = pltpu.make_async_copy(src, dst, in_sem.at[which])
+        copy.start()
+        return copy
+
+    small = [pull(src, dst, place) for place, (src, dst) in enumerate((
+        (u0_in, u0), (u1_in, u1), (u2_in, u2), (v0_in, v0), (v1_in, v1), (v2_in, v2), (sig_in, sig), (cor_in, cor)))]
+    got_e0 = pull(e0_in, e0, 8)
+    got_x0 = [pull(x_real, x0.at[pl.ds(0, n_rows), :], 9), pull(x_fake, x0.at[pl.ds(n_rows, n_rows), :], 10)]
+    got_e1 = pull(e1_in, e1, 11)
+
+    def x1_copy(tile_no):
+        cols = pl.ds(pl.multiple_of(tile_no * wide1, 128), wide1)
+        return pltpu.make_async_copy(x1_in.at[:, cols], x1.at[:, cols], x1_sem.at[tile_no])
+
+    for tile_no in range(tiles1):
+        x1_copy(tile_no).start()
+    got_dx = pull(dx_in, dx, 12)
+    got_2 = [pull(e2_in, e2, 13), pull(x2_in, x2, 14)]
+
+    for copy in small:
+        copy.wait()
+    for src, dst in ((u0, u0_out), (u1, u1_out), (u2, u2_out), (v0, v0_out), (v1, v1_out), (v2, v2_out)):
+        dst[...] = src[...].reshape(dst.shape)
+    sig_out[...] = sig[...]
+    loss_out[...] = cor[0:1, 3:4] * (0.5 / n_rows)
+
+    def column(u_new, layer_no):
+        return jnp.broadcast_to(u_new[...] * cor[0:1, layer_no:layer_no + 1], (128, u_new.shape[1])).T[:, 0:1]
 
     def scale(layer_no):
         return 1.0 / (n_rows * sig[0:1, layer_no:layer_no + 1])
 
-    @pl.when(step == 0)
-    def _():
-        for src, dst in ((u0, u0_out), (u1, u1_out), (u2, u2_out), (v0, v0_out), (v1, v1_out), (v2, v2_out)):
-            dst[...] = src[...].reshape(dst.shape)
-        sig_out[...] = sig[...]
-        loss_out[...] = cor[0:1, 3:4] * (0.5 / n_rows)
-        for layer_no, (src, dst) in enumerate(((u0, col0), (u1, col1), (u2, col2))):
-            spread = jnp.broadcast_to(src[...] * cor[0:1, layer_no:layer_no + 1], (128, src.shape[1]))
-            dst[...] = spread.T
-
-    @pl.when(step < 8)
-    def _():
-        cols = pl.ds(pl.multiple_of(step * dw1.shape[1], 128), dw1.shape[1])
-        dw1[...] = (dot_n(e1[...], x1[...]) - col1[:, 0:1] * v1[:, cols]) * scale(1)
-
-    @pl.when((step >= 8) & (step < 10))
-    def _():
-        cols = pl.ds(pl.multiple_of((step - 8) * dw2.shape[1], 128), dw2.shape[1])
-        dw2[...] = (dot_n(e2[...], x2[...]) - col2[:, 0:1] * v2[:, cols]) * scale(2)
-
-    @pl.when((step >= 10) & (step < 15))
-    def _():
-        rows = pl.ds(pl.multiple_of((step - 10) * dw0.shape[0], 128), dw0.shape[0])
-        outer = dot_n(e0[:, 0:n_rows], x_real[...]) + dot_n(e0[:, n_rows:], x_fake[...])
-        dw0[...] = (outer - col0[rows, 0:1] * v0[...]) * scale(0)
+    got_e0.wait()
+    for copy in got_x0:
+        copy.wait()
+    col0, scale0 = column(u0, 0), scale(0)
+
+    def dw0_copy(tile_no):
+        cols = pl.ds(pl.multiple_of(tile_no * wide0, 128), wide0)
+        return pltpu.make_async_copy(dw0.at[:, cols], dw0_out.at[:, cols], dw0_sem.at[tile_no])
+
+    def dw0_tile(tile_no, carry):
+        cols = pl.ds(pl.multiple_of(tile_no * wide0, 128), wide0)
+        dw0[:, cols] = (dot_n(e0[...], x0[:, cols]) - col0 * v0[:, cols]) * scale0
+        dw0_copy(tile_no).start()
+        return carry
+
+    lax.fori_loop(0, tiles0, dw0_tile, 0)
+    got_e1.wait()
+    col1, scale1 = column(u1, 1), scale(1)
+
+    def dw1_copy(tile_no):
+        cols = pl.ds(pl.multiple_of(tile_no * wide1, 128), wide1)
+        return pltpu.make_async_copy(dw1.at[:, cols], dw1_out.at[:, cols], dw1_sem.at[tile_no])
+
+    def dw1_tile(tile_no, carry):
+        cols = pl.ds(pl.multiple_of(tile_no * wide1, 128), wide1)
+        x1_copy(tile_no).wait()
+        dw1[:, cols] = (dot_n(e1[...], x1[:, cols]) - col1 * v1[:, cols]) * scale1
+        dw1_copy(tile_no).start()
+        return carry
+
+    lax.fori_loop(0, tiles1, dw1_tile, 0)
+    got_dx.wait()
+    pushes = [
+        pltpu.make_async_copy(dx.at[pl.ds(0, n_rows), :], dx_real, out_sem.at[0]),
+        pltpu.make_async_copy(dx.at[pl.ds(n_rows, n_rows), :], dx_fake, out_sem.at[1]),
+    ]
+    for copy in pushes:
+        copy.start()
+    for copy in got_2:
+        copy.wait()
+    dw2[...] = (dot_n(e2[...], x2[...]) - column(u2, 2) * v2[...]) * scale(2)
+    last = pltpu.make_async_copy(dw2, dw2_out, out_sem.at[2])
+    last.start()
+
+    def drain0(tile_no, carry):
+        dw0_copy(tile_no).wait()
+        return carry
+
+    def drain1(tile_no, carry):
+        dw1_copy(tile_no).wait()
+        return carry
+
+    lax.fori_loop(0, tiles0, drain0, 0)
+    lax.fori_loop(0, tiles1, drain1, 0)
+    for copy in (*pushes, last):
+        copy.wait()
 
 
 def run_grads(x1, e1, x2, e2, x_real, x_fake, e0, dx, u0, u1, u2, v0, v1, v2, sig, cor):
@@ -441,49 +504,33 @@
     n2 = x2.shape[1]
     rows2 = e1.shape[0]
     rows1 = e0.shape[0]
-    steps = 16
-    dx_rows = n_rows // steps
+    tiles1, tiles0 = 8, 5
     shape = jax.ShapeDtypeStruct
+    hbm = pl.BlockSpec(memory_space=pl.ANY)
     vmem = pl.BlockSpec(memory_space=pltpu.VMEM)
-
-    def whole(array):
-        return pl.BlockSpec(array.shape, lambda step: (0, 0))
-
-    def at1(step):
-        return (0, jnp.minimum(step, 7))
-
-    def at2(step):
-        return (0, jnp.clip(step - 8, 0, 1))
-
-    def at0(step):
-        return (jnp.clip(step - 10, 0, 4), 0)
-
+    dma = pltpu.SemaphoreType.DMA
     flops = 2 * both * (rows2 * (n1 + n2) + rows1 * n0)
+    inputs = (x1, e1, x2, e2, x_real, x_fake, e0, dx, u0, u1, u2, v0, v1, v2, sig, cor)
     return pl.pallas_call(
         grad_kernel,
-        grid=(steps,),
         out_shape=(
             shape((rows1, n0), F32), shape((rows2, n1), F32), shape((rows2, n2), F32), shape((n_rows, n0), F32), shape((n_rows, n0), F32),
             shape((rows1,), F32), shape((rows2,), F32), shape((rows2,), F32), shape((n0,), F32), shape((n1,), F32), shape((n2,), F32),
             shape((8, 128), F32), shape((1, 1), F32),
         ),
-        in_specs=[
-            pl.BlockSpec((both, n1 // 8), at1), whole(e1), pl.BlockSpec((both, n2 // 2), at2), whole(e2),
-            whole(x_real), whole(x_fake), pl.BlockSpec((rows1 // 5, both), at0),
-            pl.BlockSpec((dx_rows, n0), lambda step: (step, 0)), pl.BlockSpec((dx_rows, n0), lambda step: (step + steps, 0)),
-            whole(u0), whole(u1), whole(u2), whole(v0), whole(v1), whole(v2), whole(sig), whole(cor),
+        in_specs=[hbm] * len(inputs),
+        out_specs=[hbm] * 5 + [vmem] * 8,
+        scratch_shapes=[
+            pltpu.VMEM((both, n1), BF16), pltpu.VMEM((rows2, both), BF16), pltpu.VMEM((both, n2), BF16), pltpu.VMEM((rows2, both), BF16),
+            pltpu.VMEM((both, n0), BF16), pltpu.VMEM((rows1, both), BF16), pltpu.VMEM((both, n0), F32),
+            pltpu.VMEM((rows1, n0), F32), pltpu.VMEM((rows2, n1), F32), pltpu.VMEM((rows2, n2), F32),
+            *[pltpu.VMEM(array.shape, F32) for array in (u0, u1, u2, v0, v1, v2, sig, cor)],
+            dma((15,)), dma((tiles1,)), dma((3,)), dma((tiles1,)), dma((tiles0,)),
         ],
-        out_specs=[
-            pl.BlockSpec((rows1 // 5, n0), at0), pl.BlockSpec((rows2, n1 // 8), at1), pl.BlockSpec((rows2, n2 // 2), at2),
-            pl.BlockSpec((dx_rows, n0), lambda step: (step, 0)), pl.BlockSpec((dx_rows, n0), lambda step: (step, 0)),
-            *[pl.BlockSpec((size,), lambda step: (0,)) for size in (rows1, rows2, rows2, n0, n1, n2)],
-            pl.BlockSpec((8, 128), lambda step: (0, 0)), pl.BlockSpec((1, 1), lambda step: (0, 0)),
-        ],
-        scratch_shapes=[pltpu.VMEM((rows1, 128), F32), pltpu.VMEM((rows2, 128), F32), pltpu.VMEM((rows2, 128), F32)],
-        compiler_params=pltpu.CompilerParams(dimension_semantics=("arbitrary",), vmem_limit_bytes=48 * 1024 * 1024),
+        compiler_params=pltpu.CompilerParams(vmem_limit_bytes=67043328),
         cost_estimate=pl.CostEstimate(flops=flops, bytes_accessed=45 * 1024 * 1024, transcendentals=0),
         name="grads",
-    )(x1, e1, x2, e2, x_real, x_fake, e0, dx, dx, u0, u1, u2, v0, v1, v2, sig, cor)
+    )(*inputs)
 
 
 def solution(mesh):

time: 205 us -> 193 us (0.941)
  local copies, waits for them, and re-layouts: 8.18 us -> 1.19 us
  Pallas kernels: 195 us -> 191 us
    unnamed x24 -> x0, local copies, waits for them, and re-layouts: 7.67 us -> none
    pallas_call x1, Pallas kernels: 22.6 us -> 18.5 us  [run_grads(): pl.pallas_call(grad_kernel, out_shape=(shape((rows1, n0), F32), shape((ro...]
where the time goes in v3:
time: 193 us; the launch traced here: 192 us
  Pallas kernels  191 us (99%)
    pallas_call x1, Pallas kernels, run_chain(): pl.pallas_call(chain_kernel, out_shape=(shape((2 * n_rows, n1), BF16), sh...  172 us
    pallas_call x1, Pallas kernels, run_grads(): pl.pallas_call(grad_kernel, out_shape=(shape((rows1, n0), F32), shape((ro...  18.5 us

profile of v3, /device:TPU:0, one launch (start us, length us, event | category | flops | bytes accessed | tf_op | source)
XLA Modules:
  0.0 192.4 jit_solution(2887519086515861977)
XLA Ops:
  0.6 172.0 %chain.1 = (bf16[1024,5120]{1,0:T(8,128)(2,1)}, bf16[1024,1280]{1,0:T(8,128)(2,1)}, bf16[320,1024]{1,0:T(8,128)(2,1)}, bf16[320,1024]{1,0:T(8,128)(2,1)}, bf16[1...) custom-call(bf16[512,1280]{1,0:T(8,128)(2,1)} %x_real.3, ...), custom_call_target="tpu_custom_call" | custom-call | tf_op jit(solution)/shard_map/chain/pallas_call | solution.py:373
  172.7 18.5 %grads.1 = (f32[1280,1280]{1,0:T(8,128)}, f32[320,5120]{1,0:T(8,128)}, f32[320,1280]{1,0:T(8,128)}, f32[512,1280]{1,0:T(8,128)}, f32[512,1280]{1,0:T(8,128)}, /*...) custom-call(bf16[1024,5120]{1,0:T(8,128)(2,1)} %get-tuple-element.40, ...), custom_call_target="tpu_custom_call" | custom-call | flops 7549747200 | bytes 47185920 | tf_op jit(solution)/shard_map/grads/pallas_call | solution.py:514
  191.2 1.2 slice_bitcast_fusion

commit v4 on v3

--- a/solution.py
+++ b/solution.py
@@ -9,6 +9,7 @@
 EPSILON = 1e-12
 MESH = pl.DeviceIdType.MESH
 CHUNKS = 4
+EARLY = 1
 PIECES = 4
 TILE = 256
 BF16 = jnp.bfloat16
@@ -40,11 +41,11 @@
 
 
 def chain_kernel(x_real, x_fake, w0_in, w1_in, w2_in, u0_in, u1_in, u2_in, t_real, t_fake,
-                 x1_out, x2_out, e2_out, e1_out, e0_out, dx_out, v0_out, v1_out, v2_out, u0_out, u1_out, u2_out, sig_out, cor_out,
+                 x1_out, x2_out, e2_out, e1_out, e0_out, dx_out, sum_out, both_out, v0_out, v1_out, v2_out, u0_out, u1_out, u2_out, sig_out, cor_out,
                  w0, w1, w1x, w2, x0, x1, x2, y0, y1, tt, e2_t, h2_own, h2_put, h2_got, e1, e1_t, e0, e0_t, h0_put, h0_got, dx,
                  p_buf, n_buf, c_buf,
                  eye, load_sem, put_sem, w_send, w_recv, w1x_send, w1x_recv, fwd_send, fwd_recv, small_send, small_recv,
-                 x1_send, x1_recv, x2_send, x2_recv, h2_send, h2_recv, e1_send, e1_recv, h0_send, h0_recv, out_send, out_recv, dx_sem, dx_send, dx_recv):
+                 x1_send, x1_recv, x2_send, x2_recv, h2_send, h2_recv, e1_send, e1_recv, h0_send, h0_recv, out_send, out_recv, dx_sem, dx_send, dx_recv, sum_sem, both_sem, both_send, both_recv):
     me = lax.axis_index("model")
     chip = me // 2
     core = me % 2
@@ -286,6 +287,22 @@
     for piece_no in range(PIECES):
         w1x_forward(piece_no).wait_recv()
 
+    late = n_rows - EARLY * step
+
+    def h0_copy(chunk_no):
+        rows = part(chunk_no, step)
+        return send(h0_put.at[rows, :], h0_got.at[rows, :], h0_send.at[chunk_no], h0_recv.at[chunk_no], far)
+
+    def late_copies(chunk_no):
+        src = h0_put.at[part(chunk_no, step), :]
+        place = chunk_no - EARLY
+        dst = both_out.at[pl.ds(pl.multiple_of(core * late + place * step, step), step), :]
+        return (
+            pltpu.make_async_copy(src, sum_out.at[part(place, step), :], sum_sem.at[place]),
+            pltpu.make_async_copy(src, dst, both_sem.at[place]),
+            send(src, dst, both_send.at[place], both_recv.at[place], mate),
+        )
+
     def back0(chunk_no, corr0):
         rows = part(chunk_no, step)
         chunk_copy(e1, other, chunk_no, e1_send, e1_recv).wait_recv()
@@ -303,10 +320,21 @@
 
         corr0 = lax.fori_loop(0, wide1 // TILE, h1_tile, corr0)
         h0_put[rows, :] = dot_n(e0[...], w0[...]).astype(BF16)
-        send(h0_put.at[rows, :], h0_got.at[rows, :], h0_send.at[chunk_no], h0_recv.at[chunk_no], far).start()
         return corr0
 
-    corr0 = lax.fori_loop(0, CHUNKS, back0, zero)
+    def back0_early(chunk_no, corr0):
+        corr0 = back0(chunk_no, corr0)
+        h0_copy(chunk_no).start()
+        return corr0
+
+    def back0_late(chunk_no, corr0):
+        corr0 = back0(chunk_no, corr0)
+        for copy in late_copies(chunk_no):
+            copy.start()
+        return corr0
+
+    corr0 = lax.fori_loop(0, EARLY, back0_early, zero)
+    corr0 = lax.fori_loop(EARLY, CHUNKS, back0_late, corr0)
     e0_pair = halves(e0_t, e0_out, rows1, 6)
     for copy in e0_pair:
         copy.start()
@@ -317,7 +345,7 @@
 
     def dx_copies(chunk_no):
         rows = part(chunk_no, step)
-        dst = dx_out.at[pl.ds(pl.multiple_of(core * n_rows + chunk_no * step, step), step), :]
+        dst = dx_out.at[pl.ds(pl.multiple_of((core * EARLY + chunk_no) * step, step), step), :]
         return (
             pltpu.make_async_copy(dx.at[rows, :], dst, dx_sem.at[chunk_no]),
             send(dx.at[rows, :], dst, dx_send.at[chunk_no], dx_recv.at[chunk_no], mate),
@@ -325,13 +353,13 @@
 
     def finish(chunk_no, carry):
         rows = part(chunk_no, step)
-        send(h0_put.at[rows, :], h0_got.at[rows, :], h0_send.at[chunk_no], h0_recv.at[chunk_no], far).wait_recv()
+        h0_copy(chunk_no).wait_recv()
         dx[rows, :] = (h0_put[rows, :].astype(F32) + h0_got[rows, :].astype(F32)) / sig0
         for copy in dx_copies(chunk_no):
             copy.start()
         return carry
 
-    lax.fori_loop(0, CHUNKS, finish, 0)
+    lax.fori_loop(0, EARLY, finish, 0)
     for copy in c_copies:
         copy.wait()
     cor_out[...] = c_buf[0] + c_buf[1] + c_buf[2] + c_buf[3]
@@ -352,12 +380,24 @@
         chunk_copy(x2, chip, chunk_no, x2_send, x2_recv).wait_send()
         send(h2_put.at[rows, :], h2_got.at[rows, :], h2_send.at[chunk_no], h2_recv.at[chunk_no], far).wait_send()
         chunk_copy(e1, chip, chunk_no, e1_send, e1_recv).wait_send()
-        send(h0_put.at[rows, :], h0_got.at[rows, :], h0_send.at[chunk_no], h0_recv.at[chunk_no], far).wait_send()
+        return carry
+
+    lax.fori_loop(0, CHUNKS, drain, 0)
+
+    def drain_early(chunk_no, carry):
+        h0_copy(chunk_no).wait_send()
         for copy in dx_copies(chunk_no):
             copy.wait()
         return carry
 
-    lax.fori_loop(0, CHUNKS, drain, 0)
+    lax.fori_loop(0, EARLY, drain_early, 0)
+
+    def drain_late(chunk_no, carry):
+        for copy in late_copies(chunk_no):
+            copy.wait()
+        return carry
+
+    lax.fori_loop(EARLY, CHUNKS, drain_late, 0)
 
 
 def run_chain(x_real, x_fake, weight0, weight1, weight2, u_left0, u_left1, u_left2, t_real, t_fake):
@@ -366,6 +406,8 @@
     rows2, n1 = weight1.shape
     wide1, wide2 = 2 * rows1, 2 * rows2
     n2 = 2 * wide2
+    early = n_rows // CHUNKS * EARLY
+    late = n_rows - early
     hbm = pl.BlockSpec(memory_space=pl.ANY)
     vmem = pl.BlockSpec(memory_space=pltpu.VMEM)
     shape = jax.ShapeDtypeStruct
@@ -374,24 +416,25 @@
         chain_kernel,
         out_shape=(
             shape((2 * n_rows, n1), BF16), shape((2 * n_rows, n2), BF16), shape((rows2, 2 * n_rows), BF16), shape((rows2, 2 * n_rows), BF16),
-            shape((rows1, 2 * n_rows), BF16), shape((2 * n_rows, n0), F32),
+            shape((rows1, 2 * n_rows), BF16), shape((2 * early, n0), F32), shape((late, n0), BF16), shape((2 * late, n0), BF16),
             shape((1, n0), F32), shape((1, n1), F32), shape((1, n2), F32),
             shape((1, rows1), F32), shape((1, rows2), F32), shape((1, rows2), F32),
             shape((8, 128), F32), shape((8, 128), F32),
         ),
         in_specs=[hbm] * 5 + [vmem] * 3 + [hbm] * 2,
-        out_specs=[hbm] * 6 + [vmem] * 8,
+        out_specs=[hbm] * 8 + [vmem] * 8,
         scratch_shapes=[
             pltpu.VMEM((wide1, n0), BF16), pltpu.VMEM((wide2, n1), BF16), pltpu.VMEM((wide2, wide1), BF16), pltpu.VMEM((wide2, n2), BF16),
             pltpu.VMEM((n_rows, n0), BF16), pltpu.VMEM((2, n_rows, wide1), BF16), pltpu.VMEM((2, n_rows, wide2), BF16),
             pltpu.VMEM((n_rows, wide1), F32), pltpu.VMEM((n_rows, wide2), F32), pltpu.VMEM((wide2, n_rows), BF16),
             pltpu.VMEM((wide2, n_rows), BF16), pltpu.VMEM((n_rows, wide2), F32), pltpu.VMEM((n_rows, wide2), BF16), pltpu.VMEM((n_rows, wide2), BF16),
             pltpu.VMEM((2, n_rows, wide2), BF16), pltpu.VMEM((wide2, n_rows), BF16), pltpu.VMEM((n_rows // CHUNKS, wide1), BF16), pltpu.VMEM((wide1, n_rows), BF16),
-            pltpu.VMEM((n_rows, n0), BF16), pltpu.VMEM((n_rows, n0), BF16), pltpu.VMEM((n_rows, n0), F32),
+            pltpu.VMEM((n_rows, n0), BF16), pltpu.VMEM((early, n0), BF16), pltpu.VMEM((early, n0), F32),
             pltpu.VMEM((4, 1, n0 + n1 + n2), F32), pltpu.VMEM((4, 8, 128), F32), pltpu.VMEM((4, 8, 128), F32), pltpu.VMEM((128, 128), BF16),
             dma((5,)), dma((7,)), dma((4,)), dma((4,)), dma((PIECES,)), dma((PIECES,)), dma((PIECES,)), dma((PIECES,)), dma((9,)), dma((9,)),
             dma((CHUNKS,)), dma((CHUNKS,)), dma((CHUNKS,)), dma((CHUNKS,)), dma((CHUNKS,)), dma((CHUNKS,)),
-            dma((CHUNKS,)), dma((CHUNKS,)), dma((CHUNKS,)), dma((CHUNKS,)), dma((7,)), dma((7,)), dma((CHUNKS,)), dma((CHUNKS,)), dma((CHUNKS,)),
+            dma((CHUNKS,)), dma((CHUNKS,)), dma((EARLY,)), dma((EARLY,)), dma((7,)), dma((7,)), dma((EARLY,)), dma((EARLY,)), dma((EARLY,)),
+            dma((CHUNKS - EARLY,)), dma((CHUNKS - EARLY,)), dma((CHUNKS - EARLY,)), dma((CHUNKS - EARLY,)),
         ],
         compiler_params=pltpu.CompilerParams(collective_id=0, has_side_effects=True, vmem_limit_bytes=67043328),
         name="chain",
@@ -402,6 +445,7 @@
                 dw0_out, dw1_out, dw2_out, dx_real, dx_fake, u0_out, u1_out, u2_out, v0_out, v1_out, v2_out, sig_out, loss_out,
                 x1, e1, x2, e2, x0, e0, dx, dw0, dw1, dw2, u0, u1, u2, v0, v1, v2, sig, cor, in_sem, x1_sem, out_sem, dw1_sem, dw0_sem):
     n_rows = x_real.shape[0]
+    early = dx.shape[0] // 2
     tiles1 = x1_sem.shape[0]
     tiles0 = dw0_sem.shape[0]
     wide1 = x1.shape[1] // tiles1
@@ -431,7 +475,7 @@
         copy.wait()
     for src, dst in ((u0, u0_out), (u1, u1_out), (u2, u2_out), (v0, v0_out), (v1, v1_out), (v2, v2_out)):
         dst[...] = src[...].reshape(dst.shape)
-    sig_out[...] = sig[...]
+    sig_out[...] = sig[0:1, 0:3].reshape(3)
     loss_out[...] = cor[0:1, 3:4] * (0.5 / n_rows)
 
     def column(u_new, layer_no):
@@ -473,8 +517,8 @@
     lax.fori_loop(0, tiles1, dw1_tile, 0)
     got_dx.wait()
     pushes = [
-        pltpu.make_async_copy(dx.at[pl.ds(0, n_rows), :], dx_real, out_sem.at[0]),
-        pltpu.make_async_copy(dx.at[pl.ds(n_rows, n_rows), :], dx_fake, out_sem.at[1]),
+        pltpu.make_async_copy(dx.at[pl.ds(0, early), :], dx_real.at[pl.ds(0, early), :], out_sem.at[0]),
+        pltpu.make_async_copy(dx.at[pl.ds(early, early), :], dx_fake.at[pl.ds(0, early), :], out_sem.at[1]),
     ]
     for copy in pushes:
         copy.start()
@@ -516,13 +560,13 @@
         out_shape=(
             shape((rows1, n0), F32), shape((rows2, n1), F32), shape((rows2, n2), F32), shape((n_rows, n0), F32), shape((n_rows, n0), F32),
             shape((rows1,), F32), shape((rows2,), F32), shape((rows2,), F32), shape((n0,), F32), shape((n1,), F32), shape((n2,), F32),
-            shape((8, 128), F32), shape((1, 1), F32),
+            shape((3,), F32), shape((1, 1), F32),
         ),
         in_specs=[hbm] * len(inputs),
         out_specs=[hbm] * 5 + [vmem] * 8,
         scratch_shapes=[
             pltpu.VMEM((both, n1), BF16), pltpu.VMEM((rows2, both), BF16), pltpu.VMEM((both, n2), BF16), pltpu.VMEM((rows2, both), BF16),
-            pltpu.VMEM((both, n0), BF16), pltpu.VMEM((rows1, both), BF16), pltpu.VMEM((both, n0), F32),
+            pltpu.VMEM((both, n0), BF16), pltpu.VMEM((rows1, both), BF16), pltpu.VMEM(dx.shape, F32),
             pltpu.VMEM((rows1, n0), F32), pltpu.VMEM((rows2, n1), F32), pltpu.VMEM((rows2, n2), F32),
             *[pltpu.VMEM(array.shape, F32) for array in (u0, u1, u2, v0, v1, v2, sig, cor)],
             dma((15,)), dma((tiles1,)), dma((3,)), dma((tiles1,)), dma((tiles0,)),
@@ -533,6 +577,10 @@
     )(*inputs)
 
 
+def swap(values, bits):
+    return lax.ppermute(values, "model", [(dev, dev ^ bits) for dev in range(4)])
+
+
 def solution(mesh):
     rows_spec = P("rep", None)
     weight_spec = P(("rep", "model"), None)
@@ -541,8 +589,21 @@
     group_spec = P("rep")
 
     def local_step(x_real, x_fake, weight0, weight1, weight2, u_left0, u_left1, u_left2, t_real, t_fake):
-        x1, x2, e2, e1, e0, dx, v0, v1, v2, u0, u1, u2, sig, cor = run_chain(x_real, x_fake, weight0, weight1, weight2, u_left0, u_left1, u_left2, t_real, t_fake)
-        dw0, dw1, dw2, dx_real, dx_fake, u0, u1, u2, v0, v1, v2, sig, loss = run_grads(x1, e1, x2, e2, x_real, x_fake, e0, dx, u0, u1, u2, v0, v1, v2, sig, cor)
-        return (loss[0], dx_real, dx_fake, dw0, dw1, dw2, u0, u1, u2, v0, v1, v2, sig[0, :3])
+        core = lax.axis_index("model") % 2
+        x1, x2, e2, e1, e0, dx, sums, both, v0, v1, v2, u0, u1, u2, sig, cor = run_chain(x_real, x_fake, weight0, weight1, weight2, u_left0, u_left1, u_left2, t_real, t_fake)
+        came = swap(sums, 2)
+        dw0, dw1, dw2, dx_real, dx_fake, u0, u1, u2, v0, v1, v2, sigmas, loss = run_grads(x1, e1, x2, e2, x_real, x_fake, e0, dx, u0, u1, u2, v0, v1, v2, sig, cor)
+        came, sigmas = lax.optimization_barrier((came, sigmas))
+        came_mate = swap(came, 1)
+        late = sums.shape[0]
+        first = x_real.shape[0] - late
+
+        def finish(dx_batch, batch_no):
+            got = jnp.where(core == batch_no, came, came_mate)
+            own = both[batch_no * late:(batch_no + 1) * late]
+            dx_late = (own.astype(F32) + got.astype(F32)) / sigmas[0]
+            return lax.dynamic_update_slice(dx_batch, dx_late, (first, 0))
+
+        return (loss[0], finish(dx_real, 0), finish(dx_fake, 1), dw0, dw1, dw2, u0, u1, u2, v0, v1, v2, sigmas)
 
     return jax.shard_map(local_step, mesh=mesh, in_specs=(rows_spec, rows_spec, weight_spec, weight_spec, weight_spec, left_spec, left_spec, left_spec, target_spec, target_spec), out_specs=(group_spec, rows_spec, rows_spec, weight_spec, weight_spec, weight_spec, left_spec, left_spec, left_spec, group_spec, group_spec, group_spec, group_spec), check_vma=False)

time: 193 us -> 191 us (0.990)
  Pallas kernels: 191 us -> 176 us
  waiting for transfers between devices: 0 us -> 7.02 us
  other arithmetic: 0 us -> 4.99 us
  starting transfers between devices: 0 us -> 2.04 us
    pallas_call x1, Pallas kernels: 172 us -> 158 us  [run_chain(): pl.pallas_call(chain_kernel, out_shape=(shape((2 * n_rows, n1), BF16), sh...]
    ppermute x0 -> x2, waiting for transfers between devices: none -> 7.02 us  [swap(): lax.ppermute(values, 'model', [(dev, dev ^ bits) for dev in range(4)])]
    dynamic_update_slice x0 -> x1, other arithmetic: none -> 4.99 us  [finish(): return lax.dynamic_update_slice(dx_batch, dx_late, (first, 0))]
    ppermute x0 -> x2, starting transfers between devices: none -> 2.04 us  [swap(): lax.ppermute(values, 'model', [(dev, dev ^ bits) for dev in range(4)])]
  transfers between devices with their start and end apart: 0 -> 2, of which waited for: 0 -> 2; matrix products, arithmetic and copies ran while one was open for 0% -> 0% of each run, Pallas kernels for 0% -> 9%
where the time goes in v4:
time: 191 us
  Pallas kernels  176 us (92%)
  waiting for transfers between devices  7.02 us (4%)
  other arithmetic  4.99 us (3%)
  starting transfers between devices  2.04 us (1%)
    pallas_call x1, Pallas kernels, run_chain(): pl.pallas_call(chain_kernel, out_shape=(shape((2 * n_rows, n1), BF16), sh...  158 us
    pallas_call x1, Pallas kernels, run_grads(): pl.pallas_call(grad_kernel, out_shape=(shape((rows1, n0), F32), shape((ro...  17.8 us
    ppermute x2, waiting for transfers between devices, swap(): lax.ppermute(values, 'model', [(dev, dev ^ bits) for dev in range(4)])  7.02 us
    dynamic_update_slice x1, other arithmetic, finish(): return lax.dynamic_update_slice(dx_batch, dx_late, (first, 0))  4.99 us
  transfers between devices with their start and end apart: 2, of which 2 were waited for; matrix products, arithmetic and copies ran while one was open for 0% of the time, Pallas kernels for 9%

profile of v4, /device:TPU:0, one launch (start us, length us, event | category | flops | bytes accessed | tf_op | source)
XLA Modules:
  0.0 190.6 jit_solution(6654787409236533571)
XLA Ops:
  0.6 158.1 %chain.1 = (bf16[1024,5120]{1,0:T(8,128)(2,1)}, bf16[1024,1280]{1,0:T(8,128)(2,1)}, bf16[320,1024]{1,0:T(8,128)(2,1)}, bf16[320,1024]{1,0:T(8,128)(2,1)}, bf16[1...) custom-call(bf16[512,1280]{1,0:T(8,128)(2,1)} %x_real.3, ...), custom_call_target="tpu_custom_call" | custom-call | tf_op jit(solution)/shard_map/chain/pallas_call | solution.py:415
  158.7 2.0 %collective-permute-start = (bf16[384,1280]{1,0:T(8,128)(2,1)}, bf16[384,1280]{1,0:T(8,128)(2,1)}, u32[]{:S(2)}, u32[]{:S(2)}) collective-permute-start(bf16[384,1280]{1,0:T(8,128)(2,1)} %get-tuple-element.61), channel_id=1, source_target_pairs={{0,2},{1,3},{2,0},{3,1},{4,6},{5,7},{6,4},{7,5}} | collective-permute-start | bytes 2949128 | tf_op jit(solution)/shard_map/ppermute | solution.py:581
  160.8 17.8 %grads.1 = (f32[1280,1280]{1,0:T(8,128)}, f32[320,5120]{1,0:T(8,128)}, f32[320,1280]{1,0:T(8,128)}, f32[512,1280]{1,0:T(8,128)}, f32[512,1280]{1,0:T(8,128)}, /*...) custom-call(bf16[1024,5120]{1,0:T(8,128)(2,1)} %get-tuple-element.44, ...), custom_call_target="tpu_custom_call" | custom-call | flops 7549747200 | bytes 47185920 | tf_op jit(solution)/shard_map/grads/pallas_call | solution.py:558
  178.6 4.5 %collective-permute-done = bf16[384,1280]{1,0:T(8,128)(2,1)} collective-permute-done((bf16[384,1280]{1,0:T(8,128)(2,1)}, bf16[384,1280]{1,0:T(8,128)(2,1)}, u32[]{:S(2)}, u32[]{:S(2)}) %collective-permute-start) | collective-permute-done | bytes 983072 | tf_op jit(solution)/shard_map/ppermute | solution.py:581
  183.0 0.0 collective-permute-start.1
  183.0 2.6 %collective-permute-done.1 = bf16[384,1280]{1,0:T(8,128)(2,1)S(1)} collective-permute-done((bf16[384,1280]{1,0:T(8,128)(2,1)}, bf16[384,1280]{1,0:T(8,128)(2,1)S(1)}, u32[]{:S(2)}, u32[]{:S(2)}) %collective-permute-start.1) | collective-permute-done | bytes 983072 | tf_op jit(solution)/shard_map/ppermute | solution.py:581
  185.6 5.0 %divide_dynamic-update-slice_fusion = (f32[512,1280]{1,0:T(8,128)}, f32[512,1280]{1,0:T(8,128)}) fusion(f32[512,1280]{1,0:T(8,128)} %get-tuple-element.65, bf16[384,1280]{1,0:T(8,128)(2,1)} %collective-permute-done, bf16[384,1280]{1,0:T(8,128)(2,1)S(1)} %collective-permute-done.1, bf16[768,1280]{1,0:T(8,128)(2,1)} %get-tuple-element.60, f32[]{:T(128)} %bitcast.7, ...), kind=kLoop, calls=%fused_computation | loop fusion | flops 4915200 | bytes 7864834 | tf_op jit(solution)/shard_map/dynamic_update_slice | solution.py:605
Async XLA Ops:
  158.7 24.3 %collective-permute-start = (bf16[384,1280]{1,0:T(8,128)(2,1)}, bf16[384,1280]{1,0:T(8,128)(2,1)}, u32[]{:S(2)}, u32[]{:S(2)}) collective-permute-start(bf16[384,1280]{1,0:T(8,128)(2,1)} %get-tuple-element.61), channel_id=1, source_target_pairs={{0,2},{1,3},{2,0},{3,1},{4,6},{5,7},{6,4},{7,5}} | collective-permute-start | bytes 2949128 | tf_op jit(solution)/shard_map/ppermute | solution.py:581
  183.0 2.6 %collective-permute-start.1 = (bf16[384,1280]{1,0:T(8,128)(2,1)}, bf16[384,1280]{1,0:T(8,128)(2,1)S(1)}, u32[]{:S(2)}, u32[]{:S(2)}) collective-permute-start(bf16[384,1280]{1,0:T(8,128)(2,1)} %collective-permute-done), channel_id=1, source_target_pairs={{0,1},{1,0},{2,3},{3,2},{4,5},{5,4},{6,7},{7,6}} | collective-permute-start | bytes 2949128 | tf_op jit(solution)/shard_map/ppermute | solution.py:581

commit v5 on v4

--- a/solution.py
+++ b/solution.py
@@ -1,3 +1,5 @@
+import functools
+
 import jax
 import jax.numpy as jnp
 from jax import lax
@@ -9,7 +11,7 @@
 EPSILON = 1e-12
 MESH = pl.DeviceIdType.MESH
 CHUNKS = 4
-EARLY = 1
+EARLY = 2
 PIECES = 4
 TILE = 256
 BF16 = jnp.bfloat16
@@ -34,6 +36,11 @@
 
 def t_dot(left, right):
     return lax.dot_general(left, right, (((0,), (0,)), ((), ())), preferred_element_type=F32)
+
+
+def fold(values):
+    rows, cols = values.shape
+    return jnp.sum(values.reshape(rows // 8, 8, cols), axis=0)
 
 
 def total(values):
@@ -122,13 +129,14 @@
     def row(values):
         return jnp.broadcast_to(values.reshape(1, values.size).astype(BF16), (16, values.size))
 
-    lanes = lax.broadcasted_iota(jnp.int32, (128, 128), 1)
-    eye[...] = jnp.where(lanes == lax.broadcasted_iota(jnp.int32, (128, 128), 0), 1.0, 0.0).astype(BF16)
+    lanes = lax.broadcasted_iota(jnp.int32, eye.shape, 1)
+    eye[...] = jnp.where(lanes == lax.broadcasted_iota(jnp.int32, eye.shape, 0), 1.0, 0.0).astype(BF16)
 
     def store_transposed(dst, first, rows, values):
-        for place in range(values.shape[1] // 128):
-            block = dot_t(eye[...], values[:, place * 128:(place + 1) * 128])
-            dst[pl.ds(pl.multiple_of(first + place * 128, 128), 128), rows] = block.astype(BF16)
+        for begin in range(0, values.shape[1], eye.shape[0]):
+            size = min(eye.shape[0], values.shape[1] - begin)
+            block = dot_t(eye[0:size, 0:size], values[:, begin:begin + size])
+            dst[pl.ds(pl.multiple_of(first + begin, 128), size), rows] = block.astype(BF16)
 
     u_rows = [row(u0_in[...]), row(u1_in[...]), row(u2_in[...])]
     loads[0].wait()
@@ -180,6 +188,7 @@
     sigmas = jnp.sqrt(n_buf[0] + n_buf[1] + n_buf[2] + n_buf[3])
     sig_out[...] = sigmas
     sig0, sig1, sig2 = sigmas[0:1, 0:1], sigmas[0:1, 1:2], sigmas[0:1, 2:3]
+    inv0, inv1, inv2 = 1.0 / sig0, 1.0 / sig1, 1.0 / sig2
     u0_out[...] = u0_out[...] / sig0
     u1_out[...] = u1_out[...] / sig1
     u2_out[...] = u2_out[...] / sig2
@@ -189,7 +198,7 @@
 
     def y0_tile(tile_no, carry):
         cols = part(tile_no, TILE)
-        y_tile = dot_t(x0[...], w0[cols, :]) / sig0
+        y_tile = dot_t(x0[...], w0[cols, :]) * inv0
         y0[:, cols] = y_tile
         x1[chip, :, cols] = leaky_relu(y_tile).astype(BF16)
         return carry
@@ -229,7 +238,7 @@
     def layer1(chunk_no, carry):
         rows = part(chunk_no, step)
         chunk_copy(x1, other, chunk_no, x1_send, x1_recv).wait_recv()
-        y_val = (dot_t(x1[0, rows, :], w1[:, pl.ds(0, wide1)]) + dot_t(x1[1, rows, :], w1[:, pl.ds(wide1, wide1)])) / sig1
+        y_val = (dot_t(x1[0, rows, :], w1[:, pl.ds(0, wide1)]) + dot_t(x1[1, rows, :], w1[:, pl.ds(wide1, wide1)])) * inv1
         y1[rows, :] = y_val
         x2[chip, rows, :] = leaky_relu(y_val).astype(BF16)
         chunk_copy(x2, chip, chunk_no, x2_send, x2_recv).start()
@@ -249,10 +258,10 @@
         corr2, loss = carry
         rows = part(chunk_no, step)
         chunk_copy(x2, other, chunk_no, x2_send, x2_recv).wait_recv()
-        y_val = (dot_t(x2[0, rows, :], w2[:, pl.ds(0, wide2)]) + dot_t(x2[1, rows, :], w2[:, pl.ds(wide2, wide2)])) / sig2
-        e_val = y_val - dot_t(eye[...], tt[:, rows])
-        corr2 = corr2 + total(e_val * y_val)
-        loss = loss + total(e_val * e_val)
+        y_val = (dot_t(x2[0, rows, :], w2[:, pl.ds(0, wide2)]) + dot_t(x2[1, rows, :], w2[:, pl.ds(wide2, wide2)])) * inv2
+        e_val = y_val - dot_t(eye[0:step, 0:step], tt[:, rows])
+        corr2 = corr2 + fold(e_val * y_val)
+        loss = loss + fold(e_val * e_val)
         e_half = e_val.astype(BF16)
         h2_put[rows, :] = dot_n(e_half, w2[:, part(other, wide2)]).astype(BF16)
         send(h2_put.at[rows, :], h2_got.at[rows, :], h2_send.at[chunk_no], h2_recv.at[chunk_no], far).start()
@@ -260,19 +269,19 @@
         store_transposed(e2_t, 0, rows, e_half)
         return corr2, loss
 
-    zero = jnp.zeros((1, 1), F32)
+    zero = jnp.zeros((8, wide2), F32)
     corr2, loss = lax.fori_loop(0, CHUNKS, layer2, (zero, zero))
 
     def back1(chunk_no, corr1):
         rows = part(chunk_no, step)
         send(h2_put.at[rows, :], h2_got.at[rows, :], h2_send.at[chunk_no], h2_recv.at[chunk_no], far).wait_recv()
         y_val = y1[rows, :]
-        e_val = (h2_own[rows, :] + h2_got[rows, :].astype(F32)) / sig2 * leaky_slope(y_val)
+        e_val = (h2_own[rows, :] + h2_got[rows, :].astype(F32)) * (inv2 * leaky_slope(y_val))
         e_half = e_val.astype(BF16)
         e1[chip, rows, :] = e_half
         chunk_copy(e1, chip, chunk_no, e1_send, e1_recv).start()
         store_transposed(e1_t, 0, rows, e_half)
-        return corr1 + total(e_val * y_val)
+        return corr1 + fold(e_val * y_val)
 
     corr1 = lax.fori_loop(0, CHUNKS, back1, zero)
     lesser = [
@@ -308,29 +317,38 @@
         chunk_copy(e1, other, chunk_no, e1_send, e1_recv).wait_recv()
 
         def h1_tile(tile_no, corr):
-            cols = part(tile_no, TILE)
-            own_cols = pl.ds(pl.multiple_of(chip * wide1 + tile_no * TILE, TILE), TILE)
-            h_val = (dot_n(e1[chip, rows, :], w1[:, own_cols]) + dot_n(e1[other, rows, :], w1x[:, cols])) / sig1
+            cols = part(tile_no, wide2)
+            own_cols = pl.ds(pl.multiple_of(chip * wide1 + tile_no * wide2, 128), wide2)
+            h_val = dot_n(e1[chip, rows, :], w1[:, own_cols]) + dot_n(e1[other, rows, :], w1x[:, cols])
             y_val = y0[rows, cols]
-            e_val = h_val * leaky_slope(y_val)
-            e_half = e_val.astype(BF16)
-            e0[:, cols] = e_half
-            store_transposed(e0_t, tile_no * TILE, rows, e_half)
-            return corr + total(e_val * y_val)
-
-        corr0 = lax.fori_loop(0, wide1 // TILE, h1_tile, corr0)
+            e_val = h_val * (inv1 * leaky_slope(y_val))
+            e0[:, cols] = e_val.astype(BF16)
+            return corr + fold(e_val * y_val)
+
+        corr0 = lax.fori_loop(0, wide1 // wide2, h1_tile, corr0)
         h0_put[rows, :] = dot_n(e0[...], w0[...]).astype(BF16)
         return corr0
+
+    def transpose0(chunk_no):
+        rows = part(chunk_no, step)
+
+        def tile(tile_no, carry):
+            store_transposed(e0_t, tile_no * wide2, rows, e0[:, part(tile_no, wide2)])
+            return carry
+
+        lax.fori_loop(0, wide1 // wide2, tile, 0)
 
     def back0_early(chunk_no, corr0):
         corr0 = back0(chunk_no, corr0)
         h0_copy(chunk_no).start()
+        transpose0(chunk_no)
         return corr0
 
     def back0_late(chunk_no, corr0):
         corr0 = back0(chunk_no, corr0)
         for copy in late_copies(chunk_no):
             copy.start()
+        transpose0(chunk_no)
         return corr0
 
     corr0 = lax.fori_loop(0, EARLY, back0_early, zero)
@@ -338,7 +356,7 @@
     e0_pair = halves(e0_t, e0_out, rows1, 6)
     for copy in e0_pair:
         copy.start()
-    c_buf[me] = pack([corr0, corr1, corr2, loss])
+    c_buf[me] = pack([total(corr) for corr in (corr0, corr1, corr2, loss)])
     c_copies = spread(c_buf, 6)
     for copy in c_copies:
         copy.start()
@@ -354,7 +372,7 @@
     def finish(chunk_no, carry):
         rows = part(chunk_no, step)
         h0_copy(chunk_no).wait_recv()
-        dx[rows, :] = (h0_put[rows, :].astype(F32) + h0_got[rows, :].astype(F32)) / sig0
+        dx[rows, :] = (h0_put[rows, :].astype(F32) + h0_got[rows, :].astype(F32)) * inv0
         for copy in dx_copies(chunk_no):
             copy.start()
         return carry
@@ -430,7 +448,7 @@
             pltpu.VMEM((wide2, n_rows), BF16), pltpu.VMEM((n_rows, wide2), F32), pltpu.VMEM((n_rows, wide2), BF16), pltpu.VMEM((n_rows, wide2), BF16),
             pltpu.VMEM((2, n_rows, wide2), BF16), pltpu.VMEM((wide2, n_rows), BF16), pltpu.VMEM((n_rows // CHUNKS, wide1), BF16), pltpu.VMEM((wide1, n_rows), BF16),
             pltpu.VMEM((n_rows, n0), BF16), pltpu.VMEM((early, n0), BF16), pltpu.VMEM((early, n0), F32),
-            pltpu.VMEM((4, 1, n0 + n1 + n2), F32), pltpu.VMEM((4, 8, 128), F32), pltpu.VMEM((4, 8, 128), F32), pltpu.VMEM((128, 128), BF16),
+            pltpu.VMEM((4, 1, n0 + n1 + n2), F32), pltpu.VMEM((4, 8, 128), F32), pltpu.VMEM((4, 8, 128), F32), pltpu.VMEM((256, 256), BF16),
             dma((5,)), dma((7,)), dma((4,)), dma((4,)), dma((PIECES,)), dma((PIECES,)), dma((PIECES,)), dma((PIECES,)), dma((9,)), dma((9,)),
             dma((CHUNKS,)), dma((CHUNKS,)), dma((CHUNKS,)), dma((CHUNKS,)), dma((CHUNKS,)), dma((CHUNKS,)),
             dma((CHUNKS,)), dma((CHUNKS,)), dma((EARLY,)), dma((EARLY,)), dma((7,)), dma((7,)), dma((EARLY,)), dma((EARLY,)), dma((EARLY,)),
@@ -577,6 +595,73 @@
     )(*inputs)
 
 
+def finish_kernel(flip, real_in, fake_in, both_in, came_in, sig_in, real_out, fake_out, both, came, sig, dx, in_sem, out_sem):
+    me = lax.axis_index("model")
+    batch = me % 2
+    if flip:
+        batch = 1 - batch
+    pieces = out_sem.shape[0]
+    late = both.shape[0]
+    size = late // pieces
+    first = real_out.shape[0] - late
+    scale_copy = pltpu.make_async_copy(sig_in, sig, in_sem.at[2 * pieces])
+    scale_copy.start()
+
+    def pulls(piece):
+        rows = pl.ds(piece * size, size)
+        return (
+            pltpu.make_async_copy(both_in.at[pl.ds(pl.multiple_of(batch * late + piece * size, size), size), :], both.at[rows, :], in_sem.at[2 * piece]),
+            pltpu.make_async_copy(came_in.at[rows, :], came.at[rows, :], in_sem.at[2 * piece + 1]),
+        )
+
+    def push(dst, piece):
+        return pltpu.make_async_copy(dx.at[pl.ds(piece * size, size), :], dst.at[pl.ds(first + piece * size, size), :], out_sem.at[piece])
+
+    for piece in range(pieces):
+        for copy in pulls(piece):
+            copy.start()
+    scale_copy.wait()
+    inv0 = 1.0 / sig[0:1, 0:1]
+    for piece in range(pieces):
+        for copy in pulls(piece):
+            copy.wait()
+        rows = pl.ds(piece * size, size)
+        dx[rows, :] = (both[rows, :].astype(F32) + came[rows, :].astype(F32)) * inv0
+
+        @pl.when(batch == 0)
+        def _():
+            push(real_out, piece).start()
+
+        @pl.when(batch == 1)
+        def _():
+            push(fake_out, piece).start()
+
+    for piece in range(pieces):
+        push(real_out, piece).wait()
+
+
+def run_finish(flip, dx_real, dx_fake, both, came, sig):
+    late, n0 = came.shape
+    pieces = 4
+    hbm = pl.BlockSpec(memory_space=pl.ANY)
+    dma = pltpu.SemaphoreType.DMA
+    shape = jax.ShapeDtypeStruct(dx_real.shape, F32)
+    return pl.pallas_call(
+        functools.partial(finish_kernel, flip),
+        out_shape=(shape, shape),
+        in_specs=[hbm] * 5,
+        out_specs=[hbm] * 2,
+        scratch_shapes=[
+            pltpu.VMEM((late, n0), BF16), pltpu.VMEM((late, n0), BF16), pltpu.VMEM((8, 128), F32), pltpu.VMEM((late, n0), F32),
+            dma((2 * pieces + 1,)), dma((pieces,)),
+        ],
+        input_output_aliases={0: 0, 1: 1},
+        compiler_params=pltpu.CompilerParams(vmem_limit_bytes=67043328),
+        cost_estimate=pl.CostEstimate(flops=4 * late * n0, bytes_accessed=8 * late * n0, transcendentals=0),
+        name="finish",
+    )(dx_real, dx_fake, both, came, sig)
+
+
 def swap(values, bits):
     return lax.ppermute(values, "model", [(dev, dev ^ bits) for dev in range(4)])
 
@@ -589,21 +674,13 @@
     group_spec = P("rep")
 
     def local_step(x_real, x_fake, weight0, weight1, weight2, u_left0, u_left1, u_left2, t_real, t_fake):
-        core = lax.axis_index("model") % 2
         x1, x2, e2, e1, e0, dx, sums, both, v0, v1, v2, u0, u1, u2, sig, cor = run_chain(x_real, x_fake, weight0, weight1, weight2, u_left0, u_left1, u_left2, t_real, t_fake)
         came = swap(sums, 2)
         dw0, dw1, dw2, dx_real, dx_fake, u0, u1, u2, v0, v1, v2, sigmas, loss = run_grads(x1, e1, x2, e2, x_real, x_fake, e0, dx, u0, u1, u2, v0, v1, v2, sig, cor)
         came, sigmas = lax.optimization_barrier((came, sigmas))
         came_mate = swap(came, 1)
-        late = sums.shape[0]
-        first = x_real.shape[0] - late
-
-        def finish(dx_batch, batch_no):
-            got = jnp.where(core == batch_no, came, came_mate)
-            own = both[batch_no * late:(batch_no + 1) * late]
-            dx_late = (own.astype(F32) + got.astype(F32)) / sigmas[0]
-            return lax.dynamic_update_slice(dx_batch, dx_late, (first, 0))
-
-        return (loss[0], finish(dx_real, 0), finish(dx_fake, 1), dw0, dw1, dw2, u0, u1, u2, v0, v1, v2, sigmas)
+        dx_real, dx_fake = run_finish(False, dx_real, dx_fake, both, came, sig)
+        dx_real, dx_fake = run_finish(True, dx_real, dx_fake, both, came_mate, sig)
+        return (loss[0], dx_real, dx_fake, dw0, dw1, dw2, u0, u1, u2, v0, v1, v2, sigmas)
 
     return jax.shard_map(local_step, mesh=mesh, in_specs=(rows_spec, rows_spec, weight_spec, weight_spec, weight_spec, left_spec, left_spec, left_spec, target_spec, target_spec), out_specs=(group_spec, rows_spec, rows_spec, weight_spec, weight_spec, weight_spec, left_spec, left_spec, left_spec, group_spec, group_spec, group_spec, group_spec), check_vma=False)

time: 191 us -> 183 us (0.958)
  waiting for transfers between devices: 7.02 us -> 0.01 us
  other arithmetic: 4.99 us -> 0 us
  Pallas kernels: 176 us -> 180 us
    ppermute x2, waiting for transfers between devices: 7.02 us -> 0.01 us  [swap(): lax.ppermute(values, 'model', [(dev, dev ^ bits) for dev in range(4)])]
    dynamic_update_slice x1 -> x0, other arithmetic: 4.99 us -> none  [finish(): return lax.dynamic_update_slice(dx_batch, dx_late, (first, 0))]
    pallas_call x0 -> x2, Pallas kernels: none -> 4.57 us  [run_finish(): pl.pallas_call(functools.partial(finish_kernel, flip), out_shape=(shape,...]
  transfers between devices with their start and end apart: 2 -> 2, of which waited for: 2 -> 0; matrix products, arithmetic and copies ran while one was open for 0% -> 0% of each run, Pallas kernels for 9% -> 11%
where the time goes in v5:
time: 183 us
  Pallas kernels  180 us (98%)
    pallas_call x1, Pallas kernels, run_chain(): pl.pallas_call(chain_kernel, out_shape=(shape((2 * n_rows, n1), BF16), sh...  158 us
    pallas_call x1, Pallas kernels, run_grads(): pl.pallas_call(grad_kernel, out_shape=(shape((rows1, n0), F32), shape((ro...  17.8 us
    pallas_call x2, Pallas kernels, run_finish(): pl.pallas_call(functools.partial(finish_kernel, flip), out_shape=(shape,...  4.57 us
  transfers between devices with their start and end apart: 2, of which 0 were waited for; matrix products, arithmetic and copies ran while one was open for 0% of the time, Pallas kernels for 11%

profile of v5, /device:TPU:0, one launch (start us, length us, event | category | flops | bytes accessed | tf_op | source)
XLA Modules:
  0.0 182.7 jit_solution(8649863560330625656)
XLA Ops:
  0.6 158.0 %chain.1 = (bf16[1024,5120]{1,0:T(8,128)(2,1)}, bf16[1024,1280]{1,0:T(8,128)(2,1)}, bf16[320,1024]{1,0:T(8,128)(2,1)}, bf16[320,1024]{1,0:T(8,128)(2,1)}, bf16[1...) custom-call(bf16[512,1280]{1,0:T(8,128)(2,1)} %x_real.3, ...), custom_call_target="tpu_custom_call" | custom-call | tf_op jit(solution)/shard_map/chain/pallas_call | solution.py:433
  158.7 1.7 collective-permute-start
  160.3 17.8 %grads.1 = (f32[1280,1280]{1,0:T(8,128)}, f32[320,5120]{1,0:T(8,128)}, f32[320,1280]{1,0:T(8,128)}, f32[512,1280]{1,0:T(8,128)}, f32[512,1280]{1,0:T(8,128)}, /*...) custom-call(bf16[1024,5120]{1,0:T(8,128)(2,1)} %get-tuple-element.48, ...), custom_call_target="tpu_custom_call" | custom-call | flops 7549747200 | bytes 47185920 | tf_op jit(solution)/shard_map/grads/pallas_call | solution.py:576
  178.1 0.0 collective-permute-done.came_in
  178.1 0.1 collective-permute-start.1
  178.2 2.3 %finish.2 = (f32[512,1280]{1,0:T(8,128)}, f32[512,1280]{1,0:T(8,128)}) custom-call(f32[512,1280]{1,0:T(8,128)} %get-tuple-element.63.real_in, f32[512,1280]{1,0:T(8,128)} %get-tuple-element.64.fake_in, bf16[512,1280]{1,0:T(8,128)(2,1)} %get-tuple-element.65.both_in, ...), custom_call_target="tpu_custom_call", output_to_operand_aliasing={{0}: (0, {}), {1}: (1, {})} | custom-call | flops 1310720 | bytes 2621440 | tf_op jit(solution)/shard_map/finish/pallas_call | solution.py:649
  180.4 0.0 collective-permute-done.1.came_in
  180.4 2.3 %finish.3 = (f32[512,1280]{1,0:T(8,128)}, f32[512,1280]{1,0:T(8,128)}) custom-call(f32[512,1280]{1,0:T(8,128)} %get-tuple-element.69.real_in, f32[512,1280]{1,0:T(8,128)} %get-tuple-element.70.fake_in, bf16[512,1280]{1,0:T(8,128)(2,1)} %get-tuple-element.65.both_in, ...), custom_call_target="tpu_custom_call", output_to_operand_aliasing={{0}: (0, {}), {1}: (1, {})} | custom-call | flops 1310720 | bytes 2621440 | tf_op jit(solution)/shard_map/finish/pallas_call | solution.py:649
Async XLA Ops:
  158.7 19.4 %collective-permute-start = (bf16[256,1280]{1,0:T(8,128)(2,1)}, bf16[256,1280]{1,0:T(8,128)(2,1)}, u32[]{:S(2)}, u32[]{:S(2)}) collective-permute-start(bf16[256,1280]{1,0:T(8,128)(2,1)} %get-tuple-element.66), channel_id=1, source_target_pairs={{0,2},{1,3},{2,0},{3,1},{4,6},{5,7},{6,4},{7,5}} | collective-permute-start | bytes 1966088 | tf_op jit(solution)/shard_map/ppermute | solution.py:666
  178.1 2.3 %collective-permute-start.1 = (bf16[256,1280]{1,0:T(8,128)(2,1)}, bf16[256,1280]{1,0:T(8,128)(2,1)}, u32[]{:S(2)}, u32[]{:S(2)}) collective-permute-start(bf16[256,1280]{1,0:T(8,128)(2,1)} %collective-permute-done.came_in), channel_id=1, source_target_pairs={{0,1},{1,0},{2,3},{3,2},{4,5},{5,4},{6,7},{7,6}} | collective-permute-start | bytes 1966088 | tf_op jit(solution)/shard_map/ppermute | solution.py:666

commit v6 on v5

--- a/solution.py
+++ b/solution.py
@@ -50,7 +50,7 @@
 def chain_kernel(x_real, x_fake, w0_in, w1_in, w2_in, u0_in, u1_in, u2_in, t_real, t_fake,
                  x1_out, x2_out, e2_out, e1_out, e0_out, dx_out, sum_out, both_out, v0_out, v1_out, v2_out, u0_out, u1_out, u2_out, sig_out, cor_out,
                  w0, w1, w1x, w2, x0, x1, x2, y0, y1, tt, e2_t, h2_own, h2_put, h2_got, e1, e1_t, e0, e0_t, h0_put, h0_got, dx,
-                 p_buf, n_buf, c_buf,
+                 p_buf, p_sum, n_buf, c_buf,
                  eye, load_sem, put_sem, w_send, w_recv, w1x_send, w1x_recv, fwd_send, fwd_recv, small_send, small_recv,
                  x1_send, x1_recv, x2_send, x2_recv, h2_send, h2_recv, e1_send, e1_recv, h0_send, h0_recv, out_send, out_recv, dx_sem, dx_send, dx_recv, sum_sem, both_sem, both_send, both_recv):
     me = lax.axis_index("model")
@@ -155,13 +155,15 @@
     def spread(buf, first):
         return [send(buf.at[me], buf.at[me], small_send.at[first + which], small_recv.at[first + which], device) for which, device in enumerate((mate, far, diag))]
 
-    p_copies = spread(p_buf, 0)
-    for copy in p_copies:
-        copy.start()
+    p_near = send(p_buf.at[me], p_buf.at[me], small_send.at[0], small_recv.at[0], mate)
+    p_near.start()
+    p_near.wait()
+    p_sum[chip] = p_buf[2 * chip] + p_buf[2 * chip + 1]
+    p_far = send(p_sum.at[chip], p_sum.at[chip], small_send.at[1], small_recv.at[1], far)
+    p_far.start()
     w1x_copy(1).start()
-    for copy in p_copies:
-        copy.wait()
-    p_all = p_buf[0] + p_buf[1] + p_buf[2] + p_buf[3]
+    p_far.wait()
+    p_all = p_sum[0] + p_sum[1]
     spans = ((0, n0, v0_out), (n0, n1, v1_out), (n0 + n1, 2 * wide2, v2_out))
     for first, size, v_out in spans:
         p_vec = p_all[:, first:first + size]
@@ -448,7 +450,7 @@
             pltpu.VMEM((wide2, n_rows), BF16), pltpu.VMEM((n_rows, wide2), F32), pltpu.VMEM((n_rows, wide2), BF16), pltpu.VMEM((n_rows, wide2), BF16),
             pltpu.VMEM((2, n_rows, wide2), BF16), pltpu.VMEM((wide2, n_rows), BF16), pltpu.VMEM((n_rows // CHUNKS, wide1), BF16), pltpu.VMEM((wide1, n_rows), BF16),
             pltpu.VMEM((n_rows, n0), BF16), pltpu.VMEM((early, n0), BF16), pltpu.VMEM((early, n0), F32),
-            pltpu.VMEM((4, 1, n0 + n1 + n2), F32), pltpu.VMEM((4, 8, 128), F32), pltpu.VMEM((4, 8, 128), F32), pltpu.VMEM((256, 256), BF16),
+            pltpu.VMEM((4, 1, n0 + n1 + n2), F32), pltpu.VMEM((2, 1, n0 + n1 + n2), F32), pltpu.VMEM((4, 8, 128), F32), pltpu.VMEM((4, 8, 128), F32), pltpu.VMEM((256, 256), BF16),
             dma((5,)), dma((7,)), dma((4,)), dma((4,)), dma((PIECES,)), dma((PIECES,)), dma((PIECES,)), dma((PIECES,)), dma((9,)), dma((9,)),
             dma((CHUNKS,)), dma((CHUNKS,)), dma((CHUNKS,)), dma((CHUNKS,)), dma((CHUNKS,)), dma((CHUNKS,)),
             dma((CHUNKS,)), dma((CHUNKS,)), dma((EARLY,)), dma((EARLY,)), dma((7,)), dma((7,)), dma((EARLY,)), dma((EARLY,)), dma((EARLY,)),
@@ -466,8 +468,6 @@
     early = dx.shape[0] // 2
     tiles1 = x1_sem.shape[0]
     tiles0 = dw0_sem.shape[0]
-    wide1 = x1.shape[1] // tiles1
-    wide0 = x0.shape[1] // tiles0
 
     def pull(src, dst, which):
         copy = pltpu.make_async_copy(src, dst, in_sem.at[which])
@@ -476,16 +476,18 @@
 
     small = [pull(src, dst, place) for place, (src, dst) in enumerate((
         (u0_in, u0), (u1_in, u1), (u2_in, u2), (v0_in, v0), (v1_in, v1), (v2_in, v2), (sig_in, sig), (cor_in, cor)))]
+    def tile_of(size, tiles, tile_no):
+        return pl.ds(tile_no * (size // tiles), size // tiles)
+
+    got_e1 = pull(e1_in, e1, 11)
+    got_x1 = []
+    for tile_no in range(tiles1):
+        cols = tile_of(x1.shape[1], tiles1, tile_no)
+        copy = pltpu.make_async_copy(x1_in.at[:, cols], x1.at[:, cols], x1_sem.at[tile_no])
+        copy.start()
+        got_x1.append(copy)
     got_e0 = pull(e0_in, e0, 8)
     got_x0 = [pull(x_real, x0.at[pl.ds(0, n_rows), :], 9), pull(x_fake, x0.at[pl.ds(n_rows, n_rows), :], 10)]
-    got_e1 = pull(e1_in, e1, 11)
-
-    def x1_copy(tile_no):
-        cols = pl.ds(pl.multiple_of(tile_no * wide1, 128), wide1)
-        return pltpu.make_async_copy(x1_in.at[:, cols], x1.at[:, cols], x1_sem.at[tile_no])
-
-    for tile_no in range(tiles1):
-        x1_copy(tile_no).start()
     got_dx = pull(dx_in, dx, 12)
     got_2 = [pull(e2_in, e2, 13), pull(x2_in, x2, 14)]
 
@@ -502,61 +504,36 @@
     def scale(layer_no):
         return 1.0 / (n_rows * sig[0:1, layer_no:layer_no + 1])
 
+    pushes = []
+
+    def gradient(errors, layer_in, cols, col, v_new, rate, dst, out, sem):
+        dst[:, cols] = (dot_n(errors[...], layer_in[:, cols]) - col * v_new[:, cols]) * rate
+        copy = pltpu.make_async_copy(dst.at[:, cols], out.at[:, cols], sem)
+        copy.start()
+        pushes.append(copy)
+
+    got_e1.wait()
+    col1, scale1 = column(u1, 1), scale(1)
+    for tile_no in range(tiles1):
+        got_x1[tile_no].wait()
+        gradient(e1, x1, tile_of(x1.shape[1], tiles1, tile_no), col1, v1, scale1, dw1, dw1_out, dw1_sem.at[tile_no])
+    got_dx.wait()
+    for place, dst in enumerate((dx_real, dx_fake)):
+        copy = pltpu.make_async_copy(dx.at[pl.ds(place * early, early), :], dst.at[pl.ds(0, early), :], out_sem.at[place])
+        copy.start()
+        pushes.append(copy)
     got_e0.wait()
     for copy in got_x0:
         copy.wait()
     col0, scale0 = column(u0, 0), scale(0)
-
-    def dw0_copy(tile_no):
-        cols = pl.ds(pl.multiple_of(tile_no * wide0, 128), wide0)
-        return pltpu.make_async_copy(dw0.at[:, cols], dw0_out.at[:, cols], dw0_sem.at[tile_no])
-
-    def dw0_tile(tile_no, carry):
-        cols = pl.ds(pl.multiple_of(tile_no * wide0, 128), wide0)
-        dw0[:, cols] = (dot_n(e0[...], x0[:, cols]) - col0 * v0[:, cols]) * scale0
-        dw0_copy(tile_no).start()
-        return carry
-
-    lax.fori_loop(0, tiles0, dw0_tile, 0)
-    got_e1.wait()
-    col1, scale1 = column(u1, 1), scale(1)
-
-    def dw1_copy(tile_no):
-        cols = pl.ds(pl.multiple_of(tile_no * wide1, 128), wide1)
-        return pltpu.make_async_copy(dw1.at[:, cols], dw1_out.at[:, cols], dw1_sem.at[tile_no])
-
-    def dw1_tile(tile_no, carry):
-        cols = pl.ds(pl.multiple_of(tile_no * wide1, 128), wide1)
-        x1_copy(tile_no).wait()
-        dw1[:, cols] = (dot_n(e1[...], x1[:, cols]) - col1 * v1[:, cols]) * scale1
-        dw1_copy(tile_no).start()
-        return carry
-
-    lax.fori_loop(0, tiles1, dw1_tile, 0)
-    got_dx.wait()
-    pushes = [
-        pltpu.make_async_copy(dx.at[pl.ds(0, early), :], dx_real.at[pl.ds(0, early), :], out_sem.at[0]),
-        pltpu.make_async_copy(dx.at[pl.ds(early, early), :], dx_fake.at[pl.ds(0, early), :], out_sem.at[1]),
-    ]
-    for copy in pushes:
-        copy.start()
+    for tile_no in range(tiles0):
+        gradient(e0, x0, tile_of(x0.shape[1], tiles0, tile_no), col0, v0, scale0, dw0, dw0_out, dw0_sem.at[tile_no])
     for copy in got_2:
         copy.wait()
-    dw2[...] = (dot_n(e2[...], x2[...]) - column(u2, 2) * v2[...]) * scale(2)
-    last = pltpu.make_async_copy(dw2, dw2_out, out_sem.at[2])
-    last.start()
-
-    def drain0(tile_no, carry):
-        dw0_copy(tile_no).wait()
-        return carry
-
-    def drain1(tile_no, carry):
-        dw1_copy(tile_no).wait()
-        return carry
-
-    lax.fori_loop(0, tiles0, drain0, 0)
-    lax.fori_loop(0, tiles1, drain1, 0)
-    for copy in (*pushes, last):
+    col2, scale2 = column(u2, 2), scale(2)
+    for tile_no in range(2):
+        gradient(e2, x2, tile_of(x2.shape[1], 2, tile_no), col2, v2, scale2, dw2, dw2_out, out_sem.at[2 + tile_no])
+    for copy in pushes:
         copy.wait()
 
 
@@ -566,7 +543,7 @@
     n2 = x2.shape[1]
     rows2 = e1.shape[0]
     rows1 = e0.shape[0]
-    tiles1, tiles0 = 8, 5
+    tiles1, tiles0 = 10, 5
     shape = jax.ShapeDtypeStruct
     hbm = pl.BlockSpec(memory_space=pl.ANY)
     vmem = pl.BlockSpec(memory_space=pltpu.VMEM)
@@ -587,7 +564,7 @@
             pltpu.VMEM((both, n0), BF16), pltpu.VMEM((rows1, both), BF16), pltpu.VMEM(dx.shape, F32),
             pltpu.VMEM((rows1, n0), F32), pltpu.VMEM((rows2, n1), F32), pltpu.VMEM((rows2, n2), F32),
             *[pltpu.VMEM(array.shape, F32) for array in (u0, u1, u2, v0, v1, v2, sig, cor)],
-            dma((15,)), dma((tiles1,)), dma((3,)), dma((tiles1,)), dma((tiles0,)),
+            dma((15,)), dma((tiles1,)), dma((4,)), dma((tiles1,)), dma((tiles0,)),
         ],
         compiler_params=pltpu.CompilerParams(vmem_limit_bytes=67043328),
         cost_estimate=pl.CostEstimate(flops=flops, bytes_accessed=45 * 1024 * 1024, transcendentals=0),

time: 183 us -> 185 us (1.011)
  Pallas kernels: 180 us -> 182 us
    pallas_call x1, Pallas kernels: 158 us -> 161 us  [run_chain(): pl.pallas_call(chain_kernel, out_shape=(shape((2 * n_rows, n1), BF16), sh...]
where the time goes in v6:
time: 185 us
  Pallas kernels  182 us (98%)
  starting transfers between devices  1.93 us (1%)
    pallas_call x1, Pallas kernels, run_chain(): pl.pallas_call(chain_kernel, out_shape=(shape((2 * n_rows, n1), BF16), sh...  161 us
    pallas_call x1, Pallas kernels, run_grads(): pl.pallas_call(grad_kernel, out_shape=(shape((rows1, n0), F32), shape((ro...  17.2 us
    pallas_call x2, Pallas kernels, run_finish(): pl.pallas_call(functools.partial(finish_kernel, flip), out_shape=(shape,...  4.59 us
  transfers between devices with their start and end apart: 2, of which 0 were waited for; matrix products, arithmetic and copies ran while one was open for 0% of the time, Pallas kernels for 11%

profile of v6, /device:TPU:0, one launch (start us, length us, event | category | flops | bytes accessed | tf_op | source)
XLA Modules:
  0.0 185.2 jit_solution(3077515296907705897)
XLA Ops:
  0.6 160.6 %chain.1 = (bf16[1024,5120]{1,0:T(8,128)(2,1)}, bf16[1024,1280]{1,0:T(8,128)(2,1)}, bf16[320,1024]{1,0:T(8,128)(2,1)}, bf16[320,1024]{1,0:T(8,128)(2,1)}, bf16[1...) custom-call(bf16[512,1280]{1,0:T(8,128)(2,1)} %x_real.3, ...), custom_call_target="tpu_custom_call" | custom-call | tf_op jit(solution)/shard_map/chain/pallas_call | solution.py:435
  161.3 1.9 %collective-permute-start = (bf16[256,1280]{1,0:T(8,128)(2,1)}, bf16[256,1280]{1,0:T(8,128)(2,1)}, u32[]{:S(2)}, u32[]{:S(2)}) collective-permute-start(bf16[256,1280]{1,0:T(8,128)(2,1)} %get-tuple-element.66), channel_id=1, source_target_pairs={{0,2},{1,3},{2,0},{3,1},{4,6},{5,7},{6,4},{7,5}} | collective-permute-start | bytes 1966088 | tf_op jit(solution)/shard_map/ppermute | solution.py:643
  163.2 17.2 %grads.1 = (f32[1280,1280]{1,0:T(8,128)}, f32[320,5120]{1,0:T(8,128)}, f32[320,1280]{1,0:T(8,128)}, f32[512,1280]{1,0:T(8,128)}, f32[512,1280]{1,0:T(8,128)}, /*...) custom-call(bf16[1024,5120]{1,0:T(8,128)(2,1)} %get-tuple-element.48, ...), custom_call_target="tpu_custom_call" | custom-call | flops 7549747200 | bytes 47185920 | tf_op jit(solution)/shard_map/grads/pallas_call | solution.py:553
  180.4 0.0 collective-permute-done.came_in
  180.4 0.0 collective-permute-start.1
  180.5 2.3 %finish.2 = (f32[512,1280]{1,0:T(8,128)}, f32[512,1280]{1,0:T(8,128)}) custom-call(f32[512,1280]{1,0:T(8,128)} %get-tuple-element.63.real_in, f32[512,1280]{1,0:T(8,128)} %get-tuple-element.64.fake_in, bf16[512,1280]{1,0:T(8,128)(2,1)} %get-tuple-element.65.both_in, ...), custom_call_target="tpu_custom_call", output_to_operand_aliasing={{0}: (0, {}), {1}: (1, {})} | custom-call | flops 1310720 | bytes 2621440 | tf_op jit(solution)/shard_map/finish/pallas_call | solution.py:626
  182.8 0.0 collective-permute-done.1.came_in
  182.8 2.3 %finish.3 = (f32[512,1280]{1,0:T(8,128)}, f32[512,1280]{1,0:T(8,128)}) custom-call(f32[512,1280]{1,0:T(8,128)} %get-tuple-element.69.real_in, f32[512,1280]{1,0:T(8,128)} %get-tuple-element.70.fake_in, bf16[512,1280]{1,0:T(8,128)(2,1)} %get-tuple-element.65.both_in, ...), custom_call_target="tpu_custom_call", output_to_operand_aliasing={{0}: (0, {}), {1}: (1, {})} | custom-call | flops 1310720 | bytes 2621440 | tf_op jit(solution)/shard_map/finish/pallas_call | solution.py:626
Async XLA Ops:
  161.3 19.2 %collective-permute-start = (bf16[256,1280]{1,0:T(8,128)(2,1)}, bf16[256,1280]{1,0:T(8,128)(2,1)}, u32[]{:S(2)}, u32[]{:S(2)}) collective-permute-start(bf16[256,1280]{1,0:T(8,128)(2,1)} %get-tuple-element.66), channel_id=1, source_target_pairs={{0,2},{1,3},{2,0},{3,1},{4,6},{5,7},{6,4},{7,5}} | collective-permute-start | bytes 1966088 | tf_op jit(solution)/shard_map/ppermute | solution.py:643
  180.4 2.3 %collective-permute-start.1 = (bf16[256,1280]{1,0:T(8,128)(2,1)}, bf16[256,1280]{1,0:T(8,128)(2,1)}, u32[]{:S(2)}, u32[]{:S(2)}) collective-permute-start(bf16[256,1280]{1,0:T(8,128)(2,1)} %collective-permute-done.came_in), channel_id=1, source_target_pairs={{0,1},{1,0},{2,3},{3,2},{4,5},{5,4},{6,7},{7,6}} | collective-permute-start | bytes 1966088 | tf_op jit(solution)/shard_map/ppermute | solution.py:643

commit v7 on v6

--- a/solution.py
+++ b/solution.py
@@ -12,7 +12,7 @@
 MESH = pl.DeviceIdType.MESH
 CHUNKS = 4
 EARLY = 2
-PIECES = 4
+PIECES = 5
 TILE = 256
 BF16 = jnp.bfloat16
 F32 = jnp.float32
@@ -97,34 +97,31 @@
         pltpu.make_async_copy(w2_in, w2.at[own2, :], load_sem.at[2]),
     ]
     gives = [
-        send(w0_in, w0.at[own1, :], w_send.at[0], w_recv.at[0], mate),
-        send(w1_in, w1.at[own2, :], w_send.at[1], w_recv.at[1], mate),
-        send(w2_in, w2.at[own2, :], w_send.at[2], w_recv.at[2], mate),
+        send(w0.at[own1, :], w0.at[own1, :], w_send.at[0], w_recv.at[0], mate),
+        send(w1.at[own2, :], w1.at[own2, :], w_send.at[1], w_recv.at[1], mate),
+        send(w2.at[own2, :], w2.at[own2, :], w_send.at[2], w_recv.at[2], mate),
     ]
-    loads[0].start()
     w1x_copy(0).start()
-    for copy in loads[1:]:
-        copy.start()
-
-    def mine(x_in, t_own, t_mate):
+    for copy in loads:
+        copy.start()
+
+    w1x_copy(1).start()
+
+    def mine(x_in, t_own):
         return (
             pltpu.make_async_copy(x_in, x0, load_sem.at[3]),
             pltpu.make_async_copy(t_own, tt.at[own2, :], load_sem.at[4]),
-            send(t_mate, tt.at[own2, :], w_send.at[3], w_recv.at[3], mate),
         )
 
     @pl.when(core == 0)
     def _():
-        for copy in mine(x_real, t_real, t_fake):
+        for copy in mine(x_real, t_real):
             copy.start()
 
     @pl.when(core == 1)
     def _():
-        for copy in mine(x_fake, t_fake, t_real):
+        for copy in mine(x_fake, t_fake):
             copy.start()
-
-    for copy in gives:
-        copy.start()
 
     def row(values):
         return jnp.broadcast_to(values.reshape(1, values.size).astype(BF16), (16, values.size))
@@ -157,11 +154,22 @@
 
     p_near = send(p_buf.at[me], p_buf.at[me], small_send.at[0], small_recv.at[0], mate)
     p_near.start()
+    gives[0].start()
     p_near.wait()
     p_sum[chip] = p_buf[2 * chip] + p_buf[2 * chip + 1]
     p_far = send(p_sum.at[chip], p_sum.at[chip], small_send.at[1], small_recv.at[1], far)
     p_far.start()
-    w1x_copy(1).start()
+    w1x_copy(2).start()
+
+    pltpu.make_async_copy(x_real, x0, load_sem.at[3]).wait()
+    gives[0].wait_recv()
+
+    def y0_tile(tile_no, carry):
+        cols = part(tile_no, TILE)
+        y0[:, cols] = dot_t(x0[...], w0[cols, :])
+        return carry
+
+    lax.fori_loop(0, wide1 // TILE, y0_tile, 0)
     p_far.wait()
     p_all = p_sum[0] + p_sum[1]
     spans = ((0, n0, v0_out), (n0, n1, v1_out), (n0 + n1, 2 * wide2, v2_out))
@@ -183,8 +191,19 @@
     n_copies = spread(n_buf, 3)
     for copy in n_copies:
         copy.start()
-    for piece_no in range(2, PIECES):
+    for piece_no in range(3, PIECES):
         w1x_copy(piece_no).start()
+    for copy in gives[1:]:
+        copy.start()
+
+    @pl.when(core == 0)
+    def _():
+        send(t_fake, tt.at[own2, :], w_send.at[3], w_recv.at[3], mate).start()
+
+    @pl.when(core == 1)
+    def _():
+        send(t_real, tt.at[own2, :], w_send.at[3], w_recv.at[3], mate).start()
+
     for copy in n_copies:
         copy.wait()
     sigmas = jnp.sqrt(n_buf[0] + n_buf[1] + n_buf[2] + n_buf[3])
@@ -195,24 +214,17 @@
     u1_out[...] = u1_out[...] / sig1
     u2_out[...] = u2_out[...] / sig2
 
-    pltpu.make_async_copy(x_real, x0, load_sem.at[3]).wait()
-    gives[0].wait_recv()
-
-    def y0_tile(tile_no, carry):
-        cols = part(tile_no, TILE)
-        y_tile = dot_t(x0[...], w0[cols, :]) * inv0
-        y0[:, cols] = y_tile
-        x1[chip, :, cols] = leaky_relu(y_tile).astype(BF16)
-        return carry
-
-    lax.fori_loop(0, wide1 // TILE, y0_tile, 0)
-
     def chunk_copy(buf, slot, chunk_no, send_sem, recv_sem):
         rows = buf.at[slot, part(chunk_no, step), :]
         return send(rows, rows, send_sem.at[chunk_no], recv_sem.at[chunk_no], far)
 
-    for chunk_no in range(CHUNKS):
+    def layer0(chunk_no, carry):
+        rows = part(chunk_no, step)
+        x1[chip, rows, :] = leaky_relu(y0[rows, :] * inv0).astype(BF16)
         chunk_copy(x1, chip, chunk_no, x1_send, x1_recv).start()
+        return carry
+
+    lax.fori_loop(0, CHUNKS, layer0, 0)
 
     batch = part(core, n_rows)
 
@@ -358,7 +370,7 @@
     e0_pair = halves(e0_t, e0_out, rows1, 6)
     for copy in e0_pair:
         copy.start()
-    c_buf[me] = pack([total(corr) for corr in (corr0, corr1, corr2, loss)])
+    c_buf[me] = pack([total(corr0) * inv0, total(corr1), total(corr2), total(loss)])
     c_copies = spread(c_buf, 6)
     for copy in c_copies:
         copy.start()
@@ -479,17 +491,25 @@
     def tile_of(size, tiles, tile_no):
         return pl.ds(tile_no * (size // tiles), size // tiles)
 
+    def load(src, dst, which):
+        return pltpu.make_async_copy(src, dst, in_sem.at[which])
+
     got_e1 = pull(e1_in, e1, 11)
     got_x1 = []
     for tile_no in range(tiles1):
         cols = tile_of(x1.shape[1], tiles1, tile_no)
-        copy = pltpu.make_async_copy(x1_in.at[:, cols], x1.at[:, cols], x1_sem.at[tile_no])
-        copy.start()
-        got_x1.append(copy)
-    got_e0 = pull(e0_in, e0, 8)
-    got_x0 = [pull(x_real, x0.at[pl.ds(0, n_rows), :], 9), pull(x_fake, x0.at[pl.ds(n_rows, n_rows), :], 10)]
-    got_dx = pull(dx_in, dx, 12)
-    got_2 = [pull(e2_in, e2, 13), pull(x2_in, x2, 14)]
+        got_x1.append(pltpu.make_async_copy(x1_in.at[:, cols], x1.at[:, cols], x1_sem.at[tile_no]))
+    got_e0 = load(e0_in, e0, 8)
+    got_x0 = [load(x_real, x0.at[pl.ds(0, n_rows), :], 9), load(x_fake, x0.at[pl.ds(n_rows, n_rows), :], 10)]
+    got_dx = load(dx_in, dx, 12)
+    got_2 = [load(e2_in, e2, 13), load(x2_in, x2, 14)]
+    queue = [*got_x1, *got_x0, got_e0, got_dx, *got_2]
+
+    def read_on(count=1):
+        for _ in range(min(count, len(queue))):
+            queue.pop(0).start()
+
+    read_on(3)
 
     for copy in small:
         copy.wait()
@@ -516,18 +536,20 @@
     col1, scale1 = column(u1, 1), scale(1)
     for tile_no in range(tiles1):
         got_x1[tile_no].wait()
+        read_on()
         gradient(e1, x1, tile_of(x1.shape[1], tiles1, tile_no), col1, v1, scale1, dw1, dw1_out, dw1_sem.at[tile_no])
-    got_dx.wait()
-    for place, dst in enumerate((dx_real, dx_fake)):
-        copy = pltpu.make_async_copy(dx.at[pl.ds(place * early, early), :], dst.at[pl.ds(0, early), :], out_sem.at[place])
-        copy.start()
-        pushes.append(copy)
     got_e0.wait()
+    read_on(3)
     for copy in got_x0:
         copy.wait()
     col0, scale0 = column(u0, 0), scale(0)
     for tile_no in range(tiles0):
         gradient(e0, x0, tile_of(x0.shape[1], tiles0, tile_no), col0, v0, scale0, dw0, dw0_out, dw0_sem.at[tile_no])
+    got_dx.wait()
+    for place, dst in enumerate((dx_real, dx_fake)):
+        copy = pltpu.make_async_copy(dx.at[pl.ds(place * early, early), :], dst.at[pl.ds(0, early), :], out_sem.at[place])
+        copy.start()
+        pushes.append(copy)
     for copy in got_2:
         copy.wait()
     col2, scale2 = column(u2, 2), scale(2)

time: 185 us -> 182 us (0.984)
  Pallas kernels: 182 us -> 180 us
    pallas_call x1, Pallas kernels: 161 us -> 158 us  [run_chain(): pl.pallas_call(chain_kernel, out_shape=(shape((2 * n_rows, n1), BF16), sh...]
where the time goes in v7:
time: 182 us
  Pallas kernels  180 us (99%)
    pallas_call x1, Pallas kernels, run_chain(): pl.pallas_call(chain_kernel, out_shape=(shape((2 * n_rows, n1), BF16), sh...  158 us
    pallas_call x1, Pallas kernels, run_grads(): pl.pallas_call(grad_kernel, out_shape=(shape((rows1, n0), F32), shape((ro...  17.6 us
    pallas_call x2, Pallas kernels, run_finish(): pl.pallas_call(functools.partial(finish_kernel, flip), out_shape=(shape,...  4.59 us
  transfers between devices with their start and end apart: 2, of which 0 were waited for; matrix products, arithmetic and copies ran while one was open for 0% of the time, Pallas kernels for 11%

profile of v7, /device:TPU:0, one launch (start us, length us, event | category | flops | bytes accessed | tf_op | source)
XLA Modules:
  0.0 182.2 jit_solution(8810598783458629587)
XLA Ops:
  0.6 157.5 %chain.1 = (bf16[1024,5120]{1,0:T(8,128)(2,1)}, bf16[1024,1280]{1,0:T(8,128)(2,1)}, bf16[320,1024]{1,0:T(8,128)(2,1)}, bf16[320,1024]{1,0:T(8,128)(2,1)}, bf16[1...) custom-call(bf16[512,1280]{1,0:T(8,128)(2,1)} %x_real.3, ...), custom_call_target="tpu_custom_call" | custom-call | tf_op jit(solution)/shard_map/chain/pallas_call | solution.py:447
  158.2 1.7 collective-permute-start
  159.9 17.6 %grads.1 = (f32[1280,1280]{1,0:T(8,128)}, f32[320,5120]{1,0:T(8,128)}, f32[320,1280]{1,0:T(8,128)}, f32[512,1280]{1,0:T(8,128)}, f32[512,1280]{1,0:T(8,128)}, /*...) custom-call(bf16[1024,5120]{1,0:T(8,128)(2,1)} %get-tuple-element.48, ...), custom_call_target="tpu_custom_call" | custom-call | flops 7549747200 | bytes 47185920 | tf_op jit(solution)/shard_map/grads/pallas_call | solution.py:575
  177.4 0.0 collective-permute-done.came_in
  177.4 0.0 collective-permute-start.1
  177.5 2.3 %finish.2 = (f32[512,1280]{1,0:T(8,128)}, f32[512,1280]{1,0:T(8,128)}) custom-call(f32[512,1280]{1,0:T(8,128)} %get-tuple-element.63.real_in, f32[512,1280]{1,0:T(8,128)} %get-tuple-element.64.fake_in, bf16[512,1280]{1,0:T(8,128)(2,1)} %get-tuple-element.65.both_in, ...), custom_call_target="tpu_custom_call", output_to_operand_aliasing={{0}: (0, {}), {1}: (1, {})} | custom-call | flops 1310720 | bytes 2621440 | tf_op jit(solution)/shard_map/finish/pallas_call | solution.py:648
  179.8 0.0 collective-permute-done.1.came_in
  179.8 2.3 %finish.3 = (f32[512,1280]{1,0:T(8,128)}, f32[512,1280]{1,0:T(8,128)}) custom-call(f32[512,1280]{1,0:T(8,128)} %get-tuple-element.69.real_in, f32[512,1280]{1,0:T(8,128)} %get-tuple-element.70.fake_in, bf16[512,1280]{1,0:T(8,128)(2,1)} %get-tuple-element.65.both_in, ...), custom_call_target="tpu_custom_call", output_to_operand_aliasing={{0}: (0, {}), {1}: (1, {})} | custom-call | flops 1310720 | bytes 2621440 | tf_op jit(solution)/shard_map/finish/pallas_call | solution.py:648
Async XLA Ops:
  158.2 19.2 %collective-permute-start = (bf16[256,1280]{1,0:T(8,128)(2,1)}, bf16[256,1280]{1,0:T(8,128)(2,1)}, u32[]{:S(2)}, u32[]{:S(2)}) collective-permute-start(bf16[256,1280]{1,0:T(8,128)(2,1)} %get-tuple-element.66), channel_id=1, source_target_pairs={{0,2},{1,3},{2,0},{3,1},{4,6},{5,7},{6,4},{7,5}} | collective-permute-start | bytes 1966088 | tf_op jit(solution)/shard_map/ppermute | solution.py:665
  177.4 2.3 %collective-permute-start.1 = (bf16[256,1280]{1,0:T(8,128)(2,1)}, bf16[256,1280]{1,0:T(8,128)(2,1)}, u32[]{:S(2)}, u32[]{:S(2)}) collective-permute-start(bf16[256,1280]{1,0:T(8,128)(2,1)} %collective-permute-done.came_in), channel_id=1, source_target_pairs={{0,1},{1,0},{2,3},{3,2},{4,5},{5,4},{6,7},{7,6}} | collective-permute-start | bytes 1966088 | tf_op jit(solution)/shard_map/ppermute | solution.py:665

commit v8 on v7

--- a/solution.py
+++ b/solution.py
@@ -11,7 +11,7 @@
 EPSILON = 1e-12
 MESH = pl.DeviceIdType.MESH
 CHUNKS = 4
-EARLY = 2
+EARLY = 1
 PIECES = 5
 TILE = 256
 BF16 = jnp.bfloat16

time: 182 us -> 181 us (level)
  Pallas kernels: 180 us -> 173 us
  waiting for transfers between devices: 0.01 us -> 4.69 us
    pallas_call x1, Pallas kernels: 158 us -> 151 us  [run_chain(): pl.pallas_call(chain_kernel, out_shape=(shape((2 * n_rows, n1), BF16), sh...]
    ppermute x2, waiting for transfers between devices: 0.01 us -> 4.69 us  [swap(): lax.ppermute(values, 'model', [(dev, dev ^ bits) for dev in range(4)])]
  transfers between devices with their start and end apart: 2 -> 2, of which waited for: 0 -> 1; matrix products, arithmetic and copies ran while one was open for 0% -> 0% of each run, Pallas kernels for 11% -> 11%
where the time goes in v8:
time: 181 us
  Pallas kernels  173 us (96%)
  waiting for transfers between devices  4.69 us (3%)
  starting transfers between devices  1.82 us (1%)
    pallas_call x1, Pallas kernels, run_chain(): pl.pallas_call(chain_kernel, out_shape=(shape((2 * n_rows, n1), BF16), sh...  151 us
    pallas_call x1, Pallas kernels, run_grads(): pl.pallas_call(grad_kernel, out_shape=(shape((rows1, n0), F32), shape((ro...  17.5 us
    pallas_call x2, Pallas kernels, run_finish(): pl.pallas_call(functools.partial(finish_kernel, flip), out_shape=(shape,...  5.2 us
    ppermute x2, waiting for transfers between devices, swap(): lax.ppermute(values, 'model', [(dev, dev ^ bits) for dev in range(4)])  4.69 us
  transfers between devices with their start and end apart: 2, of which 1 were waited for; matrix products, arithmetic and copies ran while one was open for 0% of the time, Pallas kernels for 11%

profile of v8, /device:TPU:0, one launch (start us, length us, event | category | flops | bytes accessed | tf_op | source)
XLA Modules:
  0.0 180.8 jit_solution(7138908896080472308)
XLA Ops:
  0.6 150.7 %chain.1 = (bf16[1024,5120]{1,0:T(8,128)(2,1)}, bf16[1024,1280]{1,0:T(8,128)(2,1)}, bf16[320,1024]{1,0:T(8,128)(2,1)}, bf16[320,1024]{1,0:T(8,128)(2,1)}, bf16[1...) custom-call(bf16[512,1280]{1,0:T(8,128)(2,1)} %x_real.3, ...), custom_call_target="tpu_custom_call" | custom-call | tf_op jit(solution)/shard_map/chain/pallas_call | solution.py:447
  151.4 1.8 %collective-permute-start = (bf16[384,1280]{1,0:T(8,128)(2,1)}, bf16[384,1280]{1,0:T(8,128)(2,1)}, u32[]{:S(2)}, u32[]{:S(2)}) collective-permute-start(bf16[384,1280]{1,0:T(8,128)(2,1)} %get-tuple-element.66), channel_id=1, source_target_pairs={{0,2},{1,3},{2,0},{3,1},{4,6},{5,7},{6,4},{7,5}} | collective-permute-start | bytes 2949128 | tf_op jit(solution)/shard_map/ppermute | solution.py:665
  153.2 17.5 %grads.1 = (f32[1280,1280]{1,0:T(8,128)}, f32[320,5120]{1,0:T(8,128)}, f32[320,1280]{1,0:T(8,128)}, f32[512,1280]{1,0:T(8,128)}, f32[512,1280]{1,0:T(8,128)}, /*...) custom-call(bf16[1024,5120]{1,0:T(8,128)(2,1)} %get-tuple-element.48, ...), custom_call_target="tpu_custom_call" | custom-call | flops 7549747200 | bytes 47185920 | tf_op jit(solution)/shard_map/grads/pallas_call | solution.py:575
  170.7 4.7 %collective-permute-done.came_in = bf16[384,1280]{1,0:T(8,128)(2,1)} collective-permute-done((bf16[384,1280]{1,0:T(8,128)(2,1)}, bf16[384,1280]{1,0:T(8,128)(2,1)}, u32[]{:S(2)}, u32[]{:S(2)}) %collective-permute-start) | collective-permute-done | bytes 983072 | tf_op jit(solution)/shard_map/ppermute | solution.py:665
  175.4 0.0 collective-permute-start.1
  175.4 2.6 %finish.2 = (f32[512,1280]{1,0:T(8,128)}, f32[512,1280]{1,0:T(8,128)}) custom-call(f32[512,1280]{1,0:T(8,128)} %get-tuple-element.63.real_in, f32[512,1280]{1,0:T(8,128)} %get-tuple-element.64.fake_in, bf16[768,1280]{1,0:T(8,128)(2,1)} %get-tuple-element.65.both_in, ...), custom_call_target="tpu_custom_call", output_to_operand_aliasing={{0}: (0, {}), {1}: (1, {})} | custom-call | flops 1966080 | bytes 3932160 | tf_op jit(solution)/shard_map/finish/pallas_call | solution.py:648
  178.0 0.0 collective-permute-done.1.came_in
  178.0 2.6 %finish.3 = (f32[512,1280]{1,0:T(8,128)}, f32[512,1280]{1,0:T(8,128)}) custom-call(f32[512,1280]{1,0:T(8,128)} %get-tuple-element.69.real_in, f32[512,1280]{1,0:T(8,128)} %get-tuple-element.70.fake_in, bf16[768,1280]{1,0:T(8,128)(2,1)} %get-tuple-element.65.both_in, ...), custom_call_target="tpu_custom_call", output_to_operand_aliasing={{0}: (0, {}), {1}: (1, {})} | custom-call | flops 1966080 | bytes 3932160 | tf_op jit(solution)/shard_map/finish/pallas_call | solution.py:648
Async XLA Ops:
  151.4 24.1 %collective-permute-start = (bf16[384,1280]{1,0:T(8,128)(2,1)}, bf16[384,1280]{1,0:T(8,128)(2,1)}, u32[]{:S(2)}, u32[]{:S(2)}) collective-permute-start(bf16[384,1280]{1,0:T(8,128)(2,1)} %get-tuple-element.66), channel_id=1, source_target_pairs={{0,2},{1,3},{2,0},{3,1},{4,6},{5,7},{6,4},{7,5}} | collective-permute-start | bytes 2949128 | tf_op jit(solution)/shard_map/ppermute | solution.py:665
  175.4 2.6 %collective-permute-start.1 = (bf16[384,1280]{1,0:T(8,128)(2,1)}, bf16[384,1280]{1,0:T(8,128)(2,1)}, u32[]{:S(2)}, u32[]{:S(2)}) collective-permute-start(bf16[384,1280]{1,0:T(8,128)(2,1)} %collective-permute-done.came_in), channel_id=1, source_target_pairs={{0,1},{1,0},{2,3},{3,2},{4,5},{5,4},{6,7},{7,6}} | collective-permute-start | bytes 2949128 | tf_op jit(solution)/shard_map/ppermute | solution.py:665

commit v9 on v8

--- a/solution.py
+++ b/solution.py
@@ -160,6 +160,7 @@
     p_far = send(p_sum.at[chip], p_sum.at[chip], small_send.at[1], small_recv.at[1], far)
     p_far.start()
     w1x_copy(2).start()
+    w1x_copy(3).start()
 
     pltpu.make_async_copy(x_real, x0, load_sem.at[3]).wait()
     gives[0].wait_recv()
@@ -191,7 +192,7 @@
     n_copies = spread(n_buf, 3)
     for copy in n_copies:
         copy.start()
-    for piece_no in range(3, PIECES):
+    for piece_no in range(4, PIECES):
         w1x_copy(piece_no).start()
     for copy in gives[1:]:
         copy.start()
@@ -567,11 +568,12 @@
     rows1 = e0.shape[0]
     tiles1, tiles0 = 10, 5
     shape = jax.ShapeDtypeStruct
-    hbm = pl.BlockSpec(memory_space=pl.ANY)
+    hbm = pl.BlockSpec(memory_space=pltpu.HBM)
     vmem = pl.BlockSpec(memory_space=pltpu.VMEM)
     dma = pltpu.SemaphoreType.DMA
     flops = 2 * both * (rows2 * (n1 + n2) + rows1 * n0)
     inputs = (x1, e1, x2, e2, x_real, x_fake, e0, dx, u0, u1, u2, v0, v1, v2, sig, cor)
+    inputs = tuple(pltpu.with_memory_space_constraint(array, pltpu.HBM) for array in inputs)
     return pl.pallas_call(
         grad_kernel,
         out_shape=(
@@ -588,44 +590,30 @@
             *[pltpu.VMEM(array.shape, F32) for array in (u0, u1, u2, v0, v1, v2, sig, cor)],
             dma((15,)), dma((tiles1,)), dma((4,)), dma((tiles1,)), dma((tiles0,)),
         ],
-        compiler_params=pltpu.CompilerParams(vmem_limit_bytes=67043328),
+        compiler_params=pltpu.CompilerParams(vmem_limit_bytes=48 * 1024 * 1024),
         cost_estimate=pl.CostEstimate(flops=flops, bytes_accessed=45 * 1024 * 1024, transcendentals=0),
         name="grads",
     )(*inputs)
 
 
-def finish_kernel(flip, real_in, fake_in, both_in, came_in, sig_in, real_out, fake_out, both, came, sig, dx, in_sem, out_sem):
+def finish_kernel(flip, real_in, fake_in, both, came, sig, real_out, fake_out, dx, out_sem):
     me = lax.axis_index("model")
     batch = me % 2
     if flip:
         batch = 1 - batch
     pieces = out_sem.shape[0]
-    late = both.shape[0]
+    late = came.shape[0]
     size = late // pieces
     first = real_out.shape[0] - late
-    scale_copy = pltpu.make_async_copy(sig_in, sig, in_sem.at[2 * pieces])
-    scale_copy.start()
-
-    def pulls(piece):
-        rows = pl.ds(piece * size, size)
-        return (
-            pltpu.make_async_copy(both_in.at[pl.ds(pl.multiple_of(batch * late + piece * size, size), size), :], both.at[rows, :], in_sem.at[2 * piece]),
-            pltpu.make_async_copy(came_in.at[rows, :], came.at[rows, :], in_sem.at[2 * piece + 1]),
-        )
+    inv0 = 1.0 / sig[0:1, 0:1]
 
     def push(dst, piece):
         return pltpu.make_async_copy(dx.at[pl.ds(piece * size, size), :], dst.at[pl.ds(first + piece * size, size), :], out_sem.at[piece])
 
     for piece in range(pieces):
-        for copy in pulls(piece):
-            copy.start()
-    scale_copy.wait()
-    inv0 = 1.0 / sig[0:1, 0:1]
-    for piece in range(pieces):
-        for copy in pulls(piece):
-            copy.wait()
         rows = pl.ds(piece * size, size)
-        dx[rows, :] = (both[rows, :].astype(F32) + came[rows, :].astype(F32)) * inv0
+        own = pl.ds(pl.multiple_of(batch * late + piece * size, size), size)
+        dx[rows, :] = (both[own, :].astype(F32) + came[rows, :].astype(F32)) * inv0
 
         @pl.when(batch == 0)
         def _():
@@ -642,20 +630,17 @@
 def run_finish(flip, dx_real, dx_fake, both, came, sig):
     late, n0 = came.shape
     pieces = 4
-    hbm = pl.BlockSpec(memory_space=pl.ANY)
-    dma = pltpu.SemaphoreType.DMA
+    hbm = pl.BlockSpec(memory_space=pltpu.HBM)
+    vmem = pl.BlockSpec(memory_space=pltpu.VMEM)
     shape = jax.ShapeDtypeStruct(dx_real.shape, F32)
     return pl.pallas_call(
         functools.partial(finish_kernel, flip),
         out_shape=(shape, shape),
-        in_specs=[hbm] * 5,
+        in_specs=[hbm] * 2 + [vmem] * 3,
         out_specs=[hbm] * 2,
-        scratch_shapes=[
-            pltpu.VMEM((late, n0), BF16), pltpu.VMEM((late, n0), BF16), pltpu.VMEM((8, 128), F32), pltpu.VMEM((late, n0), F32),
-            dma((2 * pieces + 1,)), dma((pieces,)),
-        ],
+        scratch_shapes=[pltpu.VMEM((late, n0), F32), pltpu.SemaphoreType.DMA((pieces,))],
         input_output_aliases={0: 0, 1: 1},
-        compiler_params=pltpu.CompilerParams(vmem_limit_bytes=67043328),
+        compiler_params=pltpu.CompilerParams(vmem_limit_bytes=16 * 1024 * 1024),
         cost_estimate=pl.CostEstimate(flops=4 * late * n0, bytes_accessed=8 * late * n0, transcendentals=0),
         name="finish",
     )(dx_real, dx_fake, both, came, sig)

time: 181 us -> 180 us (level)
  Pallas kernels: 173 us -> 171 us
    pallas_call x2, Pallas kernels: 5.2 us -> 2.85 us  [run_finish(): pl.pallas_call(functools.partial(finish_kernel, flip), out_shape=(shape,...]
  transfers between devices with their start and end apart: 2 -> 2, of which waited for: 1 -> 2; matrix products, arithmetic and copies ran while one was open for 0% -> 0% of each run, Pallas kernels for 11% -> 11%
where the time goes in v9:
time: 180 us
  Pallas kernels  171 us (95%)
  waiting for transfers between devices  5.65 us (3%)
  starting transfers between devices  1.82 us (1%)
    pallas_call x1, Pallas kernels, run_chain(): pl.pallas_call(chain_kernel, out_shape=(shape((2 * n_rows, n1), BF16), sh...  151 us
    pallas_call x1, Pallas kernels, run_grads(): pl.pallas_call(grad_kernel, out_shape=(shape((rows1, n0), F32), shape((ro...  17.7 us
    ppermute x2, waiting for transfers between devices, swap(): lax.ppermute(values, 'model', [(dev, dev ^ bits) for dev in range(4)])  5.65 us
  transfers between devices with their start and end apart: 2, of which 2 were waited for; matrix products, arithmetic and copies ran while one was open for 0% of the time, Pallas kernels for 11%

profile of v9, /device:TPU:0, one launch (start us, length us, event | category | flops | bytes accessed | tf_op | source)
XLA Modules:
  0.0 179.6 jit_solution(17203285824048345197)
XLA Ops:
  0.6 150.7 %chain.1 = (bf16[1024,5120]{1,0:T(8,128)(2,1)}, bf16[1024,1280]{1,0:T(8,128)(2,1)}, bf16[320,1024]{1,0:T(8,128)(2,1)}, bf16[320,1024]{1,0:T(8,128)(2,1)}, bf16[1...) custom-call(bf16[512,1280]{1,0:T(8,128)(2,1)} %x_real.3, ...), custom_call_target="tpu_custom_call" | custom-call | tf_op jit(solution)/shard_map/chain/pallas_call | solution.py:448
  151.4 1.8 %collective-permute-start = (bf16[384,1280]{1,0:T(8,128)(2,1)}, bf16[384,1280]{1,0:T(8,128)(2,1)S(1)}, u32[]{:S(2)}, u32[]{:S(2)}) collective-permute-start(bf16[384,1280]{1,0:T(8,128)(2,1)} %get-tuple-element.66), channel_id=1, source_target_pairs={{0,2},{1,3},{2,0},{3,1},{4,6},{5,7},{6,4},{7,5}} | collective-permute-start | bytes 2949128 | tf_op jit(solution)/shard_map/ppermute | solution.py:650
  153.2 0.0 copy-start
  153.2 0.0 copy-start.1
  153.2 17.7 %grads.1 = (f32[1280,1280]{1,0:T(8,128)}, f32[320,5120]{1,0:T(8,128)}, f32[320,1280]{1,0:T(8,128)}, f32[512,1280]{1,0:T(8,128)}, f32[512,1280]{1,0:T(8,128)}, /*...) custom-call(bf16[1024,5120]{1,0:T(8,128)(2,1)} %get-tuple-element.48, ...), custom_call_target="tpu_custom_call" | custom-call | flops 7549747200 | bytes 47185920 | tf_op jit(solution)/shard_map/grads/pallas_call | solution.py:577
  170.9 4.5 %collective-permute-done.came = bf16[384,1280]{1,0:T(8,128)(2,1)S(1)} collective-permute-done((bf16[384,1280]{1,0:T(8,128)(2,1)}, bf16[384,1280]{1,0:T(8,128)(2,1)S(1)}, u32[]{:S(2)}, u32[]{:S(2)}) %collective-permute-start) | collective-permute-done | bytes 983072 | tf_op jit(solution)/shard_map/ppermute | solution.py:650
  175.4 0.0 collective-permute-start.1
  175.5 0.0 copy-done
  175.5 0.0 copy-done.1
  175.5 1.4 finish.2
  176.9 1.1 collective-permute-done.1.came
  178.0 1.4 finish.3
Async XLA Ops:
  151.4 24.1 %collective-permute-start = (bf16[384,1280]{1,0:T(8,128)(2,1)}, bf16[384,1280]{1,0:T(8,128)(2,1)S(1)}, u32[]{:S(2)}, u32[]{:S(2)}) collective-permute-start(bf16[384,1280]{1,0:T(8,128)(2,1)} %get-tuple-element.66), channel_id=1, source_target_pairs={{0,2},{1,3},{2,0},{3,1},{4,6},{5,7},{6,4},{7,5}} | collective-permute-start | bytes 2949128 | tf_op jit(solution)/shard_map/ppermute | solution.py:650
  153.2 22.2 %copy-start = (bf16[768,1280]{1,0:T(8,128)(2,1)S(1)}, bf16[768,1280]{1,0:T(8,128)(2,1)}, u32[]{:S(2)}) copy-start(bf16[768,1280]{1,0:T(8,128)(2,1)} %get-tuple-element.65.both) | copy-start | bytes 5898244
  153.2 22.2 %copy-start.1 = (f32[8,128]{1,0:T(8,128)S(1)}, f32[8,128]{1,0:T(8,128)}, u32[]{:S(2)}) copy-start(f32[8,128]{1,0:T(8,128)} %get-tuple-element.60.sig_in.sig) | copy-start | bytes 12292
  175.4 2.6 %collective-permute-start.1 = (bf16[384,1280]{1,0:T(8,128)(2,1)S(1)}, bf16[384,1280]{1,0:T(8,128)(2,1)S(1)}, u32[]{:S(2)}, u32[]{:S(2)}) collective-permute-start(bf16[384,1280]{1,0:T(8,128)(2,1)S(1)} %collective-permute-done.came), channel_id=1, source_target_pairs={{0,1},{1,0},{2,3},{3,2},{4,5},{5,4},{6,7},{7,6}} | collective-permute-start | bytes 2949128 | tf_op jit(solution)/shard_map/ppermute | solution.py:650

commit v10 on v9

--- a/solution.py
+++ b/solution.py
@@ -7,11 +7,13 @@
 from jax.experimental.pallas import tpu as pltpu
 from jax.sharding import PartitionSpec as P
 
+
 SLOPE = 0.2
 EPSILON = 1e-12
 MESH = pl.DeviceIdType.MESH
 CHUNKS = 4
 EARLY = 1
+MIDDLE = 2
 PIECES = 5
 TILE = 256
 BF16 = jnp.bfloat16
@@ -34,10 +36,6 @@
     return lax.dot_general(left, right, (((1,), (0,)), ((), ())), preferred_element_type=F32)
 
 
-def t_dot(left, right):
-    return lax.dot_general(left, right, (((0,), (0,)), ((), ())), preferred_element_type=F32)
-
-
 def fold(values):
     rows, cols = values.shape
     return jnp.sum(values.reshape(rows // 8, 8, cols), axis=0)
@@ -48,11 +46,11 @@
 
 
 def chain_kernel(x_real, x_fake, w0_in, w1_in, w2_in, u0_in, u1_in, u2_in, t_real, t_fake,
-                 x1_out, x2_out, e2_out, e1_out, e0_out, dx_out, sum_out, both_out, v0_out, v1_out, v2_out, u0_out, u1_out, u2_out, sig_out, cor_out,
-                 w0, w1, w1x, w2, x0, x1, x2, y0, y1, tt, e2_t, h2_own, h2_put, h2_got, e1, e1_t, e0, e0_t, h0_put, h0_got, dx,
+                 x1_out, x2_out, e2_out, e1_out, e0_out, got_out, mid_out, last_out, both_out, v0_out, v1_out, v2_out, u0_out, u1_out, u2_out, sig_out, cor_out,
+                 w0, w1, w1x, w2, x0, x1, x2, y0, y1, tt, e2_t, h2_own, h2_put, h2_got, e1, e1_t, e0, e0_t, h0_put,
                  p_buf, p_sum, n_buf, c_buf,
                  eye, load_sem, put_sem, w_send, w_recv, w1x_send, w1x_recv, fwd_send, fwd_recv, small_send, small_recv,
-                 x1_send, x1_recv, x2_send, x2_recv, h2_send, h2_recv, e1_send, e1_recv, h0_send, h0_recv, out_send, out_recv, dx_sem, dx_send, dx_recv, sum_sem, both_sem, both_send, both_recv):
+                 x1_send, x1_recv, x2_send, x2_recv, h2_send, h2_recv, e1_send, e1_recv, h0_send, h0_recv, out_send, out_recv, sum_sem, both_sem, both_send, both_recv):
     me = lax.axis_index("model")
     chip = me // 2
     core = me % 2
@@ -311,21 +309,21 @@
     for piece_no in range(PIECES):
         w1x_forward(piece_no).wait_recv()
 
-    late = n_rows - EARLY * step
-
     def h0_copy(chunk_no):
         rows = part(chunk_no, step)
-        return send(h0_put.at[rows, :], h0_got.at[rows, :], h0_send.at[chunk_no], h0_recv.at[chunk_no], far)
-
-    def late_copies(chunk_no):
+        return send(h0_put.at[rows, :], got_out.at[rows, :], h0_send.at[chunk_no], h0_recv.at[chunk_no], far)
+
+    def both_copies(chunk_no):
         src = h0_put.at[part(chunk_no, step), :]
-        place = chunk_no - EARLY
-        dst = both_out.at[pl.ds(pl.multiple_of(core * late + place * step, step), step), :]
+        dst = both_out.at[pl.ds(pl.multiple_of(core * n_rows + chunk_no * step, step), step), :]
         return (
-            pltpu.make_async_copy(src, sum_out.at[part(place, step), :], sum_sem.at[place]),
-            pltpu.make_async_copy(src, dst, both_sem.at[place]),
-            send(src, dst, both_send.at[place], both_recv.at[place], mate),
+            pltpu.make_async_copy(src, dst, both_sem.at[chunk_no]),
+            send(src, dst, both_send.at[chunk_no], both_recv.at[chunk_no], mate),
         )
+
+    def late_copy(sum_out, start, chunk_no):
+        dst = sum_out.at[part(chunk_no - start, step), :]
+        return pltpu.make_async_copy(h0_put.at[part(chunk_no, step), :], dst, sum_sem.at[chunk_no])
 
     def back0(chunk_no, corr0):
         rows = part(chunk_no, step)
@@ -353,21 +351,24 @@
 
         lax.fori_loop(0, wide1 // wide2, tile, 0)
 
-    def back0_early(chunk_no, corr0):
+    def early_chunk(chunk_no, corr0):
         corr0 = back0(chunk_no, corr0)
-        h0_copy(chunk_no).start()
-        transpose0(chunk_no)
-        return corr0
-
-    def back0_late(chunk_no, corr0):
-        corr0 = back0(chunk_no, corr0)
-        for copy in late_copies(chunk_no):
+        for copy in (h0_copy(chunk_no), *both_copies(chunk_no)):
             copy.start()
         transpose0(chunk_no)
         return corr0
 
-    corr0 = lax.fori_loop(0, EARLY, back0_early, zero)
-    corr0 = lax.fori_loop(EARLY, CHUNKS, back0_late, corr0)
+    def late_chunk(sum_out, start, chunk_no, corr0):
+        corr0 = back0(chunk_no, corr0)
+        for copy in (late_copy(sum_out, start, chunk_no), *both_copies(chunk_no)):
+            copy.start()
+        transpose0(chunk_no)
+        return corr0
+
+    corr0 = jnp.zeros((8, wide2), F32)
+    corr0 = lax.fori_loop(0, EARLY, early_chunk, corr0)
+    corr0 = lax.fori_loop(EARLY, EARLY + MIDDLE, functools.partial(late_chunk, mid_out, EARLY), corr0)
+    corr0 = lax.fori_loop(EARLY + MIDDLE, CHUNKS, functools.partial(late_chunk, last_out, EARLY + MIDDLE), corr0)
     e0_pair = halves(e0_t, e0_out, rows1, 6)
     for copy in e0_pair:
         copy.start()
@@ -376,23 +377,6 @@
     for copy in c_copies:
         copy.start()
 
-    def dx_copies(chunk_no):
-        rows = part(chunk_no, step)
-        dst = dx_out.at[pl.ds(pl.multiple_of((core * EARLY + chunk_no) * step, step), step), :]
-        return (
-            pltpu.make_async_copy(dx.at[rows, :], dst, dx_sem.at[chunk_no]),
-            send(dx.at[rows, :], dst, dx_send.at[chunk_no], dx_recv.at[chunk_no], mate),
-        )
-
-    def finish(chunk_no, carry):
-        rows = part(chunk_no, step)
-        h0_copy(chunk_no).wait_recv()
-        dx[rows, :] = (h0_put[rows, :].astype(F32) + h0_got[rows, :].astype(F32)) * inv0
-        for copy in dx_copies(chunk_no):
-            copy.start()
-        return carry
-
-    lax.fori_loop(0, EARLY, finish, 0)
     for copy in c_copies:
         copy.wait()
     cor_out[...] = c_buf[0] + c_buf[1] + c_buf[2] + c_buf[3]
@@ -417,20 +401,15 @@
 
     lax.fori_loop(0, CHUNKS, drain, 0)
 
-    def drain_early(chunk_no, carry):
-        h0_copy(chunk_no).wait_send()
-        for copy in dx_copies(chunk_no):
+    for chunk_no in range(CHUNKS):
+        if chunk_no < EARLY:
+            h0_copy(chunk_no).wait()
+        elif chunk_no < EARLY + MIDDLE:
+            late_copy(mid_out, EARLY, chunk_no).wait()
+        else:
+            late_copy(last_out, EARLY + MIDDLE, chunk_no).wait()
+        for copy in both_copies(chunk_no):
             copy.wait()
-        return carry
-
-    lax.fori_loop(0, EARLY, drain_early, 0)
-
-    def drain_late(chunk_no, carry):
-        for copy in late_copies(chunk_no):
-            copy.wait()
-        return carry
-
-    lax.fori_loop(EARLY, CHUNKS, drain_late, 0)
 
 
 def run_chain(x_real, x_fake, weight0, weight1, weight2, u_left0, u_left1, u_left2, t_real, t_fake):
@@ -439,8 +418,9 @@
     rows2, n1 = weight1.shape
     wide1, wide2 = 2 * rows1, 2 * rows2
     n2 = 2 * wide2
-    early = n_rows // CHUNKS * EARLY
-    late = n_rows - early
+    step = n_rows // CHUNKS
+    early, middle = EARLY * step, MIDDLE * step
+    last = n_rows - early - middle
     hbm = pl.BlockSpec(memory_space=pl.ANY)
     vmem = pl.BlockSpec(memory_space=pltpu.VMEM)
     shape = jax.ShapeDtypeStruct
@@ -449,36 +429,35 @@
         chain_kernel,
         out_shape=(
             shape((2 * n_rows, n1), BF16), shape((2 * n_rows, n2), BF16), shape((rows2, 2 * n_rows), BF16), shape((rows2, 2 * n_rows), BF16),
-            shape((rows1, 2 * n_rows), BF16), shape((2 * early, n0), F32), shape((late, n0), BF16), shape((2 * late, n0), BF16),
+            shape((rows1, 2 * n_rows), BF16), shape((early, n0), BF16), shape((middle, n0), BF16), shape((last, n0), BF16), shape((2 * n_rows, n0), BF16),
             shape((1, n0), F32), shape((1, n1), F32), shape((1, n2), F32),
             shape((1, rows1), F32), shape((1, rows2), F32), shape((1, rows2), F32),
             shape((8, 128), F32), shape((8, 128), F32),
         ),
         in_specs=[hbm] * 5 + [vmem] * 3 + [hbm] * 2,
-        out_specs=[hbm] * 8 + [vmem] * 8,
+        out_specs=[hbm] * 9 + [vmem] * 8,
         scratch_shapes=[
             pltpu.VMEM((wide1, n0), BF16), pltpu.VMEM((wide2, n1), BF16), pltpu.VMEM((wide2, wide1), BF16), pltpu.VMEM((wide2, n2), BF16),
             pltpu.VMEM((n_rows, n0), BF16), pltpu.VMEM((2, n_rows, wide1), BF16), pltpu.VMEM((2, n_rows, wide2), BF16),
             pltpu.VMEM((n_rows, wide1), F32), pltpu.VMEM((n_rows, wide2), F32), pltpu.VMEM((wide2, n_rows), BF16),
             pltpu.VMEM((wide2, n_rows), BF16), pltpu.VMEM((n_rows, wide2), F32), pltpu.VMEM((n_rows, wide2), BF16), pltpu.VMEM((n_rows, wide2), BF16),
             pltpu.VMEM((2, n_rows, wide2), BF16), pltpu.VMEM((wide2, n_rows), BF16), pltpu.VMEM((n_rows // CHUNKS, wide1), BF16), pltpu.VMEM((wide1, n_rows), BF16),
-            pltpu.VMEM((n_rows, n0), BF16), pltpu.VMEM((early, n0), BF16), pltpu.VMEM((early, n0), F32),
+            pltpu.VMEM((n_rows, n0), BF16),
             pltpu.VMEM((4, 1, n0 + n1 + n2), F32), pltpu.VMEM((2, 1, n0 + n1 + n2), F32), pltpu.VMEM((4, 8, 128), F32), pltpu.VMEM((4, 8, 128), F32), pltpu.VMEM((256, 256), BF16),
             dma((5,)), dma((7,)), dma((4,)), dma((4,)), dma((PIECES,)), dma((PIECES,)), dma((PIECES,)), dma((PIECES,)), dma((9,)), dma((9,)),
             dma((CHUNKS,)), dma((CHUNKS,)), dma((CHUNKS,)), dma((CHUNKS,)), dma((CHUNKS,)), dma((CHUNKS,)),
-            dma((CHUNKS,)), dma((CHUNKS,)), dma((EARLY,)), dma((EARLY,)), dma((7,)), dma((7,)), dma((EARLY,)), dma((EARLY,)), dma((EARLY,)),
-            dma((CHUNKS - EARLY,)), dma((CHUNKS - EARLY,)), dma((CHUNKS - EARLY,)), dma((CHUNKS - EARLY,)),
+            dma((CHUNKS,)), dma((CHUNKS,)), dma((EARLY,)), dma((EARLY,)), dma((7,)), dma((7,)),
+            dma((CHUNKS,)), dma((CHUNKS,)), dma((CHUNKS,)), dma((CHUNKS,)),
         ],
         compiler_params=pltpu.CompilerParams(collective_id=0, has_side_effects=True, vmem_limit_bytes=67043328),
         name="chain",
     )(x_real, x_fake, weight0, weight1, weight2, u_left0, u_left1, u_left2, t_real.T, t_fake.T)
 
 
-def grad_kernel(x1_in, e1_in, x2_in, e2_in, x_real, x_fake, e0_in, dx_in, u0_in, u1_in, u2_in, v0_in, v1_in, v2_in, sig_in, cor_in,
-                dw0_out, dw1_out, dw2_out, dx_real, dx_fake, u0_out, u1_out, u2_out, v0_out, v1_out, v2_out, sig_out, loss_out,
-                x1, e1, x2, e2, x0, e0, dx, dw0, dw1, dw2, u0, u1, u2, v0, v1, v2, sig, cor, in_sem, x1_sem, out_sem, dw1_sem, dw0_sem):
+def grad_kernel(x1_in, e1_in, x2_in, e2_in, x_real, x_fake, e0_in, u0_in, u1_in, u2_in, v0_in, v1_in, v2_in, sig_in, cor_in,
+                dw0_out, dw1_out, dw2_out, u0_out, u1_out, u2_out, v0_out, v1_out, v2_out, sig_out, loss_out,
+                x1, e1, x2, e2, x0, e0, dw0, dw1, dw2, u0, u1, u2, v0, v1, v2, sig, cor, in_sem, x1_sem, out_sem, dw1_sem, dw0_sem):
     n_rows = x_real.shape[0]
-    early = dx.shape[0] // 2
     tiles1 = x1_sem.shape[0]
     tiles0 = dw0_sem.shape[0]
 
@@ -489,6 +468,7 @@
 
     small = [pull(src, dst, place) for place, (src, dst) in enumerate((
         (u0_in, u0), (u1_in, u1), (u2_in, u2), (v0_in, v0), (v1_in, v1), (v2_in, v2), (sig_in, sig), (cor_in, cor)))]
+
     def tile_of(size, tiles, tile_no):
         return pl.ds(tile_no * (size // tiles), size // tiles)
 
@@ -502,9 +482,8 @@
         got_x1.append(pltpu.make_async_copy(x1_in.at[:, cols], x1.at[:, cols], x1_sem.at[tile_no]))
     got_e0 = load(e0_in, e0, 8)
     got_x0 = [load(x_real, x0.at[pl.ds(0, n_rows), :], 9), load(x_fake, x0.at[pl.ds(n_rows, n_rows), :], 10)]
-    got_dx = load(dx_in, dx, 12)
     got_2 = [load(e2_in, e2, 13), load(x2_in, x2, 14)]
-    queue = [*got_x1, *got_x0, got_e0, got_dx, *got_2]
+    queue = [*got_x1, *got_x0, got_e0, *got_2]
 
     def read_on(count=1):
         for _ in range(min(count, len(queue))):
@@ -546,11 +525,6 @@
     col0, scale0 = column(u0, 0), scale(0)
     for tile_no in range(tiles0):
         gradient(e0, x0, tile_of(x0.shape[1], tiles0, tile_no), col0, v0, scale0, dw0, dw0_out, dw0_sem.at[tile_no])
-    got_dx.wait()
-    for place, dst in enumerate((dx_real, dx_fake)):
-        copy = pltpu.make_async_copy(dx.at[pl.ds(place * early, early), :], dst.at[pl.ds(0, early), :], out_sem.at[place])
-        copy.start()
-        pushes.append(copy)
     for copy in got_2:
         copy.wait()
     col2, scale2 = column(u2, 2), scale(2)
@@ -560,9 +534,9 @@
         copy.wait()
 
 
-def run_grads(x1, e1, x2, e2, x_real, x_fake, e0, dx, u0, u1, u2, v0, v1, v2, sig, cor):
+def run_grads(x1, e1, x2, e2, x_real, x_fake, e0, u0, u1, u2, v0, v1, v2, sig, cor):
     both, n1 = x1.shape
-    n_rows, n0 = x_real.shape
+    _, n0 = x_real.shape
     n2 = x2.shape[1]
     rows2 = e1.shape[0]
     rows1 = e0.shape[0]
@@ -572,20 +546,20 @@
     vmem = pl.BlockSpec(memory_space=pltpu.VMEM)
     dma = pltpu.SemaphoreType.DMA
     flops = 2 * both * (rows2 * (n1 + n2) + rows1 * n0)
-    inputs = (x1, e1, x2, e2, x_real, x_fake, e0, dx, u0, u1, u2, v0, v1, v2, sig, cor)
+    inputs = (x1, e1, x2, e2, x_real, x_fake, e0, u0, u1, u2, v0, v1, v2, sig, cor)
     inputs = tuple(pltpu.with_memory_space_constraint(array, pltpu.HBM) for array in inputs)
     return pl.pallas_call(
         grad_kernel,
         out_shape=(
-            shape((rows1, n0), F32), shape((rows2, n1), F32), shape((rows2, n2), F32), shape((n_rows, n0), F32), shape((n_rows, n0), F32),
+            shape((rows1, n0), F32), shape((rows2, n1), F32), shape((rows2, n2), F32),
             shape((rows1,), F32), shape((rows2,), F32), shape((rows2,), F32), shape((n0,), F32), shape((n1,), F32), shape((n2,), F32),
             shape((3,), F32), shape((1, 1), F32),
         ),
         in_specs=[hbm] * len(inputs),
-        out_specs=[hbm] * 5 + [vmem] * 8,
+        out_specs=[hbm] * 3 + [vmem] * 8,
         scratch_shapes=[
             pltpu.VMEM((both, n1), BF16), pltpu.VMEM((rows2, both), BF16), pltpu.VMEM((both, n2), BF16), pltpu.VMEM((rows2, both), BF16),
-            pltpu.VMEM((both, n0), BF16), pltpu.VMEM((rows1, both), BF16), pltpu.VMEM(dx.shape, F32),
+            pltpu.VMEM((both, n0), BF16), pltpu.VMEM((rows1, both), BF16),
             pltpu.VMEM((rows1, n0), F32), pltpu.VMEM((rows2, n1), F32), pltpu.VMEM((rows2, n2), F32),
             *[pltpu.VMEM(array.shape, F32) for array in (u0, u1, u2, v0, v1, v2, sig, cor)],
             dma((15,)), dma((tiles1,)), dma((4,)), dma((tiles1,)), dma((tiles0,)),
@@ -596,54 +570,59 @@
     )(*inputs)
 
 
-def finish_kernel(flip, real_in, fake_in, both, came, sig, real_out, fake_out, dx, out_sem):
-    me = lax.axis_index("model")
-    batch = me % 2
-    if flip:
-        batch = 1 - batch
-    pieces = out_sem.shape[0]
-    late = came.shape[0]
-    size = late // pieces
-    first = real_out.shape[0] - late
+def finish_kernel(plan, in_place, *refs):
+    refs = refs[2:] if in_place else refs
+    both, sig = refs[:2]
+    cames = refs[2:2 + len(plan)]
+    real_out, fake_out, dx, out_sem = refs[2 + len(plan):]
+    core = lax.axis_index("model") % 2
+    n_rows = real_out.shape[0]
     inv0 = 1.0 / sig[0:1, 0:1]
-
-    def push(dst, piece):
-        return pltpu.make_async_copy(dx.at[pl.ds(piece * size, size), :], dst.at[pl.ds(first + piece * size, size), :], out_sem.at[piece])
-
-    for piece in range(pieces):
-        rows = pl.ds(piece * size, size)
-        own = pl.ds(pl.multiple_of(batch * late + piece * size, size), size)
-        dx[rows, :] = (both[own, :].astype(F32) + came[rows, :].astype(F32)) * inv0
+    size = dx.shape[0] // out_sem.shape[0]
+    jobs = []
+    for came, (flip, first) in zip(cames, plan):
+        batch = 1 - core if flip else core
+        for begin in range(0, came.shape[0], size):
+            jobs.append((came, begin, batch, first + begin))
+
+    def push(dst, place, first):
+        return pltpu.make_async_copy(dx.at[pl.ds(place * size, size), :], dst.at[pl.ds(first, size), :], out_sem.at[place])
+
+    for place, (came, begin, batch, first) in enumerate(jobs):
+        own = pl.ds(pl.multiple_of(batch * n_rows + first, size), size)
+        dx[pl.ds(place * size, size), :] = (both[own, :].astype(F32) + came[pl.ds(begin, size), :].astype(F32)) * inv0
 
         @pl.when(batch == 0)
         def _():
-            push(real_out, piece).start()
+            push(real_out, place, first).start()
 
         @pl.when(batch == 1)
         def _():
-            push(fake_out, piece).start()
-
-    for piece in range(pieces):
-        push(real_out, piece).wait()
-
-
-def run_finish(flip, dx_real, dx_fake, both, came, sig):
-    late, n0 = came.shape
-    pieces = 4
+            push(fake_out, place, first).start()
+
+    for place, (_, _, _, first) in enumerate(jobs):
+        push(real_out, place, first).wait()
+
+
+def run_finish(old, both, sig, parts):
+    cames = [came for came, _, _ in parts]
+    rows = sum(came.shape[0] for came in cames)
+    n0 = both.shape[1]
+    size = 64
     hbm = pl.BlockSpec(memory_space=pltpu.HBM)
     vmem = pl.BlockSpec(memory_space=pltpu.VMEM)
-    shape = jax.ShapeDtypeStruct(dx_real.shape, F32)
+    shape = jax.ShapeDtypeStruct((both.shape[0] // 2, n0), F32)
     return pl.pallas_call(
-        functools.partial(finish_kernel, flip),
+        functools.partial(finish_kernel, tuple((flip, first) for _, flip, first in parts), bool(old)),
         out_shape=(shape, shape),
-        in_specs=[hbm] * 2 + [vmem] * 3,
+        in_specs=[hbm] * len(old) + [vmem] * (2 + len(cames)),
         out_specs=[hbm] * 2,
-        scratch_shapes=[pltpu.VMEM((late, n0), F32), pltpu.SemaphoreType.DMA((pieces,))],
-        input_output_aliases={0: 0, 1: 1},
+        scratch_shapes=[pltpu.VMEM((rows, n0), F32), pltpu.SemaphoreType.DMA((rows // size,))],
+        input_output_aliases={0: 0, 1: 1} if old else {},
         compiler_params=pltpu.CompilerParams(vmem_limit_bytes=16 * 1024 * 1024),
-        cost_estimate=pl.CostEstimate(flops=4 * late * n0, bytes_accessed=8 * late * n0, transcendentals=0),
+        cost_estimate=pl.CostEstimate(flops=4 * rows * n0, bytes_accessed=8 * rows * n0, transcendentals=0),
         name="finish",
-    )(dx_real, dx_fake, both, came, sig)
+    )(*old, both, sig, *cames)
 
 
 def swap(values, bits):
@@ -658,13 +637,22 @@
     group_spec = P("rep")
 
     def local_step(x_real, x_fake, weight0, weight1, weight2, u_left0, u_left1, u_left2, t_real, t_fake):
-        x1, x2, e2, e1, e0, dx, sums, both, v0, v1, v2, u0, u1, u2, sig, cor = run_chain(x_real, x_fake, weight0, weight1, weight2, u_left0, u_left1, u_left2, t_real, t_fake)
-        came = swap(sums, 2)
-        dw0, dw1, dw2, dx_real, dx_fake, u0, u1, u2, v0, v1, v2, sigmas, loss = run_grads(x1, e1, x2, e2, x_real, x_fake, e0, dx, u0, u1, u2, v0, v1, v2, sig, cor)
-        came, sigmas = lax.optimization_barrier((came, sigmas))
-        came_mate = swap(came, 1)
-        dx_real, dx_fake = run_finish(False, dx_real, dx_fake, both, came, sig)
-        dx_real, dx_fake = run_finish(True, dx_real, dx_fake, both, came_mate, sig)
+        x1, x2, e2, e1, e0, first, middle, last, both, v0, v1, v2, u0, u1, u2, sig, cor = run_chain(x_real, x_fake, weight0, weight1, weight2, u_left0, u_left1, u_left2, t_real, t_fake)
+        row1 = first.shape[0]
+        row2 = row1 + middle.shape[0]
+        middle = swap(middle, 2)
+        last = swap(last, 2)
+        first_mate = swap(first, 1)
+        grads = run_grads(x1, e1, x2, e2, x_real, x_fake, e0, u0, u1, u2, v0, v1, v2, sig, cor)
+        dw0, dw1, dw2, u0, u1, u2, v0, v1, v2, sigmas, loss = grads
+        middle, sigmas = lax.optimization_barrier((middle, sigmas))
+        middle_mate = swap(middle, 1)
+        dx = run_finish((), both, sig, ((first, False, 0), (first_mate, True, 0), (middle, False, row1)))
+        dx = run_finish(dx, both, sig, ((middle_mate, True, row1),))
+        last, *dx = lax.optimization_barrier((last, *dx))
+        last_mate = swap(last, 1)
+        dx = run_finish(dx, both, sig, ((last, False, row2),))
+        dx_real, dx_fake = run_finish(dx, both, sig, ((last_mate, True, row2),))
         return (loss[0], dx_real, dx_fake, dw0, dw1, dw2, u0, u1, u2, v0, v1, v2, sigmas)
 
     return jax.shard_map(local_step, mesh=mesh, in_specs=(rows_spec, rows_spec, weight_spec, weight_spec, weight_spec, left_spec, left_spec, left_spec, target_spec, target_spec), out_specs=(group_spec, rows_spec, rows_spec, weight_spec, weight_spec, weight_spec, left_spec, left_spec, left_spec, group_spec, group_spec, group_spec, group_spec), check_vma=False)

time: 180 us -> 184 us (1.022)
  Pallas kernels: 171 us -> 174 us
    pallas_call x2 -> x4, Pallas kernels: 2.85 us -> 4.67 us  [run_finish(): pl.pallas_call(functools.partial(finish_kernel, tuple(((flip, first) for...]
    ppermute x2 -> x5, waiting for transfers between devices: 5.65 us -> 6.64 us  [swap(): lax.ppermute(values, 'model', [(dev, dev ^ bits) for dev in range(4)])]
  transfers between devices with their start and end apart: 2 -> 5, of which waited for: 2 -> 3; matrix products, arithmetic and copies ran while one was open for 0% -> 0% of each run, Pallas kernels for 11% -> 12%
where the time goes in v10:
time: 184 us
  Pallas kernels  174 us (95%)
  waiting for transfers between devices  6.64 us (4%)
  starting transfers between devices  2.57 us (1%)
    pallas_call x1, Pallas kernels, run_chain(): pl.pallas_call(chain_kernel, out_shape=(shape((2 * n_rows, n1), BF16), sh...  151 us
    pallas_call x1, Pallas kernels, run_grads(): pl.pallas_call(grad_kernel, out_shape=(shape((rows1, n0), F32), shape((ro...  18 us
    ppermute x5, waiting for transfers between devices, swap(): lax.ppermute(values, 'model', [(dev, dev ^ bits) for dev in range(4)])  6.64 us
    pallas_call x4, Pallas kernels, run_finish(): pl.pallas_call(functools.partial(finish_kernel, tuple(((flip, first) for...  4.67 us
  transfers between devices with their start and end apart: 5, of which 3 were waited for; matrix products, arithmetic and copies ran while one was open for 0% of the time, Pallas kernels for 12%

profile of v10, /device:TPU:0, one launch (start us, length us, event | category | flops | bytes accessed | tf_op | source)
XLA Modules:
  0.0 183.7 jit_solution(13036571819960397296)
XLA Ops:
  0.6 150.9 %chain.1 = (bf16[1024,5120]{1,0:T(8,128)(2,1)}, bf16[1024,1280]{1,0:T(8,128)(2,1)}, bf16[320,1024]{1,0:T(8,128)(2,1)}, bf16[320,1024]{1,0:T(8,128)(2,1)}, bf16[1...) custom-call(bf16[512,1280]{1,0:T(8,128)(2,1)} %x_real.3, ...), custom_call_target="tpu_custom_call" | custom-call | tf_op jit(solution)/shard_map/chain/pallas_call | solution.py:428
  151.6 1.1 collective-permute-start.2
  152.7 0.0 copy-start.1
  152.7 0.0 copy-start.3
  152.7 0.0 copy-start
  152.7 0.0 copy-start.2
  152.7 18.0 %grads.1 = (f32[1280,1280]{1,0:T(8,128)}, f32[320,5120]{1,0:T(8,128)}, f32[320,1280]{1,0:T(8,128)}, f32[1280]{0:T(1024)}, f32[320]{0:T(512)}, /*index=5*/f32[320...) custom-call(bf16[1024,5120]{1,0:T(8,128)(2,1)} %get-tuple-element.54.x1_in, ...), custom_call_target="tpu_custom_call" | custom-call | flops 7549747200 | bytes 47185920 | tf_op jit(solution)/shard_map/grads/pallas_call | solution.py:551
  170.7 0.0 collective-permute-done.2.refs_4_
  170.7 0.1 collective-permute-start.3
  170.8 0.0 copy-done.1
  170.8 0.4 collective-permute-start.1
  171.3 0.0 copy-done.3
  171.3 0.9 collective-permute-start
  172.2 1.1 collective-permute-done.1.refs_3_
  173.3 0.0 copy-done
  173.3 0.0 copy-done.2
  173.3 1.6 finish.4
  175.0 0.0 collective-permute-done.3.refs_4_
  175.0 1.2 finish.5
  176.1 4.8 %collective-permute-done.refs_4_ = bf16[128,1280]{1,0:T(8,128)(2,1)S(1)} collective-permute-done((bf16[128,1280]{1,0:T(8,128)(2,1)S(1)}, bf16[128,1280]{1,0:T(8,128)(2,1)S(1)}, u32[]{:S(2)}, u32[]{:S(2)}) %collective-permute-start) | collective-permute-done | bytes 327712 | tf_op jit(solution)/shard_map/ppermute | solution.py:629
  181.0 0.0 collective-permute-start.4
  181.0 0.9 finish.6
  181.9 0.7 collective-permute-done.4.refs_4_
  182.6 0.9 finish.7
Async XLA Ops:
  151.6 19.1 %collective-permute-start.2 = (bf16[256,1280]{1,0:T(8,128)(2,1)}, bf16[256,1280]{1,0:T(8,128)(2,1)S(1)}, u32[]{:S(2)}, u32[]{:S(2)}) collective-permute-start(bf16[256,1280]{1,0:T(8,128)(2,1)} %get-tuple-element.71), channel_id=1, source_target_pairs={{0,2},{1,3},{2,0},{3,1},{4,6},{5,7},{6,4},{7,5}} | collective-permute-start | bytes 1966088 | tf_op jit(solution)/shard_map/ppermute | solution.py:629
  152.7 18.1 %copy-start.1 = (bf16[128,1280]{1,0:T(8,128)(2,1)S(1)}, bf16[128,1280]{1,0:T(8,128)(2,1)}, u32[]{:S(2)}) copy-start(bf16[128,1280]{1,0:T(8,128)(2,1)} %get-tuple-element.70.refs_2_) | copy-start | bytes 983044
  152.7 18.6 %copy-start.3 = (bf16[128,1280]{1,0:T(8,128)(2,1)S(1)}, bf16[128,1280]{1,0:T(8,128)(2,1)}, u32[]{:S(2)}) copy-start(bf16[128,1280]{1,0:T(8,128)(2,1)} %get-tuple-element.68) | copy-start | bytes 983044
  152.7 20.6 %copy-start = (bf16[1024,1280]{1,0:T(8,128)(2,1)S(1)}, bf16[1024,1280]{1,0:T(8,128)(2,1)}, u32[]{:S(2)}) copy-start(bf16[1024,1280]{1,0:T(8,128)(2,1)} %get-tuple-element.69.refs_0_.refs_2_) | copy-start | bytes 7864324
  152.7 20.6 %copy-start.2 = (f32[8,128]{1,0:T(8,128)S(1)}, f32[8,128]{1,0:T(8,128)}, u32[]{:S(2)}) copy-start(f32[8,128]{1,0:T(8,128)} %get-tuple-element.65.sig_in.refs_1_.refs_3_) | copy-start | bytes 12292
  170.7 4.2 %collective-permute-start.3 = (bf16[256,1280]{1,0:T(8,128)(2,1)S(1)}, bf16[256,1280]{1,0:T(8,128)(2,1)S(1)}, u32[]{:S(2)}, u32[]{:S(2)}) collective-permute-start(bf16[256,1280]{1,0:T(8,128)(2,1)S(1)} %collective-permute-done.2.refs_4_), channel_id=1, source_target_pairs={{0,1},{1,0},{2,3},{3,2},{4,5},{5,4},{6,7},{7,6}} | collective-permute-start | bytes 1966088 | tf_op jit(solution)/shard_map/ppermute | solution.py:629
  170.8 2.5 %collective-permute-start.1 = (bf16[128,1280]{1,0:T(8,128)(2,1)S(1)}, bf16[128,1280]{1,0:T(8,128)(2,1)S(1)}, u32[]{:S(2)}, u32[]{:S(2)}) collective-permute-start(bf16[128,1280]{1,0:T(8,128)(2,1)S(1)} %copy-done.1), channel_id=1, source_target_pairs={{0,1},{1,0},{2,3},{3,2},{4,5},{5,4},{6,7},{7,6}} | collective-permute-start | bytes 983048 | tf_op jit(solution)/shard_map/ppermute | solution.py:629
  171.3 9.7 %collective-permute-start = (bf16[128,1280]{1,0:T(8,128)(2,1)S(1)}, bf16[128,1280]{1,0:T(8,128)(2,1)S(1)}, u32[]{:S(2)}, u32[]{:S(2)}) collective-permute-start(bf16[128,1280]{1,0:T(8,128)(2,1)S(1)} %copy-done.3), channel_id=1, source_target_pairs={{0,2},{1,3},{2,0},{3,1},{4,6},{5,7},{6,4},{7,5}} | collective-permute-start | bytes 983048 | tf_op jit(solution)/shard_map/ppermute | solution.py:629
  181.0 1.6 collective-permute-start.4

commit v11 on v10

--- a/solution.py
+++ b/solution.py
@@ -50,7 +50,7 @@
                  w0, w1, w1x, w2, x0, x1, x2, y0, y1, tt, e2_t, h2_own, h2_put, h2_got, e1, e1_t, e0, e0_t, h0_put,
                  p_buf, p_sum, n_buf, c_buf,
                  eye, load_sem, put_sem, w_send, w_recv, w1x_send, w1x_recv, fwd_send, fwd_recv, small_send, small_recv,
-                 x1_send, x1_recv, x2_send, x2_recv, h2_send, h2_recv, e1_send, e1_recv, h0_send, h0_recv, out_send, out_recv, sum_sem, both_sem, both_send, both_recv):
+                 x1_send, x1_recv, x2_send, x2_recv, h2_send, h2_recv, e1_send, e1_recv, h0_send, h0_recv, out_send, out_recv, sum_sem, both_sem, both_send, both_recv, e0_sem, e0_send, e0_recv):
     me = lax.axis_index("model")
     chip = me // 2
     core = me % 2
@@ -333,7 +333,7 @@
             cols = part(tile_no, wide2)
             own_cols = pl.ds(pl.multiple_of(chip * wide1 + tile_no * wide2, 128), wide2)
             h_val = dot_n(e1[chip, rows, :], w1[:, own_cols]) + dot_n(e1[other, rows, :], w1x[:, cols])
-            y_val = y0[rows, cols]
+            y_val = y0[rows, cols] * inv0
             e_val = h_val * (inv1 * leaky_slope(y_val))
             e0[:, cols] = e_val.astype(BF16)
             return corr + fold(e_val * y_val)
@@ -350,6 +350,16 @@
             return carry
 
         lax.fori_loop(0, wide1 // wide2, tile, 0)
+        for copy in e0_copies(chunk_no):
+            copy.start()
+
+    def e0_copies(chunk_no):
+        rows = part(chunk_no, step)
+        dst = e0_out.at[:, pl.ds(pl.multiple_of(core * n_rows + chunk_no * step, step), step)]
+        return (
+            pltpu.make_async_copy(e0_t.at[part(core, rows1), rows], dst, e0_sem.at[chunk_no]),
+            send(e0_t.at[part(1 - core, rows1), rows], dst, e0_send.at[chunk_no], e0_recv.at[chunk_no], mate),
+        )
 
     def early_chunk(chunk_no, corr0):
         corr0 = back0(chunk_no, corr0)
@@ -369,10 +379,7 @@
     corr0 = lax.fori_loop(0, EARLY, early_chunk, corr0)
     corr0 = lax.fori_loop(EARLY, EARLY + MIDDLE, functools.partial(late_chunk, mid_out, EARLY), corr0)
     corr0 = lax.fori_loop(EARLY + MIDDLE, CHUNKS, functools.partial(late_chunk, last_out, EARLY + MIDDLE), corr0)
-    e0_pair = halves(e0_t, e0_out, rows1, 6)
-    for copy in e0_pair:
-        copy.start()
-    c_buf[me] = pack([total(corr0) * inv0, total(corr1), total(corr2), total(loss)])
+    c_buf[me] = pack([total(corr) for corr in (corr0, corr1, corr2, loss)])
     c_copies = spread(c_buf, 6)
     for copy in c_copies:
         copy.start()
@@ -387,7 +394,7 @@
     for piece_no in range(PIECES):
         w1x_copy(piece_no).wait_send()
         w1x_forward(piece_no).wait_send()
-    for pair in (x1_near, x1_far, *lesser, e0_pair):
+    for pair in (x1_near, x1_far, *lesser):
         for copy in pair:
             copy.wait()
 
@@ -408,7 +415,7 @@
             late_copy(mid_out, EARLY, chunk_no).wait()
         else:
             late_copy(last_out, EARLY + MIDDLE, chunk_no).wait()
-        for copy in both_copies(chunk_no):
+        for copy in (*both_copies(chunk_no), *e0_copies(chunk_no)):
             copy.wait()
 
 
@@ -447,7 +454,7 @@
             dma((5,)), dma((7,)), dma((4,)), dma((4,)), dma((PIECES,)), dma((PIECES,)), dma((PIECES,)), dma((PIECES,)), dma((9,)), dma((9,)),
             dma((CHUNKS,)), dma((CHUNKS,)), dma((CHUNKS,)), dma((CHUNKS,)), dma((CHUNKS,)), dma((CHUNKS,)),
             dma((CHUNKS,)), dma((CHUNKS,)), dma((EARLY,)), dma((EARLY,)), dma((7,)), dma((7,)),
-            dma((CHUNKS,)), dma((CHUNKS,)), dma((CHUNKS,)), dma((CHUNKS,)),
+            dma((CHUNKS,)), dma((CHUNKS,)), dma((CHUNKS,)), dma((CHUNKS,)), dma((CHUNKS,)), dma((CHUNKS,)), dma((CHUNKS,)),
         ],
         compiler_params=pltpu.CompilerParams(collective_id=0, has_side_effects=True, vmem_limit_bytes=67043328),
         name="chain",

time: 184 us -> 183 us (level)
  no operation moved by 1% of the time
where the time goes in v11:
time: 183 us
  Pallas kernels  174 us (95%)
  waiting for transfers between devices  5.77 us (3%)
  starting transfers between devices  2.53 us (1%)
    pallas_call x1, Pallas kernels, run_chain(): pl.pallas_call(chain_kernel, out_shape=(shape((2 * n_rows, n1), BF16), sh...  151 us
    pallas_call x1, Pallas kernels, run_grads(): pl.pallas_call(grad_kernel, out_shape=(shape((rows1, n0), F32), shape((ro...  18 us
    ppermute x5, waiting for transfers between devices, swap(): lax.ppermute(values, 'model', [(dev, dev ^ bits) for dev in range(4)])  5.77 us
    pallas_call x4, Pallas kernels, run_finish(): pl.pallas_call(functools.partial(finish_kernel, tuple(((flip, first) for...  4.67 us
  transfers between devices with their start and end apart: 5, of which 3 were waited for; matrix products, arithmetic and copies ran while one was open for 0% of the time, Pallas kernels for 12%

profile of v11, /device:TPU:0, one launch (start us, length us, event | category | flops | bytes accessed | tf_op | source)
XLA Modules:
  0.0 182.9 jit_solution(12865257895315624739)
XLA Ops:
  0.6 151.0 %chain.1 = (bf16[1024,5120]{1,0:T(8,128)(2,1)}, bf16[1024,1280]{1,0:T(8,128)(2,1)}, bf16[320,1024]{1,0:T(8,128)(2,1)}, bf16[320,1024]{1,0:T(8,128)(2,1)}, bf16[1...) custom-call(bf16[512,1280]{1,0:T(8,128)(2,1)} %x_real.3, ...), custom_call_target="tpu_custom_call" | custom-call | tf_op jit(solution)/shard_map/chain/pallas_call | solution.py:435
  151.6 0.0 collective-permute-start.2
  151.7 0.0 copy-start.1
  151.7 0.0 copy-start.3
  151.7 0.0 copy-start
  151.7 0.0 copy-start.2
  151.7 18.0 %grads.1 = (f32[1280,1280]{1,0:T(8,128)}, f32[320,5120]{1,0:T(8,128)}, f32[320,1280]{1,0:T(8,128)}, f32[1280]{0:T(1024)}, f32[320]{0:T(512)}, /*index=5*/f32[320...) custom-call(bf16[1024,5120]{1,0:T(8,128)(2,1)} %get-tuple-element.54.x1_in, ...), custom_call_target="tpu_custom_call" | custom-call | flops 7549747200 | bytes 47185920 | tf_op jit(solution)/shard_map/grads/pallas_call | solution.py:558
  169.7 0.0 collective-permute-done.2.refs_4_
  169.7 0.1 collective-permute-start.3
  169.8 0.0 copy-done.1
  169.9 0.4 collective-permute-start.1
  170.3 0.0 copy-done.3
  170.3 2.0 %collective-permute-start = (bf16[128,1280]{1,0:T(8,128)(2,1)S(1)}, bf16[128,1280]{1,0:T(8,128)(2,1)S(1)}, u32[]{:S(2)}, u32[]{:S(2)}) collective-permute-start(bf16[128,1280]{1,0:T(8,128)(2,1)S(1)} %copy-done.3), channel_id=1, source_target_pairs={{0,2},{1,3},{2,0},{3,1},{4,6},{5,7},{6,4},{7,5}} | collective-permute-start | bytes 983048 | tf_op jit(solution)/shard_map/ppermute | solution.py:636
  172.2 0.1 collective-permute-done.1.refs_3_
  172.3 0.0 copy-done
  172.3 0.0 copy-done.2
  172.3 1.6 finish.4
  174.0 0.0 collective-permute-done.3.refs_4_
  174.0 1.2 finish.5
  175.2 5.0 %collective-permute-done.refs_4_ = bf16[128,1280]{1,0:T(8,128)(2,1)S(1)} collective-permute-done((bf16[128,1280]{1,0:T(8,128)(2,1)S(1)}, bf16[128,1280]{1,0:T(8,128)(2,1)S(1)}, u32[]{:S(2)}, u32[]{:S(2)}) %collective-permute-start) | collective-permute-done | bytes 327712 | tf_op jit(solution)/shard_map/ppermute | solution.py:636
  180.2 0.0 collective-permute-start.4
  180.2 0.9 finish.6
  181.1 0.7 collective-permute-done.4.refs_4_
  181.8 0.9 finish.7
Async XLA Ops:
  151.6 18.1 %collective-permute-start.2 = (bf16[256,1280]{1,0:T(8,128)(2,1)}, bf16[256,1280]{1,0:T(8,128)(2,1)S(1)}, u32[]{:S(2)}, u32[]{:S(2)}) collective-permute-start(bf16[256,1280]{1,0:T(8,128)(2,1)} %get-tuple-element.71), channel_id=1, source_target_pairs={{0,2},{1,3},{2,0},{3,1},{4,6},{5,7},{6,4},{7,5}} | collective-permute-start | bytes 1966088 | tf_op jit(solution)/shard_map/ppermute | solution.py:636
  151.7 18.2 %copy-start.1 = (bf16[128,1280]{1,0:T(8,128)(2,1)S(1)}, bf16[128,1280]{1,0:T(8,128)(2,1)}, u32[]{:S(2)}) copy-start(bf16[128,1280]{1,0:T(8,128)(2,1)} %get-tuple-element.70.refs_2_) | copy-start | bytes 983044
  151.7 18.6 %copy-start.3 = (bf16[128,1280]{1,0:T(8,128)(2,1)S(1)}, bf16[128,1280]{1,0:T(8,128)(2,1)}, u32[]{:S(2)}) copy-start(bf16[128,1280]{1,0:T(8,128)(2,1)} %get-tuple-element.68) | copy-start | bytes 983044
  151.7 20.6 %copy-start = (bf16[1024,1280]{1,0:T(8,128)(2,1)S(1)}, bf16[1024,1280]{1,0:T(8,128)(2,1)}, u32[]{:S(2)}) copy-start(bf16[1024,1280]{1,0:T(8,128)(2,1)} %get-tuple-element.69.refs_0_.refs_2_) | copy-start | bytes 7864324
  151.7 20.6 %copy-start.2 = (f32[8,128]{1,0:T(8,128)S(1)}, f32[8,128]{1,0:T(8,128)}, u32[]{:S(2)}) copy-start(f32[8,128]{1,0:T(8,128)} %get-tuple-element.65.sig_in.refs_1_.refs_3_) | copy-start | bytes 12292
  169.7 4.2 %collective-permute-start.3 = (bf16[256,1280]{1,0:T(8,128)(2,1)S(1)}, bf16[256,1280]{1,0:T(8,128)(2,1)S(1)}, u32[]{:S(2)}, u32[]{:S(2)}) collective-permute-start(bf16[256,1280]{1,0:T(8,128)(2,1)S(1)} %collective-permute-done.2.refs_4_), channel_id=1, source_target_pairs={{0,1},{1,0},{2,3},{3,2},{4,5},{5,4},{6,7},{7,6}} | collective-permute-start | bytes 1966088 | tf_op jit(solution)/shard_map/ppermute | solution.py:636
  169.9 2.5 %collective-permute-start.1 = (bf16[128,1280]{1,0:T(8,128)(2,1)S(1)}, bf16[128,1280]{1,0:T(8,128)(2,1)S(1)}, u32[]{:S(2)}, u32[]{:S(2)}) collective-permute-start(bf16[128,1280]{1,0:T(8,128)(2,1)S(1)} %copy-done.1), channel_id=1, source_target_pairs={{0,1},{1,0},{2,3},{3,2},{4,5},{5,4},{6,7},{7,6}} | collective-permute-start | bytes 983048 | tf_op jit(solution)/shard_map/ppermute | solution.py:636
  170.3 9.9 %collective-permute-start = (bf16[128,1280]{1,0:T(8,128)(2,1)S(1)}, bf16[128,1280]{1,0:T(8,128)(2,1)S(1)}, u32[]{:S(2)}, u32[]{:S(2)}) collective-permute-start(bf16[128,1280]{1,0:T(8,128)(2,1)S(1)} %copy-done.3), channel_id=1, source_target_pairs={{0,2},{1,3},{2,0},{3,1},{4,6},{5,7},{6,4},{7,5}} | collective-permute-start | bytes 983048 | tf_op jit(solution)/shard_map/ppermute | solution.py:636
  180.2 1.6 collective-permute-start.4

commit v12 on v11

--- a/solution.py
+++ b/solution.py
@@ -45,11 +45,11 @@
     return jnp.sum(jnp.sum(values, axis=1, keepdims=True), axis=0, keepdims=True)
 
 
-def chain_kernel(x_real, x_fake, w0_in, w1_in, w2_in, u0_in, u1_in, u2_in, t_real, t_fake,
-                 x1_out, x2_out, e2_out, e1_out, e0_out, got_out, mid_out, last_out, both_out, v0_out, v1_out, v2_out, u0_out, u1_out, u2_out, sig_out, cor_out,
+def chain_kernel(x_real, x_fake, w0_in, w1_in, w2_in, u0_hbm, u1_hbm, u2_hbm, t_real, t_fake,
+                 x1_out, x2_out, e2_out, e1_out, e0_out, got_out, mid_out, last_out, both_out, v0_hbm, v1_hbm, v2_hbm, u0_new, u1_new, u2_new, sig_hbm, cor_hbm,
                  w0, w1, w1x, w2, x0, x1, x2, y0, y1, tt, e2_t, h2_own, h2_put, h2_got, e1, e1_t, e0, e0_t, h0_put,
                  p_buf, p_sum, n_buf, c_buf,
-                 eye, load_sem, put_sem, w_send, w_recv, w1x_send, w1x_recv, fwd_send, fwd_recv, small_send, small_recv,
+                 eye, u0_in, u1_in, u2_in, v0_out, v1_out, v2_out, u0_out, u1_out, u2_out, sig_out, small_sem, load_sem, put_sem, w_send, w_recv, w1x_send, w1x_recv, fwd_send, fwd_recv, small_send, small_recv,
                  x1_send, x1_recv, x2_send, x2_recv, h2_send, h2_recv, e1_send, e1_recv, h0_send, h0_recv, out_send, out_recv, sum_sem, both_sem, both_send, both_recv, e0_sem, e0_send, e0_recv):
     me = lax.axis_index("model")
     chip = me // 2
@@ -104,6 +104,9 @@
         copy.start()
 
     w1x_copy(1).start()
+    u_loads = [pltpu.make_async_copy(src, dst, small_sem.at[place]) for place, (src, dst) in enumerate(((u0_hbm, u0_in), (u1_hbm, u1_in), (u2_hbm, u2_in)))]
+    for copy in u_loads:
+        copy.start()
 
     def mine(x_in, t_own):
         return (
@@ -133,6 +136,8 @@
             block = dot_t(eye[0:size, 0:size], values[:, begin:begin + size])
             dst[pl.ds(pl.multiple_of(first + begin, 128), size), rows] = block.astype(BF16)
 
+    for copy in u_loads:
+        copy.wait()
     u_rows = [row(u0_in[...]), row(u1_in[...]), row(u2_in[...])]
     loads[0].wait()
     p_buf[me, :, pl.ds(0, n0)] = dot_n(u_rows[0], w0[own1, :])[0:1]
@@ -212,6 +217,10 @@
     u0_out[...] = u0_out[...] / sig0
     u1_out[...] = u1_out[...] / sig1
     u2_out[...] = u2_out[...] / sig2
+    results = [pltpu.make_async_copy(src, dst, small_sem.at[3 + place]) for place, (src, dst) in enumerate((
+        (v0_out, v0_hbm), (v1_out, v1_hbm), (v2_out, v2_hbm), (u0_out, u0_new), (u1_out, u1_new), (u2_out, u2_new), (sig_out, sig_hbm)))]
+    for copy in results:
+        copy.start()
 
     def chunk_copy(buf, slot, chunk_no, send_sem, recv_sem):
         rows = buf.at[slot, part(chunk_no, step), :]
@@ -380,13 +389,15 @@
     corr0 = lax.fori_loop(EARLY, EARLY + MIDDLE, functools.partial(late_chunk, mid_out, EARLY), corr0)
     corr0 = lax.fori_loop(EARLY + MIDDLE, CHUNKS, functools.partial(late_chunk, last_out, EARLY + MIDDLE), corr0)
     c_buf[me] = pack([total(corr) for corr in (corr0, corr1, corr2, loss)])
-    c_copies = spread(c_buf, 6)
+    c_copies = [send(c_buf.at[me], cor_hbm.at[me], small_send.at[6 + which], small_recv.at[6 + which], device) for which, device in enumerate((mate, far, diag))]
+    c_copies.append(pltpu.make_async_copy(c_buf.at[me], cor_hbm.at[me], small_sem.at[10]))
     for copy in c_copies:
         copy.start()
 
     for copy in c_copies:
         copy.wait()
-    cor_out[...] = c_buf[0] + c_buf[1] + c_buf[2] + c_buf[3]
+    for copy in results:
+        copy.wait()
 
     for copy in gives:
         copy.wait_send()
@@ -439,10 +450,10 @@
             shape((rows1, 2 * n_rows), BF16), shape((early, n0), BF16), shape((middle, n0), BF16), shape((last, n0), BF16), shape((2 * n_rows, n0), BF16),
             shape((1, n0), F32), shape((1, n1), F32), shape((1, n2), F32),
             shape((1, rows1), F32), shape((1, rows2), F32), shape((1, rows2), F32),
-            shape((8, 128), F32), shape((8, 128), F32),
+            shape((8, 128), F32), shape((4, 8, 128), F32),
         ),
-        in_specs=[hbm] * 5 + [vmem] * 3 + [hbm] * 2,
-        out_specs=[hbm] * 9 + [vmem] * 8,
+        in_specs=[hbm] * 10,
+        out_specs=[hbm] * 17,
         scratch_shapes=[
             pltpu.VMEM((wide1, n0), BF16), pltpu.VMEM((wide2, n1), BF16), pltpu.VMEM((wide2, wide1), BF16), pltpu.VMEM((wide2, n2), BF16),
             pltpu.VMEM((n_rows, n0), BF16), pltpu.VMEM((2, n_rows, wide1), BF16), pltpu.VMEM((2, n_rows, wide2), BF16),
@@ -451,6 +462,8 @@
             pltpu.VMEM((2, n_rows, wide2), BF16), pltpu.VMEM((wide2, n_rows), BF16), pltpu.VMEM((n_rows // CHUNKS, wide1), BF16), pltpu.VMEM((wide1, n_rows), BF16),
             pltpu.VMEM((n_rows, n0), BF16),
             pltpu.VMEM((4, 1, n0 + n1 + n2), F32), pltpu.VMEM((2, 1, n0 + n1 + n2), F32), pltpu.VMEM((4, 8, 128), F32), pltpu.VMEM((4, 8, 128), F32), pltpu.VMEM((256, 256), BF16),
+            *[pltpu.VMEM(array.shape, F32) for array in (u_left0, u_left1, u_left2)],
+            *[pltpu.VMEM((1, size), F32) for size in (n0, n1, n2, rows1, rows2, rows2)], pltpu.VMEM((8, 128), F32), dma((11,)),
             dma((5,)), dma((7,)), dma((4,)), dma((4,)), dma((PIECES,)), dma((PIECES,)), dma((PIECES,)), dma((PIECES,)), dma((9,)), dma((9,)),
             dma((CHUNKS,)), dma((CHUNKS,)), dma((CHUNKS,)), dma((CHUNKS,)), dma((CHUNKS,)), dma((CHUNKS,)),
             dma((CHUNKS,)), dma((CHUNKS,)), dma((EARLY,)), dma((EARLY,)), dma((7,)), dma((7,)),
@@ -463,7 +476,7 @@
 
 def grad_kernel(x1_in, e1_in, x2_in, e2_in, x_real, x_fake, e0_in, u0_in, u1_in, u2_in, v0_in, v1_in, v2_in, sig_in, cor_in,
                 dw0_out, dw1_out, dw2_out, u0_out, u1_out, u2_out, v0_out, v1_out, v2_out, sig_out, loss_out,
-                x1, e1, x2, e2, x0, e0, dw0, dw1, dw2, u0, u1, u2, v0, v1, v2, sig, cor, in_sem, x1_sem, out_sem, dw1_sem, dw0_sem):
+                x1, e1, x2, e2, x0, e0, dw0, dw1, dw2, u0, u1, u2, v0, v1, v2, sig, cor_all, in_sem, x1_sem, out_sem, dw1_sem, dw0_sem):
     n_rows = x_real.shape[0]
     tiles1 = x1_sem.shape[0]
     tiles0 = dw0_sem.shape[0]
@@ -474,7 +487,7 @@
         return copy
 
     small = [pull(src, dst, place) for place, (src, dst) in enumerate((
-        (u0_in, u0), (u1_in, u1), (u2_in, u2), (v0_in, v0), (v1_in, v1), (v2_in, v2), (sig_in, sig), (cor_in, cor)))]
+        (u0_in, u0), (u1_in, u1), (u2_in, u2), (v0_in, v0), (v1_in, v1), (v2_in, v2), (sig_in, sig), (cor_in, cor_all)))]
 
     def tile_of(size, tiles, tile_no):
         return pl.ds(tile_no * (size // tiles), size // tiles)
@@ -500,6 +513,7 @@
 
     for copy in small:
         copy.wait()
+    cor = cor_all[0] + cor_all[1] + cor_all[2] + cor_all[3]
     for src, dst in ((u0, u0_out), (u1, u1_out), (u2, u2_out), (v0, v0_out), (v1, v1_out), (v2, v2_out)):
         dst[...] = src[...].reshape(dst.shape)
     sig_out[...] = sig[0:1, 0:3].reshape(3)

time: 183 us -> 182 us (level)
  no operation moved by 1% of the time
where the time goes in v12:
time: 182 us
  Pallas kernels  173 us (95%)
  waiting for transfers between devices  5.77 us (3%)
  starting transfers between devices  2.56 us (1%)
    pallas_call x1, Pallas kernels, run_chain(): pl.pallas_call(chain_kernel, out_shape=(shape((2 * n_rows, n1), BF16), sh...  150 us
    pallas_call x1, Pallas kernels, run_grads(): pl.pallas_call(grad_kernel, out_shape=(shape((rows1, n0), F32), shape((ro...  18 us
    ppermute x5, waiting for transfers between devices, swap(): lax.ppermute(values, 'model', [(dev, dev ^ bits) for dev in range(4)])  5.77 us
    pallas_call x4, Pallas kernels, run_finish(): pl.pallas_call(functools.partial(finish_kernel, tuple(((flip, first) for...  4.67 us
  transfers between devices with their start and end apart: 5, of which 3 were waited for; matrix products, arithmetic and copies ran while one was open for 0% of the time, Pallas kernels for 12%

profile of v12, /device:TPU:0, one launch (start us, length us, event | category | flops | bytes accessed | tf_op | source)
XLA Modules:
  0.0 181.8 jit_solution(434312556657214627)
XLA Ops:
  0.6 149.9 %chain.1 = (bf16[1024,5120]{1,0:T(8,128)(2,1)}, bf16[1024,1280]{1,0:T(8,128)(2,1)}, bf16[320,1024]{1,0:T(8,128)(2,1)}, bf16[320,1024]{1,0:T(8,128)(2,1)}, bf16[1...) custom-call(bf16[512,1280]{1,0:T(8,128)(2,1)} %x_real.3, ...), custom_call_target="tpu_custom_call" | custom-call | tf_op jit(solution)/shard_map/chain/pallas_call | solution.py:446
  150.5 0.0 collective-permute-start.2
  150.6 0.0 copy-start.1
  150.6 0.0 copy-start.3
  150.6 0.0 copy-start
  150.6 0.0 copy-start.2
  150.6 18.0 %grads.1 = (f32[1280,1280]{1,0:T(8,128)}, f32[320,5120]{1,0:T(8,128)}, f32[320,1280]{1,0:T(8,128)}, f32[1280]{0:T(1024)}, f32[320]{0:T(512)}, /*index=5*/f32[320...) custom-call(bf16[1024,5120]{1,0:T(8,128)(2,1)} %get-tuple-element.54.x1_in, ...), custom_call_target="tpu_custom_call" | custom-call | flops 7549747200 | bytes 47185920 | tf_op jit(solution)/shard_map/grads/pallas_call | solution.py:572
  168.6 0.0 collective-permute-done.2.refs_4_
  168.6 0.1 collective-permute-start.3
  168.8 0.0 copy-done.1
  168.8 0.4 collective-permute-start.1
  169.1 0.0 copy-done.3
  169.1 2.0 %collective-permute-start = (bf16[128,1280]{1,0:T(8,128)(2,1)S(1)}, bf16[128,1280]{1,0:T(8,128)(2,1)S(1)}, u32[]{:S(2)}, u32[]{:S(2)}) collective-permute-start(bf16[128,1280]{1,0:T(8,128)(2,1)S(1)} %copy-done.3), channel_id=1, source_target_pairs={{0,2},{1,3},{2,0},{3,1},{4,6},{5,7},{6,4},{7,5}} | collective-permute-start | bytes 983048 | tf_op jit(solution)/shard_map/ppermute | solution.py:650
  171.1 0.1 collective-permute-done.1.refs_3_
  171.2 0.0 copy-done
  171.2 0.0 copy-done.2
  171.2 1.6 finish.4
  172.8 0.0 collective-permute-done.3.refs_4_
  172.8 1.2 finish.5
  174.0 5.0 %collective-permute-done.refs_4_ = bf16[128,1280]{1,0:T(8,128)(2,1)S(1)} collective-permute-done((bf16[128,1280]{1,0:T(8,128)(2,1)S(1)}, bf16[128,1280]{1,0:T(8,128)(2,1)S(1)}, u32[]{:S(2)}, u32[]{:S(2)}) %collective-permute-start) | collective-permute-done | bytes 327712 | tf_op jit(solution)/shard_map/ppermute | solution.py:650
  179.1 0.0 collective-permute-start.4
  179.1 0.9 finish.6
  180.0 0.7 collective-permute-done.4.refs_4_
  180.7 0.9 finish.7
Async XLA Ops:
  150.5 18.1 %collective-permute-start.2 = (bf16[256,1280]{1,0:T(8,128)(2,1)}, bf16[256,1280]{1,0:T(8,128)(2,1)S(1)}, u32[]{:S(2)}, u32[]{:S(2)}) collective-permute-start(bf16[256,1280]{1,0:T(8,128)(2,1)} %get-tuple-element.71), channel_id=1, source_target_pairs={{0,2},{1,3},{2,0},{3,1},{4,6},{5,7},{6,4},{7,5}} | collective-permute-start | bytes 1966088 | tf_op jit(solution)/shard_map/ppermute | solution.py:650
  150.6 18.2 %copy-start.1 = (bf16[128,1280]{1,0:T(8,128)(2,1)S(1)}, bf16[128,1280]{1,0:T(8,128)(2,1)}, u32[]{:S(2)}) copy-start(bf16[128,1280]{1,0:T(8,128)(2,1)} %get-tuple-element.70.refs_2_) | copy-start | bytes 983044
  150.6 18.6 %copy-start.3 = (bf16[128,1280]{1,0:T(8,128)(2,1)S(1)}, bf16[128,1280]{1,0:T(8,128)(2,1)}, u32[]{:S(2)}) copy-start(bf16[128,1280]{1,0:T(8,128)(2,1)} %get-tuple-element.68) | copy-start | bytes 983044
  150.6 20.6 %copy-start = (bf16[1024,1280]{1,0:T(8,128)(2,1)S(1)}, bf16[1024,1280]{1,0:T(8,128)(2,1)}, u32[]{:S(2)}) copy-start(bf16[1024,1280]{1,0:T(8,128)(2,1)} %get-tuple-element.69.refs_0_.refs_2_) | copy-start | bytes 7864324
  150.6 20.6 %copy-start.2 = (f32[8,128]{1,0:T(8,128)S(1)}, f32[8,128]{1,0:T(8,128)}, u32[]{:S(2)}) copy-start(f32[8,128]{1,0:T(8,128)} %get-tuple-element.65.sig_in.refs_1_.refs_3_) | copy-start | bytes 12292
  168.6 4.2 %collective-permute-start.3 = (bf16[256,1280]{1,0:T(8,128)(2,1)S(1)}, bf16[256,1280]{1,0:T(8,128)(2,1)S(1)}, u32[]{:S(2)}, u32[]{:S(2)}) collective-permute-start(bf16[256,1280]{1,0:T(8,128)(2,1)S(1)} %collective-permute-done.2.refs_4_), channel_id=1, source_target_pairs={{0,1},{1,0},{2,3},{3,2},{4,5},{5,4},{6,7},{7,6}} | collective-permute-start | bytes 1966088 | tf_op jit(solution)/shard_map/ppermute | solution.py:650
  168.8 2.4 %collective-permute-start.1 = (bf16[128,1280]{1,0:T(8,128)(2,1)S(1)}, bf16[128,1280]{1,0:T(8,128)(2,1)S(1)}, u32[]{:S(2)}, u32[]{:S(2)}) collective-permute-start(bf16[128,1280]{1,0:T(8,128)(2,1)S(1)} %copy-done.1), channel_id=1, source_target_pairs={{0,1},{1,0},{2,3},{3,2},{4,5},{5,4},{6,7},{7,6}} | collective-permute-start | bytes 983048 | tf_op jit(solution)/shard_map/ppermute | solution.py:650
  169.1 9.9 %collective-permute-start = (bf16[128,1280]{1,0:T(8,128)(2,1)S(1)}, bf16[128,1280]{1,0:T(8,128)(2,1)S(1)}, u32[]{:S(2)}, u32[]{:S(2)}) collective-permute-start(bf16[128,1280]{1,0:T(8,128)(2,1)S(1)} %copy-done.3), channel_id=1, source_target_pairs={{0,2},{1,3},{2,0},{3,1},{4,6},{5,7},{6,4},{7,5}} | collective-permute-start | bytes 983048 | tf_op jit(solution)/shard_map/ppermute | solution.py:650
  179.1 1.6 collective-permute-start.4
